TPU v7x, 128 devices: a whole 4x4x4 slice. The times are simulated.
128 devices in a mesh: prompt: 16 (over z, x_lo, core), ctx: 8 (over x_hi, y).
Axes of the slice: x: 4 (x_hi: 2, x_lo: 2; x = x_hi * 2 + x_lo), y: 4, z: 4, core: 2. Of those that a mesh axis runs over, the one named last changes fastest.
Arguments:
- queries: bfloat16 [65536, 16, 128], P(('prompt', 'ctx')), may hold values from -8 to 8
- keys: bfloat16 [65536, 4, 128], P(('prompt', 'ctx')), may hold values from -8 to 8
- values: bfloat16 [65536, 4, 128], P(('prompt', 'ctx')), may hold values from -6 to 6
- spans: int32 [16, 2], P('prompt'), may hold values from 1 to 3072, as said below
- partner: int32 [16], replicated, may hold values from 0 to 15, each once
Outputs:
- attended: bfloat16 [65536, 16, 128], P(('prompt', 'ctx'))
- decode_cache: bfloat16 [16, 2, 16, 8, 128, 128], P('ctx', None, 'prompt')
Inputs may be any that keep to these rules, and one draw needn't show every extreme that they name: `spans`: column 0 counts the image tokens of a prompt, from 1024 to 2048, which come first; column 1 counts the text tokens after them, 1 or more; the two sum to at most 4096, and to exactly 4096 for at least one prompt.
All inputs are finite; a program needn't handle non-finite values.
Results may differ from a plain program's by a relative error of at most 0.0041.
Values may be sent and summed in bfloat16 or wider, within the bound.
No kernel may reach another device: no remote copies, remote signals or barrier semaphores. Data moves between devices by JAX's collectives and lax.ppermute only.
A program may use at most 64 MiB of HBM per device.

v0:
```python
import math

import jax
import jax.numpy as jnp
from jax import lax
from jax.experimental import pallas as pl
from jax.experimental.pallas import tpu as pltpu
from jax.sharding import PartitionSpec as P

far_below = -1e30


flips = (0, 3, 4, 7)


def route(flip):
    return [(c, c ^ flip) for c in range(8)]


def small(limit):
    return pltpu.CompilerParams(vmem_limit_bytes=limit * 1024 * 1024)


def whole(array):
    return pl.BlockSpec(array.shape, lambda *_: (0,) * len(array.shape))


def pack_kv(keys, values, spans, kv_heads):
    short, slots, width = keys.shape
    stripes = slots // kv_heads
    rows = short * stripes

    def kernel(spans_ref, k_ref, v_ref, *refs):
        outs, slot_ref, turned = refs[:4], refs[4], refs[5]
        ctx = lax.axis_index("ctx")
        group, first = ctx // 2, ctx * rows
        live = spans_ref[0, 0] + spans_ref[0, 1]
        for t, ref in enumerate((k_ref, v_ref)):
            turned[t] = jnp.swapaxes(ref[...], 0, 1)
        for k in range(4):
            for t in range(2):
                for stripe in range(stripes):
                    outs[k][t, stripe * short : (stripe + 1) * short, :] = turned[
                        t, stripe * kv_heads + (group ^ k)
                    ]
        for slot in range(slots):
            position = (
                first + lax.broadcasted_iota(jnp.int32, (short, 1), 0) * stripes + slot // kv_heads
            )
            for t in range(2):
                slot_ref[slot, t] = jnp.where(
                    position < live, turned[t, slot].astype(jnp.float32), 0.0
                ).astype(jnp.bfloat16)

    piece = jax.ShapeDtypeStruct((2, rows, width), jnp.bfloat16)
    out_shape = [piece] * 4 + [jax.ShapeDtypeStruct((slots, 2, short, width), jnp.bfloat16)]
    return pl.pallas_call(
        kernel,
        in_specs=[pl.BlockSpec(memory_space=pltpu.SMEM), whole(keys), whole(values)],
        out_specs=[whole(out) for out in out_shape],
        out_shape=out_shape,
        scratch_shapes=[pltpu.VMEM((2, slots, short, width), jnp.bfloat16)],
        compiler_params=small(12),
    )(spans, keys, values)


def pack_queries(queries):
    rows, head_count, width = queries.shape
    heads = head_count // 4

    def kernel(q_ref, *refs):
        outs, turned = refs[:4], refs[4]
        group = lax.axis_index("ctx") // 2
        turned[...] = jnp.swapaxes(q_ref[...], 0, 1)
        for k in range(4):
            outs[k][...] = turned[pl.ds((group ^ k) * heads, heads)]

    piece = jax.ShapeDtypeStruct((heads, rows, width), jnp.bfloat16)
    return pl.pallas_call(
        kernel,
        in_specs=[whole(queries)],
        out_specs=[whole(piece)] * 4,
        out_shape=[piece] * 4,
        scratch_shapes=[pltpu.VMEM((head_count, rows, width), jnp.bfloat16)],
        compiler_params=small(16),
    )(queries)


def join_heads(pieces):
    heads, rows, width = pieces[0].shape

    def kernel(*refs):
        ins, out, gathered = refs[:4], refs[4], refs[5]
        group = lax.axis_index("ctx") // 2
        for k in range(4):
            gathered[pl.ds((group ^ k) * heads, heads)] = ins[k][...]
        out[...] = jnp.swapaxes(gathered[...], 0, 1)

    out_shape = jax.ShapeDtypeStruct((rows, 4 * heads, width), jnp.bfloat16)
    return pl.pallas_call(
        kernel,
        in_specs=[whole(piece) for piece in pieces],
        out_specs=whole(out_shape),
        out_shape=out_shape,
        scratch_shapes=[pltpu.VMEM((4 * heads, rows, width), jnp.bfloat16)],
        compiler_params=small(16),
    )(*pieces)


def attend(which, queries, own, other_first, other_rest, spans, stripes):
    asked = len(which)
    members = len(own)
    heads, rows, width = queries[0].shape
    columns = heads * rows
    part_size = min(columns, 512)
    blocks = 2 * members
    log2_scale = 1.4426950408889634 / math.sqrt(width)

    def kernel(spans_ref, *refs):
        q_refs, own_refs = refs[:asked], refs[asked : asked + members]
        first_ref, rest_ref, *o_refs = refs[asked + members : 2 * asked + members + 2]
        key_blocks, values_t, query_t, mixed, peak, total, held = refs[2 * asked + members + 2 :]
        step = pl.program_id(0)
        ctx = lax.axis_index("ctx")
        live = spans_ref[0, 0] + spans_ref[0, 1]
        block = ctx ^ flips[which[0]]
        for m in range(1, asked):
            block = jnp.where(step == m, ctx ^ flips[which[m]], block)

        @pl.when(step == 0)
        def _():
            rest = [rest_ref.at[m] for m in range(members - 1)]
            for m, source in enumerate((*own_refs, first_ref, *rest)):
                there = ctx ^ flips[m] if m < members else ctx ^ 1 ^ flips[m - members]
                key_blocks[there] = source[0]
                values_t[there] = source[1].T

        @pl.when(block * rows >= live)
        def _():
            for m in range(asked):

                @pl.when(step == m)
                def _():
                    o_refs[m][...] = jnp.zeros_like(o_refs[m])

        @pl.when(block * rows < live)
        def _():
            for m in range(asked):

                @pl.when(step == m)
                def _():
                    for h in range(heads):
                        query_t[:, h * rows : (h + 1) * rows] = q_refs[m][h].T

            mixed[...] = jnp.zeros_like(mixed)
            peak[...] = jnp.full_like(peak, far_below)
            total[...] = jnp.zeros_like(total)

            def scores(j, part):
                return jnp.dot(key_blocks[j], query_t[:, part], preferred_element_type=jnp.float32)

            def fold(s, j, part):
                old = peak[:, part]
                new = jnp.maximum(old, jnp.max(s, axis=0, keepdims=True))
                weights = jnp.exp2((s - new) * log2_scale)
                factor = jnp.exp2((old - new) * log2_scale)
                total[:, part] = total[:, part] * factor + jnp.sum(weights, axis=0, keepdims=True)
                mixed[:, part] = mixed[:, part] * factor + jnp.dot(
                    values_t[j], weights.astype(jnp.bfloat16), preferred_element_type=jnp.float32
                )
                peak[:, part] = new

            parts = [slice(a, a + part_size) for a in range(0, columns, part_size)]

            def earlier(slot, j):
                for part in parts:
                    s = held[slot, :, part]
                    held[1 - slot, :, part] = scores(j + 1, part)
                    fold(s, j, part)

            def diagonal(slot):
                for part in parts:
                    key_row = lax.broadcasted_iota(jnp.int32, (rows, part_size), 0)
                    key_pos = lax.rem(key_row, rows // stripes) * stripes + key_row // (rows // stripes)
                    query_pos = lax.broadcasted_iota(jnp.int32, (rows, part_size), 1) + part.start
                    allowed = key_pos <= lax.rem(query_pos, rows)
                    fold(jnp.where(allowed, held[slot, :, part], far_below), block, part)

            for part in parts:
                held[0, :, part] = scores(0, part)

            def two(t, carry):
                earlier(0, 2 * t)
                earlier(1, 2 * t + 1)
                return carry

            lax.fori_loop(0, block // 2, two, 0)

            @pl.when(lax.rem(block, 2) == 1)
            def _():
                earlier(0, block - 1)
                diagonal(1)

            @pl.when(lax.rem(block, 2) == 0)
            def _():
                diagonal(0)

            position = block * rows + lax.broadcasted_iota(jnp.int32, (rows, 1), 0)
            for h in range(heads):
                part = slice(h * rows, (h + 1) * rows)
                mixture = (mixed[:, part] / total[:, part]).T
                mixture = jnp.where(position < live, mixture, 0.0).astype(jnp.bfloat16)
                for m in range(asked):

                    @pl.when(step == m)
                    def _():
                        o_refs[m][h] = mixture

    arrays = (*queries, *own, other_first, other_rest)
    return pl.pallas_call(
        kernel,
        grid_spec=pltpu.PrefetchScalarGridSpec(
            num_scalar_prefetch=0,
            grid=(asked,),
            in_specs=[pl.BlockSpec(memory_space=pltpu.SMEM)] + [whole(array) for array in arrays],
            out_specs=[whole(query) for query in queries],
            scratch_shapes=[
                pltpu.VMEM((blocks, rows, width), jnp.bfloat16),
                pltpu.VMEM((blocks, width, rows), jnp.bfloat16),
                pltpu.VMEM((width, columns), jnp.bfloat16),
                pltpu.VMEM((width, columns), jnp.float32),
                pltpu.VMEM((1, columns), jnp.float32),
                pltpu.VMEM((1, columns), jnp.float32),
                pltpu.VMEM((2, rows, columns), jnp.float32),
            ],
        ),
        out_shape=[jax.ShapeDtypeStruct(queries[0].shape, jnp.bfloat16)] * asked,
        compiler_params=pltpu.CompilerParams(
            dimension_semantics=("arbitrary",), vmem_limit_bytes=30 * 1024 * 1024
        ),
        cost_estimate=pl.CostEstimate(
            flops=4 * asked * members * heads * rows * rows * width,
            bytes_accessed=4 * rows * width * (asked * heads + 2 * members),
            transcendentals=asked * members * rows * rows * heads,
        ),
    )(spans, *arrays)


def take_blocks(array, order):
    def kernel(order_ref, in_ref, out_ref):
        for i in range(array.shape[0]):
            out_ref[i] = in_ref[order_ref[i]]

    return pl.pallas_call(
        kernel,
        in_specs=[pl.BlockSpec(memory_space=pltpu.SMEM), whole(array)],
        out_specs=whole(array),
        out_shape=jax.ShapeDtypeStruct(array.shape, array.dtype),
        compiler_params=small(8),
    )(order, array)


def swap(array, axis):
    return lax.all_to_all(array, axis, split_axis=0, concat_axis=0, tiled=True)


def send(array, flip):
    return lax.ppermute(array, "ctx", route(flip))


def device_step(queries, keys, values, spans, partner):
    rows, _, width = queries.shape
    kv_heads = keys.shape[1]
    blocks = lax.axis_size("ctx")
    slots = lax.axis_size("prompt")
    stripes = slots // kv_heads

    by_slot = (rows // stripes, slots, width)
    *kv_out, slot_rows = pack_kv(keys.reshape(by_slot), values.reshape(by_slot), spans, kv_heads)
    own = [kv_out[0]] + [send(kv_out[k], flips[k]) for k in (1, 2, 3)]
    other_first = send(kv_out[0], 1)
    queries, slot_rows, *kv_out = lax.optimization_barrier((queries, slot_rows, *kv_out))
    q_out = pack_queries(queries)
    q_own = [q_out[0]] + [send(q_out[k], flips[k]) for k in (1, 2, 3)]
    other_rest = send(jnp.stack(own[1:]), 1)

    by_prompt = swap(slot_rows, "prompt")
    by_row = take_blocks(by_prompt, partner)
    cache = swap(by_row, "ctx")
    held_rows = slots // blocks
    cache = cache.reshape(blocks, held_rows, 2, rows // stripes, width).transpose(1, 2, 0, 3, 4)

    done = [None] * 4
    for which in ((1, 2), (3, 0)):
        asked = [q_own[k] for k in which]
        for k, result in zip(which, attend(which, asked, own, other_first, other_rest, spans, stripes)):
            done[k] = result
    back = [done[0]] + [send(done[k], flips[k]) for k in (1, 2, 3)]
    return join_heads(back), cache[:, :, None]


def solution(mesh):
    placed = P(("prompt", "ctx"), None, None)
    return jax.shard_map(
        device_step,
        mesh=mesh,
        in_specs=(placed, placed, placed, P("prompt", None), P()),
        out_specs=(placed, P("ctx", None, "prompt", None, None, None)),
        check_vma=False,
    )
```

profile of v0, /device:TPU:0, one launch (start us, length us, event | category | flops | bytes accessed | tf_op | source)
XLA Modules:
  0.0 104.5 jit_solution(8922618919083180493)
XLA Ops:
  0.6 1.0 copy-done.2
  1.7 1.0 copy-done.3
  2.7 0.7 copy-done.5
  3.4 1.8 %shard_map.68 = (bf16[2,512,128]{2,1,0:T(8,128)(2,1)}, bf16[2,512,128]{2,1,0:T(8,128)(2,1)}, bf16[2,512,128]{2,1,0:T(8,128)(2,1)}, bf16[2,512,128]{2,1,0:T(8,128)(2,1)}, bf16[16,2,128,128]{3,2,1,0:T(8,128)(2,1)S(1)}) custom-call(s32[1,2]{1,0:T(1,128)S(1)} %copy-done.5, bf16[128,16,128]{2,1,0:T(8,128)(2,1)S(1)} %bitcast.11, bf16[128,16,128]{2,1,0:T(8,128)(2,1)S(1)} %bitcast.12), custom_call_target="tpu_custom_call" | custom-call | tf_op jit(solution)/shard_map/pallas_call | solution.py:57
  5.2 1.0 copy-done.1
  6.1 3.1 %collective-permute-start.1 = (bf16[2,512,128]{2,1,0:T(8,128)(2,1)}, bf16[2,512,128]{2,1,0:T(8,128)(2,1)S(1)}, u32[]{:S(2)}, u32[]{:S(2)}) collective-permute-start(bf16[2,512,128]{2,1,0:T(8,128)(2,1)} %get-tuple-element.19), channel_id=1, source_target_pairs={{0,3},{1,2},{2,1},{3,0},{4,7},{5,6},{6,5},{7,4},{8,11},{9,10},{10,... | collective-permute-start | bytes 786440 | tf_op jit(solution)/shard_map/ppermute | solution.py:268
  9.3 3.0 %collective-permute-start.2 = (bf16[2,512,128]{2,1,0:T(8,128)(2,1)}, bf16[2,512,128]{2,1,0:T(8,128)(2,1)}, u32[]{:S(2)}, u32[]{:S(2)}) collective-permute-start(bf16[2,512,128]{2,1,0:T(8,128)(2,1)} %get-tuple-element.20), channel_id=1, source_target_pairs={{0,4},{1,5},{2,6},{3,7},{4,0},{5,1},{6,2},{7,3},{8,12},{9,13},{10,... | collective-permute-start | bytes 786440 | tf_op jit(solution)/shard_map/ppermute | solution.py:268
  12.3 0.1 collective-permute-start.3
  12.3 6.5 %all-to-all-start = ((bf16[16,2,128,128]{3,2,1,0:T(8,128)(2,1)}), bf16[16,2,128,128]{3,2,1,0:T(8,128)(2,1)S(1)}, u32[]{:S(2)}, u32[]{:S(2)}) async-start(bf16[16,2,128,128]{3,2,1,0:T(8,128)(2,1)} %copy-done.1), calls=%async_computation | async-start | bytes 2097152 | tf_op jit(solution)/shard_map/all_to_all | solution.py:264
  18.8 0.0 copy-start.4
  18.8 1.4 %collective-permute-done.2.refs_4_ = bf16[2,512,128]{2,1,0:T(8,128)(2,1)} collective-permute-done((bf16[2,512,128]{2,1,0:T(8,128)(2,1)}, bf16[2,512,128]{2,1,0:T(8,128)(2,1)}, u32[]{:S(2)}, u32[]{:S(2)}) %collective-permute-start.2) | collective-permute-done | bytes 262176 | tf_op jit(solution)/shard_map/ppermute | solution.py:268
  20.3 4.7 %collective-permute-done.3.refs_5_ = bf16[2,512,128]{2,1,0:T(8,128)(2,1)} collective-permute-done((bf16[2,512,128]{2,1,0:T(8,128)(2,1)}, bf16[2,512,128]{2,1,0:T(8,128)(2,1)}, u32[]{:S(2)}, u32[]{:S(2)}) %collective-permute-start.3) | collective-permute-done | bytes 262176 | tf_op jit(solution)/shard_map/ppermute | solution.py:268
  24.9 2.0 %pad_maximum_fusion = bf16[3,2,512,128]{3,2,1,0:T(8,128)(2,1)} fusion(bf16[1,2,512,128]{3,2,1,0:T(8,128)(2,1)} %bitcast.4, bf16[1,2,512,128]{3,2,1,0:T(8,128)(2,1)} %bitcast.3, bf16[1,2,512,128]{3,2,1,0:T(8,128)(2,1)S(1)} %bitcast.13), kind=kLoop, calls=%fused_computation.1 | loop fusion | flops 786432 | bytes 1572864 | tf_op jit(solution)/shard_map/stack | solution.py:285
  26.9 0.1 collective-permute-start.5
  27.1 1.9 %shard_map.69 = (bf16[4,512,128]{2,1,0:T(8,128)(2,1)S(1)}, bf16[4,512,128]{2,1,0:T(8,128)(2,1)}, bf16[4,512,128]{2,1,0:T(8,128)(2,1)}, bf16[4,512,128]{2,1,0:T(8,128)(2,1)}) custom-call(bf16[512,16,128]{2,1,0:T(8,128)(2,1)S(1)} %copy-done), custom_call_target="tpu_custom_call" | custom-call | tf_op jit(solution)/shard_map/pallas_call | solution.py:79
  29.0 0.8 copy-done.7
  29.8 6.0 %collective-permute-start = (bf16[4,512,128]{2,1,0:T(8,128)(2,1)}, bf16[4,512,128]{2,1,0:T(8,128)(2,1)}, u32[]{:S(2)}, u32[]{:S(2)}) collective-permute-start(bf16[4,512,128]{2,1,0:T(8,128)(2,1)} %get-tuple-element.23), channel_id=1, source_target_pairs={{0,7},{1,6},{2,5},{3,4},{4,3},{5,2},{6,1},{7,0},{8,15},{9,14},{10,... | collective-permute-start | bytes 1572872 | tf_op jit(solution)/shard_map/ppermute | solution.py:268
  35.7 1.4 %collective-permute-start.4 = (bf16[2,512,128]{2,1,0:T(8,128)(2,1)}, bf16[2,512,128]{2,1,0:T(8,128)(2,1)S(1)}, u32[]{:S(2)}, u32[]{:S(2)}) collective-permute-start(bf16[2,512,128]{2,1,0:T(8,128)(2,1)} %get-tuple-element.18.refs_2_), channel_id=1, source_target_pairs={{0,1},{1,0},{2,3},{3,2},{4,5},{5,4},{6,7},{7,6},{8,9},{9,8},{10,11... | collective-permute-start | bytes 786440 | tf_op jit(solution)/shard_map/ppermute | solution.py:268
  37.2 1.2 %collective-permute-start.7 = (bf16[4,512,128]{2,1,0:T(8,128)(2,1)}, bf16[4,512,128]{2,1,0:T(8,128)(2,1)S(1)}, u32[]{:S(2)}, u32[]{:S(2)}) collective-permute-start(bf16[4,512,128]{2,1,0:T(8,128)(2,1)} %get-tuple-element.27), channel_id=1, source_target_pairs={{0,4},{1,5},{2,6},{3,7},{4,0},{5,1},{6,2},{7,3},{8,12},{9,13},{10,... | collective-permute-start | bytes 1572872 | tf_op jit(solution)/shard_map/ppermute | solution.py:268
  38.3 2.1 %all-to-all-done.in_ref = bf16[16,2,128,128]{3,2,1,0:T(8,128)(2,1)S(1)} async-done(((bf16[16,2,128,128]{3,2,1,0:T(8,128)(2,1)}), bf16[16,2,128,128]{3,2,1,0:T(8,128)(2,1)S(1)}, u32[]{:S(2)}, u32[]{:S(2)}) %all-to-all-start) | async-done | bytes 1048608 | tf_op jit(solution)/shard_map/all_to_all | solution.py:264
  40.4 1.6 %shard_map.73 = bf16[16,2,128,128]{3,2,1,0:T(8,128)(2,1)} custom-call(s32[16]{0:T(128)S(1)} %copy-done.4, bf16[16,2,128,128]{3,2,1,0:T(8,128)(2,1)S(1)} %all-to-all-done.in_ref), custom_call_target="tpu_custom_call" | custom-call | tf_op jit(solution)/shard_map/pallas_call | solution.py:254
  42.0 4.2 %all-to-all-start.1 = ((bf16[16,2,128,128]{3,2,1,0:T(8,128)(2,1)}), bf16[16,2,128,128]{3,2,1,0:T(8,128)(2,1)S(1)}, u32[]{:S(2)}, u32[]{:S(2)}) async-start(bf16[16,2,128,128]{3,2,1,0:T(8,128)(2,1)} %shard_map.73), calls=%async_computation.1 | async-start | bytes 2097152 | tf_op jit(solution)/shard_map/all_to_all | solution.py:264
  46.2 6.9 %collective-permute-done.4.refs_6_ = bf16[2,512,128]{2,1,0:T(8,128)(2,1)S(1)} collective-permute-done((bf16[2,512,128]{2,1,0:T(8,128)(2,1)}, bf16[2,512,128]{2,1,0:T(8,128)(2,1)S(1)}, u32[]{:S(2)}, u32[]{:S(2)}) %collective-permute-start.4) | collective-permute-done | bytes 262176 | tf_op jit(solution)/shard_map/ppermute | solution.py:268
  53.2 15.7 %shard_map.70 = (bf16[4,512,128]{2,1,0:T(8,128)(2,1)S(1)}, bf16[4,512,128]{2,1,0:T(8,128)(2,1)S(1)}) custom-call(s32[1,2]{1,0:T(1,128)S(1)} %copy-done.6, bf16[4,512,128]{2,1,0:T(8,128)(2,1)} %collective-permute-done.refs_0_, bf16[4,512,128]{2,1,0:T(8,128)(2,1)S(1)} %copy-done.8, bf16[2,512,128]{2,1,0:T(8,128)(2,1)} %get-tuple-element.18.refs_2_, ...), custom_call_target="tpu_custom_call" | custom-call | flops 4294967296 | bytes 4194304 | tf_op jit(solution)/shard_map/pallas_call | solution.py:220
  68.9 5.5 %collective-permute-start.10 = (bf16[4,512,128]{2,1,0:T(8,128)(2,1)S(1)}, bf16[4,512,128]{2,1,0:T(8,128)(2,1)S(1)}, u32[]{:S(2)}, u32[]{:S(2)}) collective-permute-start(bf16[4,512,128]{2,1,0:T(8,128)(2,1)S(1)} %get-tuple-element.30), channel_id=1, source_target_pairs={{0,7},{1,6},{2,5},{3,4},{4,3},{5,2},{6,1},{7,0},{8,15},{9,14},{10,... | collective-permute-start | bytes 1572872 | tf_op jit(solution)/shard_map/ppermute | solution.py:268
  74.4 15.5 %shard_map.71 = (bf16[4,512,128]{2,1,0:T(8,128)(2,1)S(1)}, bf16[4,512,128]{2,1,0:T(8,128)(2,1)S(1)}) custom-call(s32[1,2]{1,0:T(1,128)S(1)} %copy-done.6, bf16[4,512,128]{2,1,0:T(8,128)(2,1)S(1)} %collective-permute-done.6.refs_0_, bf16[4,512,128]{2,1,0:T(8,128)(2,1)S(1)} %collective-permute-done.7.refs_1_, bf16[2,512,128]{2,1,0:T(8,128)(2,1)} %get-tuple-element.18.refs_2_, ...), custom_call_target="tpu_custom_call" | custom-call | flops 4294967296 | bytes 4194304 | tf_op jit(solution)/shard_map/pallas_call | solution.py:220
  90.0 0.4 collective-permute-start.8
  90.4 0.6 collective-permute-start.9
  91.1 9.4 %collective-permute-done.8.refs_1_ = bf16[4,512,128]{2,1,0:T(8,128)(2,1)S(1)} collective-permute-done((bf16[4,512,128]{2,1,0:T(8,128)(2,1)S(1)}, bf16[4,512,128]{2,1,0:T(8,128)(2,1)S(1)}, u32[]{:S(2)}, u32[]{:S(2)}) %collective-permute-start.8) | collective-permute-done | bytes 524320 | tf_op jit(solution)/shard_map/ppermute | solution.py:268
  100.5 0.7 collective-permute-done.9.refs_2_
  101.1 2.3 %shard_map.72 = bf16[512,16,128]{2,1,0:T(8,128)(2,1)} custom-call(bf16[4,512,128]{2,1,0:T(8,128)(2,1)S(1)} %get-tuple-element.25.refs_0_, bf16[4,512,128]{2,1,0:T(8,128)(2,1)S(1)} %collective-permute-done.8.refs_1_, bf16[4,512,128]{2,1,0:T(8,128)(2,1)S(1)} %collective-permute-done.9.refs_2_, bf16[4,512,128]{2,1,0:T(8,128)(2,1)S(1)} %collective-permute-done.10.refs_3_), custom_call_target="tpu_custom_call" | custom-call | tf_op jit(solution)/shard_map/pallas_call | solution.py:100
  103.5 1.0 copy.9
  (20 shorter events, 0.0 us)
Async XLA Ops:
  0.6 1.0 copy-start.2
  1.7 1.0 copy-start.3
  2.7 0.7 copy-start.5
  5.2 1.0 copy-start.1
  6.1 20.9 %copy-start = (bf16[512,16,128]{2,1,0:T(8,128)(2,1)S(1)}, bf16[512,16,128]{2,1,0:T(8,128)(2,1)}, u32[]{:S(2)}) copy-start(bf16[512,16,128]{2,1,0:T(8,128)(2,1)} %q_ref) | copy-start | bytes 6291460
  6.1 12.7 %collective-permute-start.1 = (bf16[2,512,128]{2,1,0:T(8,128)(2,1)}, bf16[2,512,128]{2,1,0:T(8,128)(2,1)S(1)}, u32[]{:S(2)}, u32[]{:S(2)}) collective-permute-start(bf16[2,512,128]{2,1,0:T(8,128)(2,1)} %get-tuple-element.19), channel_id=1, source_target_pairs={{0,3},{1,2},{2,1},{3,0},{4,7},{5,6},{6,5},{7,4},{8,11},{9,10},{10,... | collective-permute-start | bytes 786440 | tf_op jit(solution)/shard_map/ppermute | solution.py:268
  9.3 11.0 %collective-permute-start.2 = (bf16[2,512,128]{2,1,0:T(8,128)(2,1)}, bf16[2,512,128]{2,1,0:T(8,128)(2,1)}, u32[]{:S(2)}, u32[]{:S(2)}) collective-permute-start(bf16[2,512,128]{2,1,0:T(8,128)(2,1)} %get-tuple-element.20), channel_id=1, source_target_pairs={{0,4},{1,5},{2,6},{3,7},{4,0},{5,1},{6,2},{7,3},{8,12},{9,13},{10,... | collective-permute-start | bytes 786440 | tf_op jit(solution)/shard_map/ppermute | solution.py:268
  12.3 12.6 %collective-permute-start.3 = (bf16[2,512,128]{2,1,0:T(8,128)(2,1)}, bf16[2,512,128]{2,1,0:T(8,128)(2,1)}, u32[]{:S(2)}, u32[]{:S(2)}) collective-permute-start(bf16[2,512,128]{2,1,0:T(8,128)(2,1)} %get-tuple-element.21), channel_id=1, source_target_pairs={{0,7},{1,6},{2,5},{3,4},{4,3},{5,2},{6,1},{7,0},{8,15},{9,14},{10,... | collective-permute-start | bytes 786440 | tf_op jit(solution)/shard_map/ppermute | solution.py:268
  12.3 28.1 %all-to-all-start = ((bf16[16,2,128,128]{3,2,1,0:T(8,128)(2,1)}), bf16[16,2,128,128]{3,2,1,0:T(8,128)(2,1)S(1)}, u32[]{:S(2)}, u32[]{:S(2)}) async-start(bf16[16,2,128,128]{3,2,1,0:T(8,128)(2,1)} %copy-done.1), calls=%async_computation | async-start | bytes 2097152 | tf_op jit(solution)/shard_map/all_to_all | solution.py:264
  18.8 21.6 %copy-start.4 = (s32[16]{0:T(128)S(1)}, s32[16]{0:T(128)}, u32[]{:S(2)}) copy-start(s32[16]{0:T(128)} %order_ref.1) | copy-start | bytes 196
  26.9 26.2 %collective-permute-start.5 = (bf16[3,2,512,128]{3,2,1,0:T(8,128)(2,1)}, bf16[3,2,512,128]{3,2,1,0:T(8,128)(2,1)}, u32[]{:S(2)}, u32[]{:S(2)}) collective-permute-start(bf16[3,2,512,128]{3,2,1,0:T(8,128)(2,1)} %pad_maximum_fusion), channel_id=1, source_target_pairs={{0,1},{1,0},{2,3},{3,2},{4,5},{5,4},{6,7},{7,6},{8,9},{9,8},{10,11... | collective-permute-start | bytes 2359304 | tf_op jit(solution)/shard_map/ppermute | solution.py:268
  29.0 0.8 copy-start.7
  29.8 23.4 %collective-permute-start = (bf16[4,512,128]{2,1,0:T(8,128)(2,1)}, bf16[4,512,128]{2,1,0:T(8,128)(2,1)}, u32[]{:S(2)}, u32[]{:S(2)}) collective-permute-start(bf16[4,512,128]{2,1,0:T(8,128)(2,1)} %get-tuple-element.23), channel_id=1, source_target_pairs={{0,7},{1,6},{2,5},{3,4},{4,3},{5,2},{6,1},{7,0},{8,15},{9,14},{10,... | collective-permute-start | bytes 1572872 | tf_op jit(solution)/shard_map/ppermute | solution.py:268
  35.7 17.4 %collective-permute-start.4 = (bf16[2,512,128]{2,1,0:T(8,128)(2,1)}, bf16[2,512,128]{2,1,0:T(8,128)(2,1)S(1)}, u32[]{:S(2)}, u32[]{:S(2)}) collective-permute-start(bf16[2,512,128]{2,1,0:T(8,128)(2,1)} %get-tuple-element.18.refs_2_), channel_id=1, source_target_pairs={{0,1},{1,0},{2,3},{3,2},{4,5},{5,4},{6,7},{7,6},{8,9},{9,8},{10,11... | collective-permute-start | bytes 786440 | tf_op jit(solution)/shard_map/ppermute | solution.py:268
  37.2 37.3 %collective-permute-start.6 = (bf16[4,512,128]{2,1,0:T(8,128)(2,1)}, bf16[4,512,128]{2,1,0:T(8,128)(2,1)S(1)}, u32[]{:S(2)}, u32[]{:S(2)}) collective-permute-start(bf16[4,512,128]{2,1,0:T(8,128)(2,1)} %get-tuple-element.26), channel_id=1, source_target_pairs={{0,3},{1,2},{2,1},{3,0},{4,7},{5,6},{6,5},{7,4},{8,11},{9,10},{10,... | collective-permute-start | bytes 1572872 | tf_op jit(solution)/shard_map/ppermute | solution.py:268
  37.2 16.0 %copy-start.6 = (s32[1,2]{1,0:T(1,128)S(1)}, s32[1,2]{1,0:T(1,128)}, u32[]{:S(2)}) copy-start(s32[1,2]{1,0:T(1,128)} %spans_ref.5) | copy-start | bytes 28
  37.2 16.0 %copy-start.8 = (bf16[4,512,128]{2,1,0:T(8,128)(2,1)S(1)}, bf16[4,512,128]{2,1,0:T(8,128)(2,1)}, u32[]{:S(2)}) copy-start(bf16[4,512,128]{2,1,0:T(8,128)(2,1)} %copy-done.7) | copy-start | bytes 1572868
  37.2 37.3 %collective-permute-start.7 = (bf16[4,512,128]{2,1,0:T(8,128)(2,1)}, bf16[4,512,128]{2,1,0:T(8,128)(2,1)S(1)}, u32[]{:S(2)}, u32[]{:S(2)}) collective-permute-start(bf16[4,512,128]{2,1,0:T(8,128)(2,1)} %get-tuple-element.27), channel_id=1, source_target_pairs={{0,4},{1,5},{2,6},{3,7},{4,0},{5,1},{6,2},{7,3},{8,12},{9,13},{10,... | collective-permute-start | bytes 1572872 | tf_op jit(solution)/shard_map/ppermute | solution.py:268
  42.0 61.4 %all-to-all-start.1 = ((bf16[16,2,128,128]{3,2,1,0:T(8,128)(2,1)}), bf16[16,2,128,128]{3,2,1,0:T(8,128)(2,1)S(1)}, u32[]{:S(2)}, u32[]{:S(2)}) async-start(bf16[16,2,128,128]{3,2,1,0:T(8,128)(2,1)} %shard_map.73), calls=%async_computation.1 | async-start | bytes 2097152 | tf_op jit(solution)/shard_map/all_to_all | solution.py:264
  68.9 22.2 %collective-permute-start.10 = (bf16[4,512,128]{2,1,0:T(8,128)(2,1)S(1)}, bf16[4,512,128]{2,1,0:T(8,128)(2,1)S(1)}, u32[]{:S(2)}, u32[]{:S(2)}) collective-permute-start(bf16[4,512,128]{2,1,0:T(8,128)(2,1)S(1)} %get-tuple-element.30), channel_id=1, source_target_pairs={{0,7},{1,6},{2,5},{3,4},{4,3},{5,2},{6,1},{7,0},{8,15},{9,14},{10,... | collective-permute-start | bytes 1572872 | tf_op jit(solution)/shard_map/ppermute | solution.py:268
  90.0 10.5 %collective-permute-start.8 = (bf16[4,512,128]{2,1,0:T(8,128)(2,1)S(1)}, bf16[4,512,128]{2,1,0:T(8,128)(2,1)S(1)}, u32[]{:S(2)}, u32[]{:S(2)}) collective-permute-start(bf16[4,512,128]{2,1,0:T(8,128)(2,1)S(1)} %get-tuple-element.28), channel_id=1, source_target_pairs={{0,3},{1,2},{2,1},{3,0},{4,7},{5,6},{6,5},{7,4},{8,11},{9,10},{10,... | collective-permute-start | bytes 1572872 | tf_op jit(solution)/shard_map/ppermute | solution.py:268
  90.4 10.7 %collective-permute-start.9 = (bf16[4,512,128]{2,1,0:T(8,128)(2,1)S(1)}, bf16[4,512,128]{2,1,0:T(8,128)(2,1)S(1)}, u32[]{:S(2)}, u32[]{:S(2)}) collective-permute-start(bf16[4,512,128]{2,1,0:T(8,128)(2,1)S(1)} %get-tuple-element.29), channel_id=1, source_target_pairs={{0,4},{1,5},{2,6},{3,7},{4,0},{5,1},{6,2},{7,3},{8,12},{9,13},{10,... | collective-permute-start | bytes 1572872 | tf_op jit(solution)/shard_map/ppermute | solution.py:268
where the time goes:
time: 105 us
  Pallas kernels  38.9 us (37%)
  starting transfers between devices  32.1 us (31%)
  waiting for transfers between devices  25.2 us (24%)
  local copies, waits for them, and re-layouts  5.58 us (5%)
  other arithmetic  1.99 us (2%)
    pallas_call x2, Pallas kernels, attend(): pl.pallas_call(kernel, grid_spec=pltpu.PrefetchScalarGridSpec(num_scalar_...  31.3 us
    ppermute x11, waiting for transfers between devices, send(): return lax.ppermute(array, 'ctx', route(flip))  23.1 us
    ppermute x11, starting transfers between devices, send(): return lax.ppermute(array, 'ctx', route(flip))  21.5 us
    all_to_all x2, starting transfers between devices, swap(): return lax.all_to_all(array, axis, split_axis=0, concat_axis=0, tiled=True)  10.7 us
    unnamed x18, local copies, waits for them, and re-layouts  4.54 us
    pallas_call x1, Pallas kernels, join_heads(): pl.pallas_call(kernel, in_specs=[whole(piece) for piece in pieces], out_s...  2.35 us
    all_to_all x2, waiting for transfers between devices, swap(): return lax.all_to_all(array, axis, split_axis=0, concat_axis=0, tiled=True)  2.11 us
  transfers between devices with their start and end apart: 13, of which 6 were waited for; matrix products, arithmetic and copies ran while one was open for 2% of the time, Pallas kernels for 36%

commit v1 on v0

--- a/solution.py
+++ b/solution.py
@@ -31,12 +31,21 @@
     rows = short * stripes
 
     def kernel(spans_ref, k_ref, v_ref, *refs):
-        outs, slot_ref, turned = refs[:4], refs[4], refs[5]
+        outs, slot_ref = refs[:4], refs[4]
+        span, k_in, v_in, turned, sems = refs[5:]
+        copies = [
+            pltpu.make_async_copy(source, target, sems.at[i])
+            for i, (source, target) in enumerate(((k_ref, k_in), (v_ref, v_in), (spans_ref, span)))
+        ]
+        for copy in copies:
+            copy.start()
         ctx = lax.axis_index("ctx")
         group, first = ctx // 2, ctx * rows
-        live = spans_ref[0, 0] + spans_ref[0, 1]
-        for t, ref in enumerate((k_ref, v_ref)):
+        for t, ref in enumerate((k_in, v_in)):
+            copies[t].wait()
             turned[t] = jnp.swapaxes(ref[...], 0, 1)
+        copies[2].wait()
+        live = span[0, 0] + span[0, 1]
         for k in range(4):
             for t in range(2):
                 for stripe in range(stripes):
@@ -56,11 +65,17 @@
     out_shape = [piece] * 4 + [jax.ShapeDtypeStruct((slots, 2, short, width), jnp.bfloat16)]
     return pl.pallas_call(
         kernel,
-        in_specs=[pl.BlockSpec(memory_space=pltpu.SMEM), whole(keys), whole(values)],
+        in_specs=[pl.BlockSpec(memory_space=pltpu.HBM)] * 3,
         out_specs=[whole(out) for out in out_shape],
         out_shape=out_shape,
-        scratch_shapes=[pltpu.VMEM((2, slots, short, width), jnp.bfloat16)],
-        compiler_params=small(12),
+        scratch_shapes=[
+            pltpu.SMEM(spans.shape, jnp.int32),
+            pltpu.VMEM(keys.shape, jnp.bfloat16),
+            pltpu.VMEM(keys.shape, jnp.bfloat16),
+            pltpu.VMEM((2, slots, short, width), jnp.bfloat16),
+            pltpu.SemaphoreType.DMA((3,)),
+        ],
+        compiler_params=small(62),
     )(spans, keys, values)
 
 
@@ -119,7 +134,7 @@
     def kernel(spans_ref, *refs):
         q_refs, own_refs = refs[:asked], refs[asked : asked + members]
         first_ref, rest_ref, *o_refs = refs[asked + members : 2 * asked + members + 2]
-        key_blocks, values_t, query_t, mixed, peak, total, held = refs[2 * asked + members + 2 :]
+        key_blocks, values_t, query_t, mixed, peak, held = refs[2 * asked + members + 2 :]
         step = pl.program_id(0)
         ctx = lax.axis_index("ctx")
         live = spans_ref[0, 0] + spans_ref[0, 1]
@@ -133,7 +148,8 @@
             for m, source in enumerate((*own_refs, first_ref, *rest)):
                 there = ctx ^ flips[m] if m < members else ctx ^ 1 ^ flips[m - members]
                 key_blocks[there] = source[0]
-                values_t[there] = source[1].T
+                values_t[there, :width] = source[1].T
+            values_t[:, width:] = jnp.ones_like(values_t[:, width:])
 
         @pl.when(block * rows >= live)
         def _():
@@ -154,7 +170,6 @@
 
             mixed[...] = jnp.zeros_like(mixed)
             peak[...] = jnp.full_like(peak, far_below)
-            total[...] = jnp.zeros_like(total)
 
             def scores(j, part):
                 return jnp.dot(key_blocks[j], query_t[:, part], preferred_element_type=jnp.float32)
@@ -164,7 +179,6 @@
                 new = jnp.maximum(old, jnp.max(s, axis=0, keepdims=True))
                 weights = jnp.exp2((s - new) * log2_scale)
                 factor = jnp.exp2((old - new) * log2_scale)
-                total[:, part] = total[:, part] * factor + jnp.sum(weights, axis=0, keepdims=True)
                 mixed[:, part] = mixed[:, part] * factor + jnp.dot(
                     values_t[j], weights.astype(jnp.bfloat16), preferred_element_type=jnp.float32
                 )
@@ -208,7 +222,7 @@
             position = block * rows + lax.broadcasted_iota(jnp.int32, (rows, 1), 0)
             for h in range(heads):
                 part = slice(h * rows, (h + 1) * rows)
-                mixture = (mixed[:, part] / total[:, part]).T
+                mixture = (mixed[:width, part] / mixed[width : width + 1, part]).T
                 mixture = jnp.where(position < live, mixture, 0.0).astype(jnp.bfloat16)
                 for m in range(asked):
 
@@ -226,10 +240,9 @@
             out_specs=[whole(query) for query in queries],
             scratch_shapes=[
                 pltpu.VMEM((blocks, rows, width), jnp.bfloat16),
-                pltpu.VMEM((blocks, width, rows), jnp.bfloat16),
+                pltpu.VMEM((blocks, width + 16, rows), jnp.bfloat16),
                 pltpu.VMEM((width, columns), jnp.bfloat16),
-                pltpu.VMEM((width, columns), jnp.float32),
-                pltpu.VMEM((1, columns), jnp.float32),
+                pltpu.VMEM((width + 16, columns), jnp.float32),
                 pltpu.VMEM((1, columns), jnp.float32),
                 pltpu.VMEM((2, rows, columns), jnp.float32),
             ],
@@ -279,7 +292,6 @@
     *kv_out, slot_rows = pack_kv(keys.reshape(by_slot), values.reshape(by_slot), spans, kv_heads)
     own = [kv_out[0]] + [send(kv_out[k], flips[k]) for k in (1, 2, 3)]
     other_first = send(kv_out[0], 1)
-    queries, slot_rows, *kv_out = lax.optimization_barrier((queries, slot_rows, *kv_out))
     q_out = pack_queries(queries)
     q_own = [q_out[0]] + [send(q_out[k], flips[k]) for k in (1, 2, 3)]
     other_rest = send(jnp.stack(own[1:]), 1)

time: 105 us -> 101 us (0.962)
  local copies, waits for them, and re-layouts: 5.58 us -> 1.85 us
    unnamed x18 -> x10, local copies, waits for them, and re-layouts: 4.54 us -> 0.8 us
    pallas_call x2, Pallas kernels: 31.3 us -> 29.6 us  [attend(): pl.pallas_call(kernel, grid_spec=pltpu.PrefetchScalarGridSpec(num_scalar_...]
  transfers between devices with their start and end apart: 13 -> 13, of which waited for: 6 -> 6; matrix products, arithmetic and copies ran while one was open for 2% -> 2% of each run, Pallas kernels for 36% -> 35%
where the time goes in v1:
time: 101 us; the launch traced here: 100 us
  Pallas kernels  38.3 us (38%)
  starting transfers between devices  32.1 us (32%)
  waiting for transfers between devices  25.4 us (25%)
  other arithmetic  1.99 us (2%)
  local copies, waits for them, and re-layouts  1.85 us (2%)
    pallas_call x2, Pallas kernels, attend(): pl.pallas_call(kernel, grid_spec=pltpu.PrefetchScalarGridSpec(num_scalar_...  29.6 us
    ppermute x11, waiting for transfers between devices, send(): return lax.ppermute(array, 'ctx', route(flip))  23.2 us
    ppermute x11, starting transfers between devices, send(): return lax.ppermute(array, 'ctx', route(flip))  21.5 us
    all_to_all x2, starting transfers between devices, swap(): return lax.all_to_all(array, axis, split_axis=0, concat_axis=0, tiled=True)  10.6 us
    pallas_call x1, Pallas kernels, pack_kv(): pl.pallas_call(kernel, in_specs=[pl.BlockSpec(memory_space=pltpu.HBM)] *...  2.79 us
    pallas_call x1, Pallas kernels, join_heads(): pl.pallas_call(kernel, in_specs=[whole(piece) for piece in pieces], out_s...  2.35 us
    all_to_all x2, waiting for transfers between devices, swap(): return lax.all_to_all(array, axis, split_axis=0, concat_axis=0, tiled=True)  2.14 us
  transfers between devices with their start and end apart: 13, of which 6 were waited for; matrix products, arithmetic and copies ran while one was open for 2% of the time, Pallas kernels for 35%

profile of v1, /device:TPU:0, one launch (start us, length us, event | category | flops | bytes accessed | tf_op | source)
XLA Modules:
  0.0 100.4 jit_solution(4874147827718185746)
XLA Ops:
  0.6 2.8 %shard_map.69 = (bf16[2,512,128]{2,1,0:T(8,128)(2,1)}, bf16[2,512,128]{2,1,0:T(8,128)(2,1)}, bf16[2,512,128]{2,1,0:T(8,128)(2,1)}, bf16[2,512,128]{2,1,0:T(8,128)(2,1)}, bf16[16,2,128,128]{3,2,1,0:T(8,128)(2,1)}) custom-call(s32[1,2]{1,0:T(1,128)} %spans_ref.5, bf16[128,16,128]{2,1,0:T(8,128)(2,1)} %bitcast.14, bf16[128,16,128]{2,1,0:T(8,128)(2,1)} %bitcast.15), custom_call_target="tpu_custom_call" | custom-call | tf_op jit(solution)/shard_map/pallas_call | solution.py:66
  3.4 0.0 copy-start
  3.4 3.2 %collective-permute-start.1 = (bf16[2,512,128]{2,1,0:T(8,128)(2,1)}, bf16[2,512,128]{2,1,0:T(8,128)(2,1)S(1)}, u32[]{:S(2)}, u32[]{:S(2)}) collective-permute-start(bf16[2,512,128]{2,1,0:T(8,128)(2,1)} %get-tuple-element.18), channel_id=1, source_target_pairs={{0,3},{1,2},{2,1},{3,0},{4,7},{5,6},{6,5},{7,4},{8,11},{9,10},{10,... | collective-permute-start | bytes 786440 | tf_op jit(solution)/shard_map/ppermute | solution.py:281
  6.6 3.0 %collective-permute-start.2 = (bf16[2,512,128]{2,1,0:T(8,128)(2,1)}, bf16[2,512,128]{2,1,0:T(8,128)(2,1)}, u32[]{:S(2)}, u32[]{:S(2)}) collective-permute-start(bf16[2,512,128]{2,1,0:T(8,128)(2,1)} %get-tuple-element.19), channel_id=1, source_target_pairs={{0,4},{1,5},{2,6},{3,7},{4,0},{5,1},{6,2},{7,3},{8,12},{9,13},{10,... | collective-permute-start | bytes 786440 | tf_op jit(solution)/shard_map/ppermute | solution.py:281
  9.7 0.1 collective-permute-start.3
  9.7 6.5 %all-to-all-start = ((bf16[16,2,128,128]{3,2,1,0:T(8,128)(2,1)}), bf16[16,2,128,128]{3,2,1,0:T(8,128)(2,1)S(1)}, u32[]{:S(2)}, u32[]{:S(2)}) async-start(bf16[16,2,128,128]{3,2,1,0:T(8,128)(2,1)} %get-tuple-element.27), calls=%async_computation | async-start | bytes 2097152 | tf_op jit(solution)/shard_map/all_to_all | solution.py:277
  16.2 0.0 copy-start.1
  16.2 0.0 collective-permute-done.1.refs_3_
  16.2 1.4 %collective-permute-done.2.refs_4_ = bf16[2,512,128]{2,1,0:T(8,128)(2,1)} collective-permute-done((bf16[2,512,128]{2,1,0:T(8,128)(2,1)}, bf16[2,512,128]{2,1,0:T(8,128)(2,1)}, u32[]{:S(2)}, u32[]{:S(2)}) %collective-permute-start.2) | collective-permute-done | bytes 262176 | tf_op jit(solution)/shard_map/ppermute | solution.py:281
  17.6 4.7 %collective-permute-done.3.refs_5_ = bf16[2,512,128]{2,1,0:T(8,128)(2,1)} collective-permute-done((bf16[2,512,128]{2,1,0:T(8,128)(2,1)}, bf16[2,512,128]{2,1,0:T(8,128)(2,1)}, u32[]{:S(2)}, u32[]{:S(2)}) %collective-permute-start.3) | collective-permute-done | bytes 262176 | tf_op jit(solution)/shard_map/ppermute | solution.py:281
  22.3 2.0 %pad_maximum_fusion = bf16[3,2,512,128]{3,2,1,0:T(8,128)(2,1)} fusion(bf16[1,2,512,128]{3,2,1,0:T(8,128)(2,1)} %bitcast.4, bf16[1,2,512,128]{3,2,1,0:T(8,128)(2,1)} %bitcast.3, bf16[1,2,512,128]{3,2,1,0:T(8,128)(2,1)S(1)} %bitcast.11), kind=kLoop, calls=%fused_computation.1 | loop fusion | flops 786432 | bytes 1572864 | tf_op jit(solution)/shard_map/stack | solution.py:297
  24.3 0.1 collective-permute-start.5
  24.4 1.9 %shard_map.68 = (bf16[4,512,128]{2,1,0:T(8,128)(2,1)S(1)}, bf16[4,512,128]{2,1,0:T(8,128)(2,1)}, bf16[4,512,128]{2,1,0:T(8,128)(2,1)}, bf16[4,512,128]{2,1,0:T(8,128)(2,1)}) custom-call(bf16[512,16,128]{2,1,0:T(8,128)(2,1)S(1)} %copy-done), custom_call_target="tpu_custom_call" | custom-call | tf_op jit(solution)/shard_map/pallas_call | solution.py:94
  26.4 0.8 copy-done.3
  27.1 6.0 %collective-permute-start = (bf16[4,512,128]{2,1,0:T(8,128)(2,1)}, bf16[4,512,128]{2,1,0:T(8,128)(2,1)}, u32[]{:S(2)}, u32[]{:S(2)}) collective-permute-start(bf16[4,512,128]{2,1,0:T(8,128)(2,1)} %get-tuple-element.15), channel_id=1, source_target_pairs={{0,7},{1,6},{2,5},{3,4},{4,3},{5,2},{6,1},{7,0},{8,15},{9,14},{10,... | collective-permute-start | bytes 1572872 | tf_op jit(solution)/shard_map/ppermute | solution.py:281
  33.1 1.4 %collective-permute-start.4 = (bf16[2,512,128]{2,1,0:T(8,128)(2,1)}, bf16[2,512,128]{2,1,0:T(8,128)(2,1)S(1)}, u32[]{:S(2)}, u32[]{:S(2)}) collective-permute-start(bf16[2,512,128]{2,1,0:T(8,128)(2,1)} %get-tuple-element.17.refs_2_), channel_id=1, source_target_pairs={{0,1},{1,0},{2,3},{3,2},{4,5},{5,4},{6,7},{7,6},{8,9},{9,8},{10,11... | collective-permute-start | bytes 786440 | tf_op jit(solution)/shard_map/ppermute | solution.py:281
  34.5 0.0 collective-permute-start.6
  34.5 1.2 %collective-permute-start.7 = (bf16[4,512,128]{2,1,0:T(8,128)(2,1)}, bf16[4,512,128]{2,1,0:T(8,128)(2,1)S(1)}, u32[]{:S(2)}, u32[]{:S(2)}) collective-permute-start(bf16[4,512,128]{2,1,0:T(8,128)(2,1)} %get-tuple-element.23), channel_id=1, source_target_pairs={{0,4},{1,5},{2,6},{3,7},{4,0},{5,1},{6,2},{7,3},{8,12},{9,13},{10,... | collective-permute-start | bytes 1572872 | tf_op jit(solution)/shard_map/ppermute | solution.py:281
  35.7 2.1 %all-to-all-done.in_ref = bf16[16,2,128,128]{3,2,1,0:T(8,128)(2,1)S(1)} async-done(((bf16[16,2,128,128]{3,2,1,0:T(8,128)(2,1)}), bf16[16,2,128,128]{3,2,1,0:T(8,128)(2,1)S(1)}, u32[]{:S(2)}, u32[]{:S(2)}) %all-to-all-start) | async-done | bytes 1048608 | tf_op jit(solution)/shard_map/all_to_all | solution.py:277
  37.8 1.6 %shard_map.73 = bf16[16,2,128,128]{3,2,1,0:T(8,128)(2,1)} custom-call(s32[16]{0:T(128)S(1)} %copy-done.1, bf16[16,2,128,128]{3,2,1,0:T(8,128)(2,1)S(1)} %all-to-all-done.in_ref), custom_call_target="tpu_custom_call" | custom-call | tf_op jit(solution)/shard_map/pallas_call | solution.py:267
  39.4 4.2 %all-to-all-start.1 = ((bf16[16,2,128,128]{3,2,1,0:T(8,128)(2,1)}), bf16[16,2,128,128]{3,2,1,0:T(8,128)(2,1)S(1)}, u32[]{:S(2)}, u32[]{:S(2)}) async-start(bf16[16,2,128,128]{3,2,1,0:T(8,128)(2,1)} %shard_map.73), calls=%async_computation.1 | async-start | bytes 2097152 | tf_op jit(solution)/shard_map/all_to_all | solution.py:277
  43.6 6.9 %collective-permute-done.4.refs_6_ = bf16[2,512,128]{2,1,0:T(8,128)(2,1)S(1)} collective-permute-done((bf16[2,512,128]{2,1,0:T(8,128)(2,1)}, bf16[2,512,128]{2,1,0:T(8,128)(2,1)S(1)}, u32[]{:S(2)}, u32[]{:S(2)}) %collective-permute-start.4) | collective-permute-done | bytes 262176 | tf_op jit(solution)/shard_map/ppermute | solution.py:281
  50.5 0.0 collective-permute-done.refs_0_
  50.6 14.9 %shard_map.70 = (bf16[4,512,128]{2,1,0:T(8,128)(2,1)S(1)}, bf16[4,512,128]{2,1,0:T(8,128)(2,1)S(1)}) custom-call(s32[1,2]{1,0:T(1,128)S(1)} %copy-done.2, bf16[4,512,128]{2,1,0:T(8,128)(2,1)} %collective-permute-done.refs_0_, bf16[4,512,128]{2,1,0:T(8,128)(2,1)S(1)} %copy-done.4, bf16[2,512,128]{2,1,0:T(8,128)(2,1)} %get-tuple-element.17.refs_2_, ...), custom_call_target="tpu_custom_call" | custom-call | flops 4294967296 | bytes 4194304 | tf_op jit(solution)/shard_map/pallas_call | solution.py:234
  65.5 5.5 %collective-permute-start.10 = (bf16[4,512,128]{2,1,0:T(8,128)(2,1)S(1)}, bf16[4,512,128]{2,1,0:T(8,128)(2,1)S(1)}, u32[]{:S(2)}, u32[]{:S(2)}) collective-permute-start(bf16[4,512,128]{2,1,0:T(8,128)(2,1)S(1)} %get-tuple-element.26), channel_id=1, source_target_pairs={{0,7},{1,6},{2,5},{3,4},{4,3},{5,2},{6,1},{7,0},{8,15},{9,14},{10,... | collective-permute-start | bytes 1572872 | tf_op jit(solution)/shard_map/ppermute | solution.py:281
  70.9 14.7 %shard_map.71 = (bf16[4,512,128]{2,1,0:T(8,128)(2,1)S(1)}, bf16[4,512,128]{2,1,0:T(8,128)(2,1)S(1)}) custom-call(s32[1,2]{1,0:T(1,128)S(1)} %copy-done.2, bf16[4,512,128]{2,1,0:T(8,128)(2,1)S(1)} %collective-permute-done.6.refs_0_, bf16[4,512,128]{2,1,0:T(8,128)(2,1)S(1)} %collective-permute-done.7.refs_1_, bf16[2,512,128]{2,1,0:T(8,128)(2,1)} %get-tuple-element.17.refs_2_, ...), custom_call_target="tpu_custom_call" | custom-call | flops 4294967296 | bytes 4194304 | tf_op jit(solution)/shard_map/pallas_call | solution.py:234
  85.7 0.6 collective-permute-start.8
  86.3 0.5 collective-permute-start.9
  86.8 9.4 %collective-permute-done.8.refs_1_ = bf16[4,512,128]{2,1,0:T(8,128)(2,1)S(1)} collective-permute-done((bf16[4,512,128]{2,1,0:T(8,128)(2,1)S(1)}, bf16[4,512,128]{2,1,0:T(8,128)(2,1)S(1)}, u32[]{:S(2)}, u32[]{:S(2)}) %collective-permute-start.8) | collective-permute-done | bytes 524320 | tf_op jit(solution)/shard_map/ppermute | solution.py:281
  96.1 0.8 collective-permute-done.9.refs_2_
  97.0 2.3 %shard_map.72 = bf16[512,16,128]{2,1,0:T(8,128)(2,1)} custom-call(bf16[4,512,128]{2,1,0:T(8,128)(2,1)S(1)} %get-tuple-element.21.refs_0_, bf16[4,512,128]{2,1,0:T(8,128)(2,1)S(1)} %collective-permute-done.8.refs_1_, bf16[4,512,128]{2,1,0:T(8,128)(2,1)S(1)} %collective-permute-done.9.refs_2_, bf16[4,512,128]{2,1,0:T(8,128)(2,1)S(1)} %collective-permute-done.10.refs_3_), custom_call_target="tpu_custom_call" | custom-call | tf_op jit(solution)/shard_map/pallas_call | solution.py:115
  99.3 1.0 %copy.9 = bf16[8,2,2,128,128]{4,3,0,2,1:T(8,128)(2,1)} copy(bf16[8,2,2,128,128]{4,3,2,1,0:T(8,128)(2,1)S(1)} %bitcast.12) | data formatting | bytes 2097152 | tf_op jit(solution)/shard_map/reshape | solution.py:303
  (12 shorter events, 0.0 us)
Async XLA Ops:
  3.4 21.0 %copy-start = (bf16[512,16,128]{2,1,0:T(8,128)(2,1)S(1)}, bf16[512,16,128]{2,1,0:T(8,128)(2,1)}, u32[]{:S(2)}) copy-start(bf16[512,16,128]{2,1,0:T(8,128)(2,1)} %q_ref.1) | copy-start | bytes 6291460
  3.4 12.8 %collective-permute-start.1 = (bf16[2,512,128]{2,1,0:T(8,128)(2,1)}, bf16[2,512,128]{2,1,0:T(8,128)(2,1)S(1)}, u32[]{:S(2)}, u32[]{:S(2)}) collective-permute-start(bf16[2,512,128]{2,1,0:T(8,128)(2,1)} %get-tuple-element.18), channel_id=1, source_target_pairs={{0,3},{1,2},{2,1},{3,0},{4,7},{5,6},{6,5},{7,4},{8,11},{9,10},{10,... | collective-permute-start | bytes 786440 | tf_op jit(solution)/shard_map/ppermute | solution.py:281
  6.6 11.0 %collective-permute-start.2 = (bf16[2,512,128]{2,1,0:T(8,128)(2,1)}, bf16[2,512,128]{2,1,0:T(8,128)(2,1)}, u32[]{:S(2)}, u32[]{:S(2)}) collective-permute-start(bf16[2,512,128]{2,1,0:T(8,128)(2,1)} %get-tuple-element.19), channel_id=1, source_target_pairs={{0,4},{1,5},{2,6},{3,7},{4,0},{5,1},{6,2},{7,3},{8,12},{9,13},{10,... | collective-permute-start | bytes 786440 | tf_op jit(solution)/shard_map/ppermute | solution.py:281
  9.7 12.6 %collective-permute-start.3 = (bf16[2,512,128]{2,1,0:T(8,128)(2,1)}, bf16[2,512,128]{2,1,0:T(8,128)(2,1)}, u32[]{:S(2)}, u32[]{:S(2)}) collective-permute-start(bf16[2,512,128]{2,1,0:T(8,128)(2,1)} %get-tuple-element.20), channel_id=1, source_target_pairs={{0,7},{1,6},{2,5},{3,4},{4,3},{5,2},{6,1},{7,0},{8,15},{9,14},{10,... | collective-permute-start | bytes 786440 | tf_op jit(solution)/shard_map/ppermute | solution.py:281
  9.7 28.1 %all-to-all-start = ((bf16[16,2,128,128]{3,2,1,0:T(8,128)(2,1)}), bf16[16,2,128,128]{3,2,1,0:T(8,128)(2,1)S(1)}, u32[]{:S(2)}, u32[]{:S(2)}) async-start(bf16[16,2,128,128]{3,2,1,0:T(8,128)(2,1)} %get-tuple-element.27), calls=%async_computation | async-start | bytes 2097152 | tf_op jit(solution)/shard_map/all_to_all | solution.py:277
  16.2 21.7 %copy-start.1 = (s32[16]{0:T(128)S(1)}, s32[16]{0:T(128)}, u32[]{:S(2)}) copy-start(s32[16]{0:T(128)} %order_ref.1) | copy-start | bytes 196
  24.3 26.2 %collective-permute-start.5 = (bf16[3,2,512,128]{3,2,1,0:T(8,128)(2,1)}, bf16[3,2,512,128]{3,2,1,0:T(8,128)(2,1)}, u32[]{:S(2)}, u32[]{:S(2)}) collective-permute-start(bf16[3,2,512,128]{3,2,1,0:T(8,128)(2,1)} %pad_maximum_fusion), channel_id=1, source_target_pairs={{0,1},{1,0},{2,3},{3,2},{4,5},{5,4},{6,7},{7,6},{8,9},{9,8},{10,11... | collective-permute-start | bytes 2359304 | tf_op jit(solution)/shard_map/ppermute | solution.py:281
  26.4 0.8 copy-start.3
  27.1 23.4 %collective-permute-start = (bf16[4,512,128]{2,1,0:T(8,128)(2,1)}, bf16[4,512,128]{2,1,0:T(8,128)(2,1)}, u32[]{:S(2)}, u32[]{:S(2)}) collective-permute-start(bf16[4,512,128]{2,1,0:T(8,128)(2,1)} %get-tuple-element.15), channel_id=1, source_target_pairs={{0,7},{1,6},{2,5},{3,4},{4,3},{5,2},{6,1},{7,0},{8,15},{9,14},{10,... | collective-permute-start | bytes 1572872 | tf_op jit(solution)/shard_map/ppermute | solution.py:281
  33.1 17.4 %collective-permute-start.4 = (bf16[2,512,128]{2,1,0:T(8,128)(2,1)}, bf16[2,512,128]{2,1,0:T(8,128)(2,1)S(1)}, u32[]{:S(2)}, u32[]{:S(2)}) collective-permute-start(bf16[2,512,128]{2,1,0:T(8,128)(2,1)} %get-tuple-element.17.refs_2_), channel_id=1, source_target_pairs={{0,1},{1,0},{2,3},{3,2},{4,5},{5,4},{6,7},{7,6},{8,9},{9,8},{10,11... | collective-permute-start | bytes 786440 | tf_op jit(solution)/shard_map/ppermute | solution.py:281
  34.5 36.4 %collective-permute-start.6 = (bf16[4,512,128]{2,1,0:T(8,128)(2,1)}, bf16[4,512,128]{2,1,0:T(8,128)(2,1)S(1)}, u32[]{:S(2)}, u32[]{:S(2)}) collective-permute-start(bf16[4,512,128]{2,1,0:T(8,128)(2,1)} %get-tuple-element.22), channel_id=1, source_target_pairs={{0,3},{1,2},{2,1},{3,0},{4,7},{5,6},{6,5},{7,4},{8,11},{9,10},{10,... | collective-permute-start | bytes 1572872 | tf_op jit(solution)/shard_map/ppermute | solution.py:281
  34.5 16.0 %copy-start.2 = (s32[1,2]{1,0:T(1,128)S(1)}, s32[1,2]{1,0:T(1,128)}, u32[]{:S(2)}) copy-start(s32[1,2]{1,0:T(1,128)} %spans_ref.5) | copy-start | bytes 28
  34.5 16.0 %copy-start.4 = (bf16[4,512,128]{2,1,0:T(8,128)(2,1)S(1)}, bf16[4,512,128]{2,1,0:T(8,128)(2,1)}, u32[]{:S(2)}) copy-start(bf16[4,512,128]{2,1,0:T(8,128)(2,1)} %copy-done.3) | copy-start | bytes 1572868
  34.5 36.4 %collective-permute-start.7 = (bf16[4,512,128]{2,1,0:T(8,128)(2,1)}, bf16[4,512,128]{2,1,0:T(8,128)(2,1)S(1)}, u32[]{:S(2)}, u32[]{:S(2)}) collective-permute-start(bf16[4,512,128]{2,1,0:T(8,128)(2,1)} %get-tuple-element.23), channel_id=1, source_target_pairs={{0,4},{1,5},{2,6},{3,7},{4,0},{5,1},{6,2},{7,3},{8,12},{9,13},{10,... | collective-permute-start | bytes 1572872 | tf_op jit(solution)/shard_map/ppermute | solution.py:281
  39.4 59.9 %all-to-all-start.1 = ((bf16[16,2,128,128]{3,2,1,0:T(8,128)(2,1)}), bf16[16,2,128,128]{3,2,1,0:T(8,128)(2,1)S(1)}, u32[]{:S(2)}, u32[]{:S(2)}) async-start(bf16[16,2,128,128]{3,2,1,0:T(8,128)(2,1)} %shard_map.73), calls=%async_computation.1 | async-start | bytes 2097152 | tf_op jit(solution)/shard_map/all_to_all | solution.py:277
  65.5 21.3 %collective-permute-start.10 = (bf16[4,512,128]{2,1,0:T(8,128)(2,1)S(1)}, bf16[4,512,128]{2,1,0:T(8,128)(2,1)S(1)}, u32[]{:S(2)}, u32[]{:S(2)}) collective-permute-start(bf16[4,512,128]{2,1,0:T(8,128)(2,1)S(1)} %get-tuple-element.26), channel_id=1, source_target_pairs={{0,7},{1,6},{2,5},{3,4},{4,3},{5,2},{6,1},{7,0},{8,15},{9,14},{10,... | collective-permute-start | bytes 1572872 | tf_op jit(solution)/shard_map/ppermute | solution.py:281
  85.7 10.5 %collective-permute-start.8 = (bf16[4,512,128]{2,1,0:T(8,128)(2,1)S(1)}, bf16[4,512,128]{2,1,0:T(8,128)(2,1)S(1)}, u32[]{:S(2)}, u32[]{:S(2)}) collective-permute-start(bf16[4,512,128]{2,1,0:T(8,128)(2,1)S(1)} %get-tuple-element.24), channel_id=1, source_target_pairs={{0,3},{1,2},{2,1},{3,0},{4,7},{5,6},{6,5},{7,4},{8,11},{9,10},{10,... | collective-permute-start | bytes 1572872 | tf_op jit(solution)/shard_map/ppermute | solution.py:281
  86.3 10.7 %collective-permute-start.9 = (bf16[4,512,128]{2,1,0:T(8,128)(2,1)S(1)}, bf16[4,512,128]{2,1,0:T(8,128)(2,1)S(1)}, u32[]{:S(2)}, u32[]{:S(2)}) collective-permute-start(bf16[4,512,128]{2,1,0:T(8,128)(2,1)S(1)} %get-tuple-element.25), channel_id=1, source_target_pairs={{0,4},{1,5},{2,6},{3,7},{4,0},{5,1},{6,2},{7,3},{8,12},{9,13},{10,... | collective-permute-start | bytes 1572872 | tf_op jit(solution)/shard_map/ppermute | solution.py:281

commit v2 on v1

--- a/solution.py
+++ b/solution.py
@@ -122,7 +122,7 @@
     )(*pieces)
 
 
-def attend(which, queries, own, other_first, other_rest, spans, stripes):
+def attend(which, queries, own, other, spans, stripes):
     asked = len(which)
     members = len(own)
     heads, rows, width = queries[0].shape
@@ -132,9 +132,9 @@
     log2_scale = 1.4426950408889634 / math.sqrt(width)
 
     def kernel(spans_ref, *refs):
-        q_refs, own_refs = refs[:asked], refs[asked : asked + members]
-        first_ref, rest_ref, *o_refs = refs[asked + members : 2 * asked + members + 2]
-        key_blocks, values_t, query_t, mixed, peak, held = refs[2 * asked + members + 2 :]
+        q_refs, kv_refs = refs[:asked], refs[asked : asked + blocks]
+        o_refs = refs[asked + blocks : 2 * asked + blocks]
+        key_blocks, values_t, query_t, mixed, peak, held = refs[2 * asked + blocks :]
         step = pl.program_id(0)
         ctx = lax.axis_index("ctx")
         live = spans_ref[0, 0] + spans_ref[0, 1]
@@ -144,8 +144,7 @@
 
         @pl.when(step == 0)
         def _():
-            rest = [rest_ref.at[m] for m in range(members - 1)]
-            for m, source in enumerate((*own_refs, first_ref, *rest)):
+            for m, source in enumerate(kv_refs):
                 there = ctx ^ flips[m] if m < members else ctx ^ 1 ^ flips[m - members]
                 key_blocks[there] = source[0]
                 values_t[there, :width] = source[1].T
@@ -230,7 +229,7 @@
                     def _():
                         o_refs[m][h] = mixture
 
-    arrays = (*queries, *own, other_first, other_rest)
+    arrays = (*queries, *own, *other)
     return pl.pallas_call(
         kernel,
         grid_spec=pltpu.PrefetchScalarGridSpec(
@@ -273,6 +272,25 @@
     )(order, array)
 
 
+def place_rows(cache, held_rows):
+    count, two, short, width = cache.shape
+    blocks = count // held_rows
+    out_shape = jax.ShapeDtypeStruct((held_rows, two, 1, blocks, short, width), cache.dtype)
+
+    def kernel(in_ref, out_ref):
+        for i in range(count):
+            for t in range(two):
+                out_ref[i % held_rows, t, 0, i // held_rows] = in_ref[i, t]
+
+    return pl.pallas_call(
+        kernel,
+        in_specs=[whole(cache)],
+        out_specs=whole(out_shape),
+        out_shape=out_shape,
+        compiler_params=small(8),
+    )(cache)
+
+
 def swap(array, axis):
     return lax.all_to_all(array, axis, split_axis=0, concat_axis=0, tiled=True)
 
@@ -294,21 +312,20 @@
     other_first = send(kv_out[0], 1)
     q_out = pack_queries(queries)
     q_own = [q_out[0]] + [send(q_out[k], flips[k]) for k in (1, 2, 3)]
-    other_rest = send(jnp.stack(own[1:]), 1)
+    other = [other_first] + [send(own[k], 1) for k in (1, 2, 3)]
 
     by_prompt = swap(slot_rows, "prompt")
     by_row = take_blocks(by_prompt, partner)
     cache = swap(by_row, "ctx")
-    held_rows = slots // blocks
-    cache = cache.reshape(blocks, held_rows, 2, rows // stripes, width).transpose(1, 2, 0, 3, 4)
+    cache = place_rows(cache, slots // blocks)
 
     done = [None] * 4
     for which in ((1, 2), (3, 0)):
         asked = [q_own[k] for k in which]
-        for k, result in zip(which, attend(which, asked, own, other_first, other_rest, spans, stripes)):
+        for k, result in zip(which, attend(which, asked, own, other, spans, stripes)):
             done[k] = result
     back = [done[0]] + [send(done[k], flips[k]) for k in (1, 2, 3)]
-    return join_heads(back), cache[:, :, None]
+    return join_heads(back), cache
 
 
 def solution(mesh):

time: 101 us -> 116 us (1.15)
  the two profiles are of different devices: /device:TPU:0 before, /device:TPU:38 now
where the time goes in v2:
time: 116 us; the launch traced here: 115 us
  starting transfers between devices  46.7 us (40%)
  waiting for transfers between devices  33.5 us (29%)
  Pallas kernels  29.3 us (25%)
  local copies, waits for them, and re-layouts  4.78 us (4%)
    ppermute x13, starting transfers between devices, send(): return lax.ppermute(array, 'ctx', route(flip))  35.5 us
    ppermute x13, waiting for transfers between devices, send(): return lax.ppermute(array, 'ctx', route(flip))  33.5 us
    pallas_call x2, Pallas kernels, attend(): pl.pallas_call(kernel, grid_spec=pltpu.PrefetchScalarGridSpec(num_scalar_...  19.8 us
    all_to_all x2, starting transfers between devices, swap(): return lax.all_to_all(array, axis, split_axis=0, concat_axis=0, tiled=True)  11.3 us
    unnamed x32, local copies, waits for them, and re-layouts  4.78 us
    pallas_call x1, Pallas kernels, pack_kv(): pl.pallas_call(kernel, in_specs=[pl.BlockSpec(memory_space=pltpu.HBM)] *...  2.79 us
    pallas_call x1, Pallas kernels, join_heads(): pl.pallas_call(kernel, in_specs=[whole(piece) for piece in pieces], out_s...  2.35 us
  transfers between devices with their start and end apart: 15, of which 6 were waited for; matrix products, arithmetic and copies ran while one was open for 0% of the time, Pallas kernels for 22%

profile of v2, /device:TPU:38, one launch (start us, length us, event | category | flops | bytes accessed | tf_op | source)
XLA Modules:
  0.0 115.1 jit_solution(3126867958675441074)
XLA Ops:
  0.6 2.8 %shard_map.69 = (bf16[2,512,128]{2,1,0:T(8,128)(2,1)}, bf16[2,512,128]{2,1,0:T(8,128)(2,1)}, bf16[2,512,128]{2,1,0:T(8,128)(2,1)}, bf16[2,512,128]{2,1,0:T(8,128)(2,1)}, bf16[16,2,128,128]{3,2,1,0:T(8,128)(2,1)}) custom-call(s32[1,2]{1,0:T(1,128)} %spans_ref.5, bf16[128,16,128]{2,1,0:T(8,128)(2,1)} %bitcast.2, bf16[128,16,128]{2,1,0:T(8,128)(2,1)} %bitcast.3), custom_call_target="tpu_custom_call" | custom-call | tf_op jit(solution)/shard_map/pallas_call | solution.py:66
  3.4 0.0 copy-start
  3.4 3.1 %collective-permute-start.1 = (bf16[2,512,128]{2,1,0:T(8,128)(2,1)}, bf16[2,512,128]{2,1,0:T(8,128)(2,1)}, u32[]{:S(2)}, u32[]{:S(2)}) collective-permute-start(bf16[2,512,128]{2,1,0:T(8,128)(2,1)} %get-tuple-element.18), channel_id=1, source_target_pairs={{0,3},{1,2},{2,1},{3,0},{4,7},{5,6},{6,5},{7,4},{8,11},{9,10},{10,... | collective-permute-start | bytes 786440 | tf_op jit(solution)/shard_map/ppermute | solution.py:299
  6.5 6.5 %all-to-all-start = ((bf16[16,2,128,128]{3,2,1,0:T(8,128)(2,1)}), bf16[16,2,128,128]{3,2,1,0:T(8,128)(2,1)S(1)}, u32[]{:S(2)}, u32[]{:S(2)}) async-start(bf16[16,2,128,128]{3,2,1,0:T(8,128)(2,1)} %get-tuple-element.27), calls=%async_computation | async-start | bytes 2097152 | tf_op jit(solution)/shard_map/all_to_all | solution.py:295
  13.0 1.4 %collective-permute-start.2 = (bf16[2,512,128]{2,1,0:T(8,128)(2,1)}, bf16[2,512,128]{2,1,0:T(8,128)(2,1)S(1)}, u32[]{:S(2)}, u32[]{:S(2)}) collective-permute-start(bf16[2,512,128]{2,1,0:T(8,128)(2,1)} %get-tuple-element.19), channel_id=1, source_target_pairs={{0,4},{1,5},{2,6},{3,7},{4,0},{5,1},{6,2},{7,3},{8,12},{9,13},{10,... | collective-permute-start | bytes 786440 | tf_op jit(solution)/shard_map/ppermute | solution.py:299
  14.4 1.8 %collective-permute-start.3 = (bf16[2,512,128]{2,1,0:T(8,128)(2,1)}, bf16[2,512,128]{2,1,0:T(8,128)(2,1)S(1)}, u32[]{:S(2)}, u32[]{:S(2)}) collective-permute-start(bf16[2,512,128]{2,1,0:T(8,128)(2,1)} %get-tuple-element.20), channel_id=1, source_target_pairs={{0,7},{1,6},{2,5},{3,4},{4,3},{5,2},{6,1},{7,0},{8,15},{9,14},{10,... | collective-permute-start | bytes 786440 | tf_op jit(solution)/shard_map/ppermute | solution.py:299
  16.2 1.8 %shard_map.68 = (bf16[4,512,128]{2,1,0:T(8,128)(2,1)S(1)}, bf16[4,512,128]{2,1,0:T(8,128)(2,1)}, bf16[4,512,128]{2,1,0:T(8,128)(2,1)}, bf16[4,512,128]{2,1,0:T(8,128)(2,1)S(1)}) custom-call(bf16[512,16,128]{2,1,0:T(8,128)(2,1)S(1)} %copy-done), custom_call_target="tpu_custom_call" | custom-call | tf_op jit(solution)/shard_map/pallas_call | solution.py:94
  18.0 3.9 %collective-permute-start = (bf16[4,512,128]{2,1,0:T(8,128)(2,1)S(1)}, bf16[4,512,128]{2,1,0:T(8,128)(2,1)S(1)}, u32[]{:S(2)}, u32[]{:S(2)}) collective-permute-start(bf16[4,512,128]{2,1,0:T(8,128)(2,1)S(1)} %get-tuple-element.15), channel_id=1, source_target_pairs={{0,7},{1,6},{2,5},{3,4},{4,3},{5,2},{6,1},{7,0},{8,15},{9,14},{10,... | collective-permute-start | bytes 1572872 | tf_op jit(solution)/shard_map/ppermute | solution.py:299
  21.9 2.0 %collective-permute-start.5 = (bf16[2,512,128]{2,1,0:T(8,128)(2,1)}, bf16[2,512,128]{2,1,0:T(8,128)(2,1)S(1)}, u32[]{:S(2)}, u32[]{:S(2)}) collective-permute-start(bf16[2,512,128]{2,1,0:T(8,128)(2,1)} %collective-permute-done.1.refs_3_), channel_id=1, source_target_pairs={{0,1},{1,0},{2,3},{3,2},{4,5},{5,4},{6,7},{7,6},{8,9},{9,8},{10,11... | collective-permute-start | bytes 786440 | tf_op jit(solution)/shard_map/ppermute | solution.py:299
  23.9 9.2 %collective-permute-done.2.refs_4_ = bf16[2,512,128]{2,1,0:T(8,128)(2,1)S(1)} collective-permute-done((bf16[2,512,128]{2,1,0:T(8,128)(2,1)}, bf16[2,512,128]{2,1,0:T(8,128)(2,1)S(1)}, u32[]{:S(2)}, u32[]{:S(2)}) %collective-permute-start.2) | collective-permute-done | bytes 262176 | tf_op jit(solution)/shard_map/ppermute | solution.py:299
  33.1 0.1 collective-permute-start.6
  33.2 5.1 %collective-permute-done.3.refs_5_ = bf16[2,512,128]{2,1,0:T(8,128)(2,1)S(1)} collective-permute-done((bf16[2,512,128]{2,1,0:T(8,128)(2,1)}, bf16[2,512,128]{2,1,0:T(8,128)(2,1)S(1)}, u32[]{:S(2)}, u32[]{:S(2)}) %collective-permute-start.3) | collective-permute-done | bytes 262176 | tf_op jit(solution)/shard_map/ppermute | solution.py:299
  38.4 0.4 collective-permute-start.7
  38.7 2.7 %collective-permute-start.8 = (bf16[4,512,128]{2,1,0:T(8,128)(2,1)}, bf16[4,512,128]{2,1,0:T(8,128)(2,1)S(1)}, u32[]{:S(2)}, u32[]{:S(2)}) collective-permute-start(bf16[4,512,128]{2,1,0:T(8,128)(2,1)} %get-tuple-element.22), channel_id=1, source_target_pairs={{0,3},{1,2},{2,1},{3,0},{4,7},{5,6},{6,5},{7,4},{8,11},{9,10},{10,... | collective-permute-start | bytes 1572872 | tf_op jit(solution)/shard_map/ppermute | solution.py:299
  41.5 2.1 %collective-permute-start.9 = (bf16[4,512,128]{2,1,0:T(8,128)(2,1)}, bf16[4,512,128]{2,1,0:T(8,128)(2,1)}, u32[]{:S(2)}, u32[]{:S(2)}) collective-permute-start(bf16[4,512,128]{2,1,0:T(8,128)(2,1)} %get-tuple-element.23), channel_id=1, source_target_pairs={{0,4},{1,5},{2,6},{3,7},{4,0},{5,1},{6,2},{7,3},{8,12},{9,13},{10,... | collective-permute-start | bytes 1572872 | tf_op jit(solution)/shard_map/ppermute | solution.py:299
  43.6 2.6 %collective-permute-done.7.refs_9_ = bf16[2,512,128]{2,1,0:T(8,128)(2,1)S(1)} collective-permute-done((bf16[2,512,128]{2,1,0:T(8,128)(2,1)S(1)}, bf16[2,512,128]{2,1,0:T(8,128)(2,1)S(1)}, u32[]{:S(2)}, u32[]{:S(2)}) %collective-permute-start.7) | collective-permute-done | bytes 262176 | tf_op jit(solution)/shard_map/ppermute | solution.py:299
  46.2 3.4 %collective-permute-done.refs_0_ = bf16[4,512,128]{2,1,0:T(8,128)(2,1)S(1)} collective-permute-done((bf16[4,512,128]{2,1,0:T(8,128)(2,1)S(1)}, bf16[4,512,128]{2,1,0:T(8,128)(2,1)S(1)}, u32[]{:S(2)}, u32[]{:S(2)}) %collective-permute-start) | collective-permute-done | bytes 524320 | tf_op jit(solution)/shard_map/ppermute | solution.py:299
  49.7 15.4 %shard_map.70 = (bf16[4,512,128]{2,1,0:T(8,128)(2,1)}, bf16[4,512,128]{2,1,0:T(8,128)(2,1)S(1)}) custom-call(s32[1,2]{1,0:T(1,128)S(1)} %copy-done.2, bf16[4,512,128]{2,1,0:T(8,128)(2,1)S(1)} %collective-permute-done.refs_0_, bf16[4,512,128]{2,1,0:T(8,128)(2,1)S(1)} %get-tuple-element.16.refs_1_, bf16[2,512,128]{2,1,0:T(8,128)(2,1)S(1)} %copy-done.3, ...), custom_call_target="tpu_custom_call" | custom-call | flops 4294967296 | bytes 4194304 | tf_op jit(solution)/shard_map/pallas_call | solution.py:233
  65.1 4.8 %collective-permute-start.12 = (bf16[4,512,128]{2,1,0:T(8,128)(2,1)}, bf16[4,512,128]{2,1,0:T(8,128)(2,1)S(1)}, u32[]{:S(2)}, u32[]{:S(2)}) collective-permute-start(bf16[4,512,128]{2,1,0:T(8,128)(2,1)} %get-tuple-element.26), channel_id=1, source_target_pairs={{0,7},{1,6},{2,5},{3,4},{4,3},{5,2},{6,1},{7,0},{8,15},{9,14},{10,... | collective-permute-start | bytes 1572872 | tf_op jit(solution)/shard_map/ppermute | solution.py:299
  69.9 1.6 %shard_map.73 = bf16[16,2,128,128]{3,2,1,0:T(8,128)(2,1)} custom-call(s32[16]{0:T(128)S(1)} %copy-done.1, bf16[16,2,128,128]{3,2,1,0:T(8,128)(2,1)S(1)} %all-to-all-done.in_ref), custom_call_target="tpu_custom_call" | custom-call | tf_op jit(solution)/shard_map/pallas_call | solution.py:266
  71.5 4.8 %all-to-all-start.1 = ((bf16[16,2,128,128]{3,2,1,0:T(8,128)(2,1)}), bf16[16,2,128,128]{3,2,1,0:T(8,128)(2,1)S(1)}, u32[]{:S(2)}, u32[]{:S(2)}) async-start(bf16[16,2,128,128]{3,2,1,0:T(8,128)(2,1)} %shard_map.73), calls=%async_computation.1 | async-start | bytes 2097152 | tf_op jit(solution)/shard_map/all_to_all | solution.py:295
  76.3 0.9 copy-done.7
  77.3 0.9 copy-done.9
  78.2 0.9 copy-done.11
  79.2 0.9 copy-done.13
  80.1 0.9 copy-done.15
  81.1 4.4 %shard_map.71 = (bf16[4,512,128]{2,1,0:T(8,128)(2,1)S(1)}, bf16[4,512,128]{2,1,0:T(8,128)(2,1)S(1)}) custom-call(s32[1,2]{1,0:T(1,128)S(1)} %copy-done.2, bf16[4,512,128]{2,1,0:T(8,128)(2,1)S(1)} %collective-permute-done.8.refs_0_, bf16[4,512,128]{2,1,0:T(8,128)(2,1)} %collective-permute-done.9.refs_1_, bf16[2,512,128]{2,1,0:T(8,128)(2,1)S(1)} %copy-done.3, ...), custom_call_target="tpu_custom_call" | custom-call | flops 4294967296 | bytes 4194304 | tf_op jit(solution)/shard_map/pallas_call | solution.py:233
  85.5 13.1 %collective-permute-start.10 = (bf16[4,512,128]{2,1,0:T(8,128)(2,1)S(1)}, bf16[4,512,128]{2,1,0:T(8,128)(2,1)S(1)}, u32[]{:S(2)}, u32[]{:S(2)}) collective-permute-start(bf16[4,512,128]{2,1,0:T(8,128)(2,1)S(1)} %get-tuple-element.24), channel_id=1, source_target_pairs={{0,3},{1,2},{2,1},{3,0},{4,7},{5,6},{6,5},{7,4},{8,11},{9,10},{10,... | collective-permute-start | bytes 1572872 | tf_op jit(solution)/shard_map/ppermute | solution.py:299
  98.6 10.2 %collective-permute-done.10.refs_1_ = bf16[4,512,128]{2,1,0:T(8,128)(2,1)S(1)} collective-permute-done((bf16[4,512,128]{2,1,0:T(8,128)(2,1)S(1)}, bf16[4,512,128]{2,1,0:T(8,128)(2,1)S(1)}, u32[]{:S(2)}, u32[]{:S(2)}) %collective-permute-start.10) | collective-permute-done | bytes 524320 | tf_op jit(solution)/shard_map/ppermute | solution.py:299
  108.7 3.0 %collective-permute-done.11.refs_2_ = bf16[4,512,128]{2,1,0:T(8,128)(2,1)S(1)} collective-permute-done((bf16[4,512,128]{2,1,0:T(8,128)(2,1)S(1)}, bf16[4,512,128]{2,1,0:T(8,128)(2,1)S(1)}, u32[]{:S(2)}, u32[]{:S(2)}) %collective-permute-start.11) | collective-permute-done | bytes 524320 | tf_op jit(solution)/shard_map/ppermute | solution.py:299
  111.7 2.3 %shard_map.72 = bf16[512,16,128]{2,1,0:T(8,128)(2,1)} custom-call(bf16[4,512,128]{2,1,0:T(8,128)(2,1)S(1)} %get-tuple-element.21.refs_0_, bf16[4,512,128]{2,1,0:T(8,128)(2,1)S(1)} %collective-permute-done.10.refs_1_, bf16[4,512,128]{2,1,0:T(8,128)(2,1)S(1)} %collective-permute-done.11.refs_2_, bf16[4,512,128]{2,1,0:T(8,128)(2,1)S(1)} %collective-permute-done.12.refs_3_), custom_call_target="tpu_custom_call" | custom-call | tf_op jit(solution)/shard_map/pallas_call | solution.py:115
  114.0 1.0 shard_map.74
  (37 shorter events, 0.1 us)
Async XLA Ops:
  3.4 12.8 %copy-start = (bf16[512,16,128]{2,1,0:T(8,128)(2,1)S(1)}, bf16[512,16,128]{2,1,0:T(8,128)(2,1)}, u32[]{:S(2)}) copy-start(bf16[512,16,128]{2,1,0:T(8,128)(2,1)} %q_ref.1) | copy-start | bytes 6291460
  3.4 18.4 %collective-permute-start.1 = (bf16[2,512,128]{2,1,0:T(8,128)(2,1)}, bf16[2,512,128]{2,1,0:T(8,128)(2,1)}, u32[]{:S(2)}, u32[]{:S(2)}) collective-permute-start(bf16[2,512,128]{2,1,0:T(8,128)(2,1)} %get-tuple-element.18), channel_id=1, source_target_pairs={{0,3},{1,2},{2,1},{3,0},{4,7},{5,6},{6,5},{7,4},{8,11},{9,10},{10,... | collective-permute-start | bytes 786440 | tf_op jit(solution)/shard_map/ppermute | solution.py:299
  6.5 15.3 %copy-start.3 = (bf16[2,512,128]{2,1,0:T(8,128)(2,1)S(1)}, bf16[2,512,128]{2,1,0:T(8,128)(2,1)}, u32[]{:S(2)}) copy-start(bf16[2,512,128]{2,1,0:T(8,128)(2,1)} %get-tuple-element.17.refs_2_) | copy-start | bytes 786436
  6.5 43.1 %copy-start.2 = (s32[1,2]{1,0:T(1,128)S(1)}, s32[1,2]{1,0:T(1,128)}, u32[]{:S(2)}) copy-start(s32[1,2]{1,0:T(1,128)} %spans_ref.5) | copy-start | bytes 28
  6.5 63.4 %all-to-all-start = ((bf16[16,2,128,128]{3,2,1,0:T(8,128)(2,1)}), bf16[16,2,128,128]{3,2,1,0:T(8,128)(2,1)S(1)}, u32[]{:S(2)}, u32[]{:S(2)}) async-start(bf16[16,2,128,128]{3,2,1,0:T(8,128)(2,1)} %get-tuple-element.27), calls=%async_computation | async-start | bytes 2097152 | tf_op jit(solution)/shard_map/all_to_all | solution.py:295
  13.0 20.1 %collective-permute-start.2 = (bf16[2,512,128]{2,1,0:T(8,128)(2,1)}, bf16[2,512,128]{2,1,0:T(8,128)(2,1)S(1)}, u32[]{:S(2)}, u32[]{:S(2)}) collective-permute-start(bf16[2,512,128]{2,1,0:T(8,128)(2,1)} %get-tuple-element.19), channel_id=1, source_target_pairs={{0,4},{1,5},{2,6},{3,7},{4,0},{5,1},{6,2},{7,3},{8,12},{9,13},{10,... | collective-permute-start | bytes 786440 | tf_op jit(solution)/shard_map/ppermute | solution.py:299
  14.4 24.0 %collective-permute-start.3 = (bf16[2,512,128]{2,1,0:T(8,128)(2,1)}, bf16[2,512,128]{2,1,0:T(8,128)(2,1)S(1)}, u32[]{:S(2)}, u32[]{:S(2)}) collective-permute-start(bf16[2,512,128]{2,1,0:T(8,128)(2,1)} %get-tuple-element.20), channel_id=1, source_target_pairs={{0,7},{1,6},{2,5},{3,4},{4,3},{5,2},{6,1},{7,0},{8,15},{9,14},{10,... | collective-permute-start | bytes 786440 | tf_op jit(solution)/shard_map/ppermute | solution.py:299
  18.0 31.6 %collective-permute-start = (bf16[4,512,128]{2,1,0:T(8,128)(2,1)S(1)}, bf16[4,512,128]{2,1,0:T(8,128)(2,1)S(1)}, u32[]{:S(2)}, u32[]{:S(2)}) collective-permute-start(bf16[4,512,128]{2,1,0:T(8,128)(2,1)S(1)} %get-tuple-element.15), channel_id=1, source_target_pairs={{0,7},{1,6},{2,5},{3,4},{4,3},{5,2},{6,1},{7,0},{8,15},{9,14},{10,... | collective-permute-start | bytes 1572872 | tf_op jit(solution)/shard_map/ppermute | solution.py:299
  21.9 16.9 %collective-permute-start.4 = (bf16[2,512,128]{2,1,0:T(8,128)(2,1)S(1)}, bf16[2,512,128]{2,1,0:T(8,128)(2,1)S(1)}, u32[]{:S(2)}, u32[]{:S(2)}) collective-permute-start(bf16[2,512,128]{2,1,0:T(8,128)(2,1)S(1)} %copy-done.3), channel_id=1, source_target_pairs={{0,1},{1,0},{2,3},{3,2},{4,5},{5,4},{6,7},{7,6},{8,9},{9,8},{10,11... | collective-permute-start | bytes 786440 | tf_op jit(solution)/shard_map/ppermute | solution.py:299
  21.9 19.6 %collective-permute-start.5 = (bf16[2,512,128]{2,1,0:T(8,128)(2,1)}, bf16[2,512,128]{2,1,0:T(8,128)(2,1)S(1)}, u32[]{:S(2)}, u32[]{:S(2)}) collective-permute-start(bf16[2,512,128]{2,1,0:T(8,128)(2,1)} %collective-permute-done.1.refs_3_), channel_id=1, source_target_pairs={{0,1},{1,0},{2,3},{3,2},{4,5},{5,4},{6,7},{7,6},{8,9},{9,8},{10,11... | collective-permute-start | bytes 786440 | tf_op jit(solution)/shard_map/ppermute | solution.py:299
  33.1 31.9 %copy-start.4 = (bf16[2,512,128]{2,1,0:T(8,128)(2,1)}, bf16[2,512,128]{2,1,0:T(8,128)(2,1)S(1)}, u32[]{:S(2)}) copy-start(bf16[2,512,128]{2,1,0:T(8,128)(2,1)S(1)} %collective-permute-done.2.refs_4_) | copy-start | bytes 786436
  33.1 10.5 %collective-permute-start.6 = (bf16[2,512,128]{2,1,0:T(8,128)(2,1)S(1)}, bf16[2,512,128]{2,1,0:T(8,128)(2,1)S(1)}, u32[]{:S(2)}, u32[]{:S(2)}) collective-permute-start(bf16[2,512,128]{2,1,0:T(8,128)(2,1)S(1)} %collective-permute-done.2.refs_4_), channel_id=1, source_target_pairs={{0,1},{1,0},{2,3},{3,2},{4,5},{5,4},{6,7},{7,6},{8,9},{9,8},{10,11... | collective-permute-start | bytes 786440 | tf_op jit(solution)/shard_map/ppermute | solution.py:299
  38.4 26.6 %copy-start.6 = (bf16[2,512,128]{2,1,0:T(8,128)(2,1)}, bf16[2,512,128]{2,1,0:T(8,128)(2,1)S(1)}, u32[]{:S(2)}) copy-start(bf16[2,512,128]{2,1,0:T(8,128)(2,1)S(1)} %collective-permute-done.3.refs_5_) | copy-start | bytes 786436
  38.4 7.8 %collective-permute-start.7 = (bf16[2,512,128]{2,1,0:T(8,128)(2,1)S(1)}, bf16[2,512,128]{2,1,0:T(8,128)(2,1)S(1)}, u32[]{:S(2)}, u32[]{:S(2)}) collective-permute-start(bf16[2,512,128]{2,1,0:T(8,128)(2,1)S(1)} %collective-permute-done.3.refs_5_), channel_id=1, source_target_pairs={{0,1},{1,0},{2,3},{3,2},{4,5},{5,4},{6,7},{7,6},{8,9},{9,8},{10,11... | collective-permute-start | bytes 786440 | tf_op jit(solution)/shard_map/ppermute | solution.py:299
  38.7 26.3 %copy-start.8 = (bf16[2,512,128]{2,1,0:T(8,128)(2,1)}, bf16[2,512,128]{2,1,0:T(8,128)(2,1)S(1)}, u32[]{:S(2)}) copy-start(bf16[2,512,128]{2,1,0:T(8,128)(2,1)S(1)} %collective-permute-done.4.refs_6_) | copy-start | bytes 786436
  38.7 37.6 %collective-permute-start.8 = (bf16[4,512,128]{2,1,0:T(8,128)(2,1)}, bf16[4,512,128]{2,1,0:T(8,128)(2,1)S(1)}, u32[]{:S(2)}, u32[]{:S(2)}) collective-permute-start(bf16[4,512,128]{2,1,0:T(8,128)(2,1)} %get-tuple-element.22), channel_id=1, source_target_pairs={{0,3},{1,2},{2,1},{3,0},{4,7},{5,6},{6,5},{7,4},{8,11},{9,10},{10,... | collective-permute-start | bytes 1572872 | tf_op jit(solution)/shard_map/ppermute | solution.py:299
  41.5 23.5 %copy-start.10 = (bf16[2,512,128]{2,1,0:T(8,128)(2,1)}, bf16[2,512,128]{2,1,0:T(8,128)(2,1)S(1)}, u32[]{:S(2)}) copy-start(bf16[2,512,128]{2,1,0:T(8,128)(2,1)S(1)} %collective-permute-done.5.refs_7_) | copy-start | bytes 786436
  41.5 34.8 %collective-permute-start.9 = (bf16[4,512,128]{2,1,0:T(8,128)(2,1)}, bf16[4,512,128]{2,1,0:T(8,128)(2,1)}, u32[]{:S(2)}, u32[]{:S(2)}) collective-permute-start(bf16[4,512,128]{2,1,0:T(8,128)(2,1)} %get-tuple-element.23), channel_id=1, source_target_pairs={{0,4},{1,5},{2,6},{3,7},{4,0},{5,1},{6,2},{7,3},{8,12},{9,13},{10,... | collective-permute-start | bytes 1572872 | tf_op jit(solution)/shard_map/ppermute | solution.py:299
  43.6 21.4 %copy-start.12 = (bf16[2,512,128]{2,1,0:T(8,128)(2,1)}, bf16[2,512,128]{2,1,0:T(8,128)(2,1)S(1)}, u32[]{:S(2)}) copy-start(bf16[2,512,128]{2,1,0:T(8,128)(2,1)S(1)} %collective-permute-done.6.refs_8_) | copy-start | bytes 786436
  46.2 18.8 %copy-start.14 = (bf16[2,512,128]{2,1,0:T(8,128)(2,1)}, bf16[2,512,128]{2,1,0:T(8,128)(2,1)S(1)}, u32[]{:S(2)}) copy-start(bf16[2,512,128]{2,1,0:T(8,128)(2,1)S(1)} %collective-permute-done.7.refs_9_) | copy-start | bytes 786436
  49.6 20.3 %copy-start.1 = (s32[16]{0:T(128)S(1)}, s32[16]{0:T(128)}, u32[]{:S(2)}) copy-start(s32[16]{0:T(128)} %order_ref.1) | copy-start | bytes 196
  65.0 11.3 %copy-start.5 = (bf16[2,512,128]{2,1,0:T(8,128)(2,1)S(1)}, bf16[2,512,128]{2,1,0:T(8,128)(2,1)}, u32[]{:S(2)}) copy-start(bf16[2,512,128]{2,1,0:T(8,128)(2,1)} %copy-done.4) | copy-start | bytes 786436
  65.1 33.5 %collective-permute-start.12 = (bf16[4,512,128]{2,1,0:T(8,128)(2,1)}, bf16[4,512,128]{2,1,0:T(8,128)(2,1)S(1)}, u32[]{:S(2)}, u32[]{:S(2)}) collective-permute-start(bf16[4,512,128]{2,1,0:T(8,128)(2,1)} %get-tuple-element.26), channel_id=1, source_target_pairs={{0,7},{1,6},{2,5},{3,4},{4,3},{5,2},{6,1},{7,0},{8,15},{9,14},{10,... | collective-permute-start | bytes 1572872 | tf_op jit(solution)/shard_map/ppermute | solution.py:299
  71.5 42.5 %all-to-all-start.1 = ((bf16[16,2,128,128]{3,2,1,0:T(8,128)(2,1)}), bf16[16,2,128,128]{3,2,1,0:T(8,128)(2,1)S(1)}, u32[]{:S(2)}, u32[]{:S(2)}) async-start(bf16[16,2,128,128]{3,2,1,0:T(8,128)(2,1)} %shard_map.73), calls=%async_computation.1 | async-start | bytes 2097152 | tf_op jit(solution)/shard_map/all_to_all | solution.py:295
  76.3 1.0 copy-start.7
  77.3 0.9 copy-start.9
  78.2 0.9 copy-start.11
  79.2 0.9 copy-start.13
  80.1 0.9 copy-start.15
  85.5 23.2 %collective-permute-start.10 = (bf16[4,512,128]{2,1,0:T(8,128)(2,1)S(1)}, bf16[4,512,128]{2,1,0:T(8,128)(2,1)S(1)}, u32[]{:S(2)}, u32[]{:S(2)}) collective-permute-start(bf16[4,512,128]{2,1,0:T(8,128)(2,1)S(1)} %get-tuple-element.24), channel_id=1, source_target_pairs={{0,3},{1,2},{2,1},{3,0},{4,7},{5,6},{6,5},{7,4},{8,11},{9,10},{10,... | collective-permute-start | bytes 1572872 | tf_op jit(solution)/shard_map/ppermute | solution.py:299
  98.5 13.1 %collective-permute-start.11 = (bf16[4,512,128]{2,1,0:T(8,128)(2,1)S(1)}, bf16[4,512,128]{2,1,0:T(8,128)(2,1)S(1)}, u32[]{:S(2)}, u32[]{:S(2)}) collective-permute-start(bf16[4,512,128]{2,1,0:T(8,128)(2,1)S(1)} %get-tuple-element.25), channel_id=1, source_target_pairs={{0,4},{1,5},{2,6},{3,7},{4,0},{5,1},{6,2},{7,3},{8,12},{9,13},{10,... | collective-permute-start | bytes 1572872 | tf_op jit(solution)/shard_map/ppermute | solution.py:299

commit v3 on v2

--- a/solution.py
+++ b/solution.py
@@ -134,39 +134,49 @@
     def kernel(spans_ref, *refs):
         q_refs, kv_refs = refs[:asked], refs[asked : asked + blocks]
         o_refs = refs[asked + blocks : 2 * asked + blocks]
-        key_blocks, values_t, query_t, mixed, peak, held = refs[2 * asked + blocks :]
+        scratch = refs[2 * asked + blocks :]
+        q_in, values_in, key_blocks, values_t, query_t, mixed, peak, held, o_out, q_sem, k_sem, v_sem, o_sem = scratch
         step = pl.program_id(0)
         ctx = lax.axis_index("ctx")
         live = spans_ref[0, 0] + spans_ref[0, 1]
         block = ctx ^ flips[which[0]]
         for m in range(1, asked):
             block = jnp.where(step == m, ctx ^ flips[which[m]], block)
+        theres = [ctx ^ flip for flip in flips] + [ctx ^ 1 ^ flip for flip in flips]
+        q_copies = [
+            pltpu.make_async_copy(q_refs[m], q_in.at[m], q_sem.at[m]) for m in range(asked)
+        ]
+        k_copies = [
+            pltpu.make_async_copy(kv_refs[m].at[0], key_blocks.at[theres[m]], k_sem.at[m])
+            for m in range(blocks)
+        ]
+        v_copies = [
+            pltpu.make_async_copy(kv_refs[m].at[1], values_in.at[m], v_sem.at[m])
+            for m in range(blocks)
+        ]
+        o_copies = [
+            pltpu.make_async_copy(o_out.at[m], o_refs[m], o_sem.at[m]) for m in range(asked)
+        ]
 
         @pl.when(step == 0)
         def _():
-            for m, source in enumerate(kv_refs):
-                there = ctx ^ flips[m] if m < members else ctx ^ 1 ^ flips[m - members]
-                key_blocks[there] = source[0]
-                values_t[there, :width] = source[1].T
+            for copy in (*v_copies, *q_copies, *k_copies):
+                copy.start()
             values_t[:, width:] = jnp.ones_like(values_t[:, width:])
+            for m in range(blocks):
+                v_copies[m].wait()
+                values_t[theres[m], :width] = values_in[m].T
+            for copy in (*q_copies, *k_copies):
+                copy.wait()
 
         @pl.when(block * rows >= live)
         def _():
-            for m in range(asked):
-
-                @pl.when(step == m)
-                def _():
-                    o_refs[m][...] = jnp.zeros_like(o_refs[m])
+            o_out[step] = jnp.zeros(o_out.shape[1:], o_out.dtype)
 
         @pl.when(block * rows < live)
         def _():
-            for m in range(asked):
-
-                @pl.when(step == m)
-                def _():
-                    for h in range(heads):
-                        query_t[:, h * rows : (h + 1) * rows] = q_refs[m][h].T
-
+            for h in range(heads):
+                query_t[:, h * rows : (h + 1) * rows] = q_in[step, h].T
             mixed[...] = jnp.zeros_like(mixed)
             peak[...] = jnp.full_like(peak, far_below)
 
@@ -222,12 +232,18 @@
             for h in range(heads):
                 part = slice(h * rows, (h + 1) * rows)
                 mixture = (mixed[:width, part] / mixed[width : width + 1, part]).T
-                mixture = jnp.where(position < live, mixture, 0.0).astype(jnp.bfloat16)
-                for m in range(asked):
-
-                    @pl.when(step == m)
-                    def _():
-                        o_refs[m][h] = mixture
+                o_out[step, h] = jnp.where(position < live, mixture, 0.0).astype(jnp.bfloat16)
+
+        for m in range(asked):
+
+            @pl.when(step == m)
+            def _():
+                o_copies[m].start()
+
+        @pl.when(step == asked - 1)
+        def _():
+            for copy in o_copies:
+                copy.wait()
 
     arrays = (*queries, *own, *other)
     return pl.pallas_call(
@@ -235,20 +251,28 @@
         grid_spec=pltpu.PrefetchScalarGridSpec(
             num_scalar_prefetch=0,
             grid=(asked,),
-            in_specs=[pl.BlockSpec(memory_space=pltpu.SMEM)] + [whole(array) for array in arrays],
-            out_specs=[whole(query) for query in queries],
+            in_specs=[pl.BlockSpec(memory_space=pltpu.SMEM)]
+            + [pl.BlockSpec(memory_space=pl.ANY)] * len(arrays),
+            out_specs=[pl.BlockSpec(memory_space=pl.ANY)] * asked,
             scratch_shapes=[
+                pltpu.VMEM((asked, heads, rows, width), jnp.bfloat16),
+                pltpu.VMEM((blocks, rows, width), jnp.bfloat16),
                 pltpu.VMEM((blocks, rows, width), jnp.bfloat16),
                 pltpu.VMEM((blocks, width + 16, rows), jnp.bfloat16),
                 pltpu.VMEM((width, columns), jnp.bfloat16),
                 pltpu.VMEM((width + 16, columns), jnp.float32),
                 pltpu.VMEM((1, columns), jnp.float32),
                 pltpu.VMEM((2, rows, columns), jnp.float32),
+                pltpu.VMEM((asked, heads, rows, width), jnp.bfloat16),
+                pltpu.SemaphoreType.DMA((asked,)),
+                pltpu.SemaphoreType.DMA((blocks,)),
+                pltpu.SemaphoreType.DMA((blocks,)),
+                pltpu.SemaphoreType.DMA((asked,)),
             ],
         ),
         out_shape=[jax.ShapeDtypeStruct(queries[0].shape, jnp.bfloat16)] * asked,
         compiler_params=pltpu.CompilerParams(
-            dimension_semantics=("arbitrary",), vmem_limit_bytes=30 * 1024 * 1024
+            dimension_semantics=("arbitrary",), vmem_limit_bytes=62 * 1024 * 1024
         ),
         cost_estimate=pl.CostEstimate(
             flops=4 * asked * members * heads * rows * rows * width,

time: 116 us -> 115 us (level)
  Pallas kernels: 29.3 us -> 32.6 us
  waiting for transfers between devices: 33.5 us -> 31.4 us
  local copies, waits for them, and re-layouts: 4.78 us -> 3.21 us
    pallas_call x2, Pallas kernels: 19.8 us -> 22.1 us  [attend(): pl.pallas_call(kernel, grid_spec=pltpu.PrefetchScalarGridSpec(num_scalar_...]
    ppermute x13, waiting for transfers between devices: 33.5 us -> 31.4 us  [send(): return lax.ppermute(array, 'ctx', route(flip))]
    unnamed x32 -> x26, local copies, waits for them, and re-layouts: 4.78 us -> 3.21 us
  transfers between devices with their start and end apart: 15 -> 15, of which waited for: 6 -> 7; matrix products, arithmetic and copies ran while one was open for 0% -> 0% of each run, Pallas kernels for 22% -> 25%
where the time goes in v3:
time: 115 us; the launch traced here: 114 us
  starting transfers between devices  46 us (40%)
  Pallas kernels  32.6 us (28%)
  waiting for transfers between devices  31.4 us (27%)
  local copies, waits for them, and re-layouts  3.21 us (3%)
    ppermute x13, starting transfers between devices, send(): return lax.ppermute(array, 'ctx', route(flip))  34.6 us
    ppermute x13, waiting for transfers between devices, send(): return lax.ppermute(array, 'ctx', route(flip))  31.4 us
    pallas_call x2, Pallas kernels, attend(): pl.pallas_call(kernel, grid_spec=pltpu.PrefetchScalarGridSpec(num_scalar_...  22.1 us
    all_to_all x2, starting transfers between devices, swap(): return lax.all_to_all(array, axis, split_axis=0, concat_axis=0, tiled=True)  11.4 us
    pallas_call x1, Pallas kernels, join_heads(): pl.pallas_call(kernel, in_specs=[whole(piece) for piece in pieces], out_s...  3.38 us
    unnamed x26, local copies, waits for them, and re-layouts  3.21 us
    pallas_call x1, Pallas kernels, pack_kv(): pl.pallas_call(kernel, in_specs=[pl.BlockSpec(memory_space=pltpu.HBM)] *...  2.79 us
  transfers between devices with their start and end apart: 15, of which 7 were waited for; matrix products, arithmetic and copies ran while one was open for 0% of the time, Pallas kernels for 25%

profile of v3, /device:TPU:38, one launch (start us, length us, event | category | flops | bytes accessed | tf_op | source)
XLA Modules:
  0.0 114.0 jit_solution(11020811714185307154)
XLA Ops:
  0.6 2.8 %shard_map.69 = (bf16[2,512,128]{2,1,0:T(8,128)(2,1)}, bf16[2,512,128]{2,1,0:T(8,128)(2,1)}, bf16[2,512,128]{2,1,0:T(8,128)(2,1)}, bf16[2,512,128]{2,1,0:T(8,128)(2,1)}, bf16[16,2,128,128]{3,2,1,0:T(8,128)(2,1)}) custom-call(s32[1,2]{1,0:T(1,128)} %spans_ref.5, bf16[128,16,128]{2,1,0:T(8,128)(2,1)} %bitcast.2, bf16[128,16,128]{2,1,0:T(8,128)(2,1)} %bitcast.3), custom_call_target="tpu_custom_call" | custom-call | tf_op jit(solution)/shard_map/pallas_call | solution.py:66
  3.4 3.1 %collective-permute-start.1 = (bf16[2,512,128]{2,1,0:T(8,128)(2,1)}, bf16[2,512,128]{2,1,0:T(8,128)(2,1)S(1)}, u32[]{:S(2)}, u32[]{:S(2)}) collective-permute-start(bf16[2,512,128]{2,1,0:T(8,128)(2,1)} %get-tuple-element.18), channel_id=1, source_target_pairs={{0,3},{1,2},{2,1},{3,0},{4,7},{5,6},{6,5},{7,4},{8,11},{9,10},{10,... | collective-permute-start | bytes 786440 | tf_op jit(solution)/shard_map/ppermute | solution.py:323
  6.5 6.5 %all-to-all-start = ((bf16[16,2,128,128]{3,2,1,0:T(8,128)(2,1)}), bf16[16,2,128,128]{3,2,1,0:T(8,128)(2,1)S(1)}, u32[]{:S(2)}, u32[]{:S(2)}) async-start(bf16[16,2,128,128]{3,2,1,0:T(8,128)(2,1)} %get-tuple-element.27), calls=%async_computation | async-start | bytes 2097152 | tf_op jit(solution)/shard_map/all_to_all | solution.py:319
  13.0 1.4 %collective-permute-start.2 = (bf16[2,512,128]{2,1,0:T(8,128)(2,1)}, bf16[2,512,128]{2,1,0:T(8,128)(2,1)S(1)}, u32[]{:S(2)}, u32[]{:S(2)}) collective-permute-start(bf16[2,512,128]{2,1,0:T(8,128)(2,1)} %get-tuple-element.19), channel_id=1, source_target_pairs={{0,4},{1,5},{2,6},{3,7},{4,0},{5,1},{6,2},{7,3},{8,12},{9,13},{10,... | collective-permute-start | bytes 786440 | tf_op jit(solution)/shard_map/ppermute | solution.py:323
  14.4 1.8 %collective-permute-start.3 = (bf16[2,512,128]{2,1,0:T(8,128)(2,1)}, bf16[2,512,128]{2,1,0:T(8,128)(2,1)S(1)}, u32[]{:S(2)}, u32[]{:S(2)}) collective-permute-start(bf16[2,512,128]{2,1,0:T(8,128)(2,1)} %get-tuple-element.20), channel_id=1, source_target_pairs={{0,7},{1,6},{2,5},{3,4},{4,3},{5,2},{6,1},{7,0},{8,15},{9,14},{10,... | collective-permute-start | bytes 786440 | tf_op jit(solution)/shard_map/ppermute | solution.py:323
  16.2 1.6 %copy-done = bf16[512,16,128]{2,1,0:T(8,128)(2,1)S(1)} copy-done((bf16[512,16,128]{2,1,0:T(8,128)(2,1)S(1)}, bf16[512,16,128]{2,1,0:T(8,128)(2,1)}, u32[]{:S(2)}) %copy-start) | copy-done | bytes 2097176
  17.8 1.8 %shard_map.68 = (bf16[4,512,128]{2,1,0:T(8,128)(2,1)S(1)}, bf16[4,512,128]{2,1,0:T(8,128)(2,1)}, bf16[4,512,128]{2,1,0:T(8,128)(2,1)}, bf16[4,512,128]{2,1,0:T(8,128)(2,1)S(1)}) custom-call(bf16[512,16,128]{2,1,0:T(8,128)(2,1)S(1)} %copy-done), custom_call_target="tpu_custom_call" | custom-call | tf_op jit(solution)/shard_map/pallas_call | solution.py:94
  19.6 0.8 copy-done.3
  20.4 3.9 %collective-permute-start = (bf16[4,512,128]{2,1,0:T(8,128)(2,1)S(1)}, bf16[4,512,128]{2,1,0:T(8,128)(2,1)S(1)}, u32[]{:S(2)}, u32[]{:S(2)}) collective-permute-start(bf16[4,512,128]{2,1,0:T(8,128)(2,1)S(1)} %get-tuple-element.15), channel_id=1, source_target_pairs={{0,7},{1,6},{2,5},{3,4},{4,3},{5,2},{6,1},{7,0},{8,15},{9,14},{10,... | collective-permute-start | bytes 1572872 | tf_op jit(solution)/shard_map/ppermute | solution.py:323
  24.2 0.0 collective-permute-start.4
  24.2 0.0 collective-permute-done.1.refs_3_
  24.2 2.0 %collective-permute-start.5 = (bf16[2,512,128]{2,1,0:T(8,128)(2,1)S(1)}, bf16[2,512,128]{2,1,0:T(8,128)(2,1)S(1)}, u32[]{:S(2)}, u32[]{:S(2)}) collective-permute-start(bf16[2,512,128]{2,1,0:T(8,128)(2,1)S(1)} %collective-permute-done.1.refs_3_), channel_id=1, source_target_pairs={{0,1},{1,0},{2,3},{3,2},{4,5},{5,4},{6,7},{7,6},{8,9},{9,8},{10,11... | collective-permute-start | bytes 786440 | tf_op jit(solution)/shard_map/ppermute | solution.py:323
  26.2 6.8 %collective-permute-done.2.refs_4_ = bf16[2,512,128]{2,1,0:T(8,128)(2,1)S(1)} collective-permute-done((bf16[2,512,128]{2,1,0:T(8,128)(2,1)}, bf16[2,512,128]{2,1,0:T(8,128)(2,1)S(1)}, u32[]{:S(2)}, u32[]{:S(2)}) %collective-permute-start.2) | collective-permute-done | bytes 262176 | tf_op jit(solution)/shard_map/ppermute | solution.py:323
  33.1 0.1 collective-permute-start.6
  33.2 5.1 %collective-permute-done.3.refs_5_ = bf16[2,512,128]{2,1,0:T(8,128)(2,1)S(1)} collective-permute-done((bf16[2,512,128]{2,1,0:T(8,128)(2,1)}, bf16[2,512,128]{2,1,0:T(8,128)(2,1)S(1)}, u32[]{:S(2)}, u32[]{:S(2)}) %collective-permute-start.3) | collective-permute-done | bytes 262176 | tf_op jit(solution)/shard_map/ppermute | solution.py:323
  38.4 0.4 collective-permute-start.7
  38.7 2.7 %collective-permute-start.8 = (bf16[4,512,128]{2,1,0:T(8,128)(2,1)}, bf16[4,512,128]{2,1,0:T(8,128)(2,1)}, u32[]{:S(2)}, u32[]{:S(2)}) collective-permute-start(bf16[4,512,128]{2,1,0:T(8,128)(2,1)} %get-tuple-element.22), channel_id=1, source_target_pairs={{0,3},{1,2},{2,1},{3,0},{4,7},{5,6},{6,5},{7,4},{8,11},{9,10},{10,... | collective-permute-start | bytes 1572872 | tf_op jit(solution)/shard_map/ppermute | solution.py:323
  41.5 2.1 %collective-permute-start.9 = (bf16[4,512,128]{2,1,0:T(8,128)(2,1)}, bf16[4,512,128]{2,1,0:T(8,128)(2,1)}, u32[]{:S(2)}, u32[]{:S(2)}) collective-permute-start(bf16[4,512,128]{2,1,0:T(8,128)(2,1)} %get-tuple-element.23), channel_id=1, source_target_pairs={{0,4},{1,5},{2,6},{3,7},{4,0},{5,1},{6,2},{7,3},{8,12},{9,13},{10,... | collective-permute-start | bytes 1572872 | tf_op jit(solution)/shard_map/ppermute | solution.py:323
  43.6 1.0 collective-permute-done.6.refs_8_
  44.6 3.9 %collective-permute-done.7.refs_9_ = bf16[2,512,128]{2,1,0:T(8,128)(2,1)S(1)} collective-permute-done((bf16[2,512,128]{2,1,0:T(8,128)(2,1)S(1)}, bf16[2,512,128]{2,1,0:T(8,128)(2,1)S(1)}, u32[]{:S(2)}, u32[]{:S(2)}) %collective-permute-start.7) | collective-permute-done | bytes 262176 | tf_op jit(solution)/shard_map/ppermute | solution.py:323
  48.6 1.1 collective-permute-done.refs_0_
  49.7 0.8 copy-done.4
  50.5 15.9 %shard_map.70 = (bf16[4,512,128]{2,1,0:T(8,128)(2,1)}, bf16[4,512,128]{2,1,0:T(8,128)(2,1)}) custom-call(s32[1,2]{1,0:T(1,128)} %spans_ref.5, bf16[4,512,128]{2,1,0:T(8,128)(2,1)} %copy-done.4, bf16[4,512,128]{2,1,0:T(8,128)(2,1)} %copy-done.3, bf16[2,512,128]{2,1,0:T(8,128)(2,1)} %get-tuple-element.17.refs_2_, bf16[2,512,128]{2,1,0:T(8,128)(2,1)} %copy-done.6, ...), custom_call_target="tpu_custom_call" | custom-call | flops 4294967296 | bytes 4194304 | tf_op jit(solution)/shard_map/pallas_call | solution.py:249
  66.3 4.7 %collective-permute-start.12 = (bf16[4,512,128]{2,1,0:T(8,128)(2,1)}, bf16[4,512,128]{2,1,0:T(8,128)(2,1)}, u32[]{:S(2)}, u32[]{:S(2)}) collective-permute-start(bf16[4,512,128]{2,1,0:T(8,128)(2,1)} %get-tuple-element.26), channel_id=1, source_target_pairs={{0,7},{1,6},{2,5},{3,4},{4,3},{5,2},{6,1},{7,0},{8,15},{9,14},{10,... | collective-permute-start | bytes 1572872 | tf_op jit(solution)/shard_map/ppermute | solution.py:323
  71.0 1.6 %shard_map.73 = bf16[16,2,128,128]{3,2,1,0:T(8,128)(2,1)} custom-call(s32[16]{0:T(128)S(1)} %copy-done.2, bf16[16,2,128,128]{3,2,1,0:T(8,128)(2,1)S(1)} %all-to-all-done.in_ref), custom_call_target="tpu_custom_call" | custom-call | tf_op jit(solution)/shard_map/pallas_call | solution.py:290
  72.6 5.0 %all-to-all-start.1 = ((bf16[16,2,128,128]{3,2,1,0:T(8,128)(2,1)}), bf16[16,2,128,128]{3,2,1,0:T(8,128)(2,1)S(1)}, u32[]{:S(2)}, u32[]{:S(2)}) async-start(bf16[16,2,128,128]{3,2,1,0:T(8,128)(2,1)} %shard_map.73), calls=%async_computation.1 | async-start | bytes 2097152 | tf_op jit(solution)/shard_map/all_to_all | solution.py:319
  77.6 6.2 %shard_map.71 = (bf16[4,512,128]{2,1,0:T(8,128)(2,1)}, bf16[4,512,128]{2,1,0:T(8,128)(2,1)}) custom-call(s32[1,2]{1,0:T(1,128)} %spans_ref.5, bf16[4,512,128]{2,1,0:T(8,128)(2,1)} %collective-permute-done.8.refs_0_, bf16[4,512,128]{2,1,0:T(8,128)(2,1)} %collective-permute-done.9.refs_1_, bf16[2,512,128]{2,1,0:T(8,128)(2,1)} %get-tuple-element.17.refs_2_, ...), custom_call_target="tpu_custom_call" | custom-call | flops 4294967296 | bytes 4194304 | tf_op jit(solution)/shard_map/pallas_call | solution.py:249
  83.8 12.4 %collective-permute-start.10 = (bf16[4,512,128]{2,1,0:T(8,128)(2,1)}, bf16[4,512,128]{2,1,0:T(8,128)(2,1)S(1)}, u32[]{:S(2)}, u32[]{:S(2)}) collective-permute-start(bf16[4,512,128]{2,1,0:T(8,128)(2,1)} %get-tuple-element.24), channel_id=1, source_target_pairs={{0,3},{1,2},{2,1},{3,0},{4,7},{5,6},{6,5},{7,4},{8,11},{9,10},{10,... | collective-permute-start | bytes 1572872 | tf_op jit(solution)/shard_map/ppermute | solution.py:323
  96.2 10.4 %collective-permute-done.10.refs_1_ = bf16[4,512,128]{2,1,0:T(8,128)(2,1)S(1)} collective-permute-done((bf16[4,512,128]{2,1,0:T(8,128)(2,1)}, bf16[4,512,128]{2,1,0:T(8,128)(2,1)S(1)}, u32[]{:S(2)}, u32[]{:S(2)}) %collective-permute-start.10) | collective-permute-done | bytes 524320 | tf_op jit(solution)/shard_map/ppermute | solution.py:323
  106.6 3.0 %collective-permute-done.11.refs_2_ = bf16[4,512,128]{2,1,0:T(8,128)(2,1)S(1)} collective-permute-done((bf16[4,512,128]{2,1,0:T(8,128)(2,1)}, bf16[4,512,128]{2,1,0:T(8,128)(2,1)S(1)}, u32[]{:S(2)}, u32[]{:S(2)}) %collective-permute-start.11) | collective-permute-done | bytes 524320 | tf_op jit(solution)/shard_map/ppermute | solution.py:323
  109.6 3.4 %shard_map.72 = bf16[512,16,128]{2,1,0:T(8,128)(2,1)} custom-call(bf16[4,512,128]{2,1,0:T(8,128)(2,1)S(1)} %copy-done.1, bf16[4,512,128]{2,1,0:T(8,128)(2,1)S(1)} %collective-permute-done.10.refs_1_, bf16[4,512,128]{2,1,0:T(8,128)(2,1)S(1)} %collective-permute-done.11.refs_2_, bf16[4,512,128]{2,1,0:T(8,128)(2,1)} %collective-permute-done.12.refs_3_), custom_call_target="tpu_custom_call" | custom-call | tf_op jit(solution)/shard_map/pallas_call | solution.py:115
  113.0 1.0 shard_map.74
  (31 shorter events, 0.1 us)
Async XLA Ops:
  3.4 20.8 %collective-permute-start.1 = (bf16[2,512,128]{2,1,0:T(8,128)(2,1)}, bf16[2,512,128]{2,1,0:T(8,128)(2,1)S(1)}, u32[]{:S(2)}, u32[]{:S(2)}) collective-permute-start(bf16[2,512,128]{2,1,0:T(8,128)(2,1)} %get-tuple-element.18), channel_id=1, source_target_pairs={{0,3},{1,2},{2,1},{3,0},{4,7},{5,6},{6,5},{7,4},{8,11},{9,10},{10,... | collective-permute-start | bytes 786440 | tf_op jit(solution)/shard_map/ppermute | solution.py:323
  6.5 17.7 %copy-start.5 = (bf16[2,512,128]{2,1,0:T(8,128)(2,1)S(1)}, bf16[2,512,128]{2,1,0:T(8,128)(2,1)}, u32[]{:S(2)}) copy-start(bf16[2,512,128]{2,1,0:T(8,128)(2,1)} %get-tuple-element.17.refs_2_) | copy-start | bytes 786436
  6.5 64.5 %all-to-all-start = ((bf16[16,2,128,128]{3,2,1,0:T(8,128)(2,1)}), bf16[16,2,128,128]{3,2,1,0:T(8,128)(2,1)S(1)}, u32[]{:S(2)}, u32[]{:S(2)}) async-start(bf16[16,2,128,128]{3,2,1,0:T(8,128)(2,1)} %get-tuple-element.27), calls=%async_computation | async-start | bytes 2097152 | tf_op jit(solution)/shard_map/all_to_all | solution.py:319
  13.0 20.1 %collective-permute-start.2 = (bf16[2,512,128]{2,1,0:T(8,128)(2,1)}, bf16[2,512,128]{2,1,0:T(8,128)(2,1)S(1)}, u32[]{:S(2)}, u32[]{:S(2)}) collective-permute-start(bf16[2,512,128]{2,1,0:T(8,128)(2,1)} %get-tuple-element.19), channel_id=1, source_target_pairs={{0,4},{1,5},{2,6},{3,7},{4,0},{5,1},{6,2},{7,3},{8,12},{9,13},{10,... | collective-permute-start | bytes 786440 | tf_op jit(solution)/shard_map/ppermute | solution.py:323
  14.4 24.0 %collective-permute-start.3 = (bf16[2,512,128]{2,1,0:T(8,128)(2,1)}, bf16[2,512,128]{2,1,0:T(8,128)(2,1)S(1)}, u32[]{:S(2)}, u32[]{:S(2)}) collective-permute-start(bf16[2,512,128]{2,1,0:T(8,128)(2,1)} %get-tuple-element.20), channel_id=1, source_target_pairs={{0,7},{1,6},{2,5},{3,4},{4,3},{5,2},{6,1},{7,0},{8,15},{9,14},{10,... | collective-permute-start | bytes 786440 | tf_op jit(solution)/shard_map/ppermute | solution.py:323
  16.2 1.6 %copy-start = (bf16[512,16,128]{2,1,0:T(8,128)(2,1)S(1)}, bf16[512,16,128]{2,1,0:T(8,128)(2,1)}, u32[]{:S(2)}) copy-start(bf16[512,16,128]{2,1,0:T(8,128)(2,1)} %q_ref.1) | copy-start | bytes 6291460
  19.6 0.8 copy-start.3
  20.4 29.3 %collective-permute-start = (bf16[4,512,128]{2,1,0:T(8,128)(2,1)S(1)}, bf16[4,512,128]{2,1,0:T(8,128)(2,1)S(1)}, u32[]{:S(2)}, u32[]{:S(2)}) collective-permute-start(bf16[4,512,128]{2,1,0:T(8,128)(2,1)S(1)} %get-tuple-element.15), channel_id=1, source_target_pairs={{0,7},{1,6},{2,5},{3,4},{4,3},{5,2},{6,1},{7,0},{8,15},{9,14},{10,... | collective-permute-start | bytes 1572872 | tf_op jit(solution)/shard_map/ppermute | solution.py:323
  24.2 14.5 %collective-permute-start.4 = (bf16[2,512,128]{2,1,0:T(8,128)(2,1)S(1)}, bf16[2,512,128]{2,1,0:T(8,128)(2,1)S(1)}, u32[]{:S(2)}, u32[]{:S(2)}) collective-permute-start(bf16[2,512,128]{2,1,0:T(8,128)(2,1)S(1)} %copy-done.5), channel_id=1, source_target_pairs={{0,1},{1,0},{2,3},{3,2},{4,5},{5,4},{6,7},{7,6},{8,9},{9,8},{10,11... | collective-permute-start | bytes 786440 | tf_op jit(solution)/shard_map/ppermute | solution.py:323
  24.2 25.4 %copy-start.6 = (bf16[2,512,128]{2,1,0:T(8,128)(2,1)}, bf16[2,512,128]{2,1,0:T(8,128)(2,1)S(1)}, u32[]{:S(2)}) copy-start(bf16[2,512,128]{2,1,0:T(8,128)(2,1)S(1)} %collective-permute-done.1.refs_3_) | copy-start | bytes 786436
  24.2 17.2 %collective-permute-start.5 = (bf16[2,512,128]{2,1,0:T(8,128)(2,1)S(1)}, bf16[2,512,128]{2,1,0:T(8,128)(2,1)S(1)}, u32[]{:S(2)}, u32[]{:S(2)}) collective-permute-start(bf16[2,512,128]{2,1,0:T(8,128)(2,1)S(1)} %collective-permute-done.1.refs_3_), channel_id=1, source_target_pairs={{0,1},{1,0},{2,3},{3,2},{4,5},{5,4},{6,7},{7,6},{8,9},{9,8},{10,11... | collective-permute-start | bytes 786440 | tf_op jit(solution)/shard_map/ppermute | solution.py:323
  33.1 16.6 %copy-start.7 = (bf16[2,512,128]{2,1,0:T(8,128)(2,1)}, bf16[2,512,128]{2,1,0:T(8,128)(2,1)S(1)}, u32[]{:S(2)}) copy-start(bf16[2,512,128]{2,1,0:T(8,128)(2,1)S(1)} %collective-permute-done.2.refs_4_) | copy-start | bytes 786436
  33.1 11.5 %collective-permute-start.6 = (bf16[2,512,128]{2,1,0:T(8,128)(2,1)S(1)}, bf16[2,512,128]{2,1,0:T(8,128)(2,1)S(1)}, u32[]{:S(2)}, u32[]{:S(2)}) collective-permute-start(bf16[2,512,128]{2,1,0:T(8,128)(2,1)S(1)} %collective-permute-done.2.refs_4_), channel_id=1, source_target_pairs={{0,1},{1,0},{2,3},{3,2},{4,5},{5,4},{6,7},{7,6},{8,9},{9,8},{10,11... | collective-permute-start | bytes 786440 | tf_op jit(solution)/shard_map/ppermute | solution.py:323
  38.4 11.3 %copy-start.8 = (bf16[2,512,128]{2,1,0:T(8,128)(2,1)}, bf16[2,512,128]{2,1,0:T(8,128)(2,1)S(1)}, u32[]{:S(2)}) copy-start(bf16[2,512,128]{2,1,0:T(8,128)(2,1)S(1)} %collective-permute-done.3.refs_5_) | copy-start | bytes 786436
  38.4 10.2 %collective-permute-start.7 = (bf16[2,512,128]{2,1,0:T(8,128)(2,1)S(1)}, bf16[2,512,128]{2,1,0:T(8,128)(2,1)S(1)}, u32[]{:S(2)}, u32[]{:S(2)}) collective-permute-start(bf16[2,512,128]{2,1,0:T(8,128)(2,1)S(1)} %collective-permute-done.3.refs_5_), channel_id=1, source_target_pairs={{0,1},{1,0},{2,3},{3,2},{4,5},{5,4},{6,7},{7,6},{8,9},{9,8},{10,11... | collective-permute-start | bytes 786440 | tf_op jit(solution)/shard_map/ppermute | solution.py:323
  38.7 10.9 %copy-start.9 = (bf16[2,512,128]{2,1,0:T(8,128)(2,1)}, bf16[2,512,128]{2,1,0:T(8,128)(2,1)S(1)}, u32[]{:S(2)}) copy-start(bf16[2,512,128]{2,1,0:T(8,128)(2,1)S(1)} %collective-permute-done.4.refs_6_) | copy-start | bytes 786436
  38.7 38.9 %collective-permute-start.8 = (bf16[4,512,128]{2,1,0:T(8,128)(2,1)}, bf16[4,512,128]{2,1,0:T(8,128)(2,1)}, u32[]{:S(2)}, u32[]{:S(2)}) collective-permute-start(bf16[4,512,128]{2,1,0:T(8,128)(2,1)} %get-tuple-element.22), channel_id=1, source_target_pairs={{0,3},{1,2},{2,1},{3,0},{4,7},{5,6},{6,5},{7,4},{8,11},{9,10},{10,... | collective-permute-start | bytes 1572872 | tf_op jit(solution)/shard_map/ppermute | solution.py:323
  41.5 8.2 %copy-start.10 = (bf16[2,512,128]{2,1,0:T(8,128)(2,1)}, bf16[2,512,128]{2,1,0:T(8,128)(2,1)S(1)}, u32[]{:S(2)}) copy-start(bf16[2,512,128]{2,1,0:T(8,128)(2,1)S(1)} %collective-permute-done.5.refs_7_) | copy-start | bytes 786436
  41.5 36.1 %collective-permute-start.9 = (bf16[4,512,128]{2,1,0:T(8,128)(2,1)}, bf16[4,512,128]{2,1,0:T(8,128)(2,1)}, u32[]{:S(2)}, u32[]{:S(2)}) collective-permute-start(bf16[4,512,128]{2,1,0:T(8,128)(2,1)} %get-tuple-element.23), channel_id=1, source_target_pairs={{0,4},{1,5},{2,6},{3,7},{4,0},{5,1},{6,2},{7,3},{8,12},{9,13},{10,... | collective-permute-start | bytes 1572872 | tf_op jit(solution)/shard_map/ppermute | solution.py:323
  44.6 5.0 %copy-start.11 = (bf16[2,512,128]{2,1,0:T(8,128)(2,1)}, bf16[2,512,128]{2,1,0:T(8,128)(2,1)S(1)}, u32[]{:S(2)}) copy-start(bf16[2,512,128]{2,1,0:T(8,128)(2,1)S(1)} %collective-permute-done.6.refs_8_) | copy-start | bytes 786436
  48.6 1.1 copy-start.12
  49.7 0.8 copy-start.4
  50.5 20.5 %copy-start.2 = (s32[16]{0:T(128)S(1)}, s32[16]{0:T(128)}, u32[]{:S(2)}) copy-start(s32[16]{0:T(128)} %order_ref.1) | copy-start | bytes 196
  66.3 29.9 %collective-permute-start.12 = (bf16[4,512,128]{2,1,0:T(8,128)(2,1)}, bf16[4,512,128]{2,1,0:T(8,128)(2,1)}, u32[]{:S(2)}, u32[]{:S(2)}) collective-permute-start(bf16[4,512,128]{2,1,0:T(8,128)(2,1)} %get-tuple-element.26), channel_id=1, source_target_pairs={{0,7},{1,6},{2,5},{3,4},{4,3},{5,2},{6,1},{7,0},{8,15},{9,14},{10,... | collective-permute-start | bytes 1572872 | tf_op jit(solution)/shard_map/ppermute | solution.py:323
  72.6 40.4 %all-to-all-start.1 = ((bf16[16,2,128,128]{3,2,1,0:T(8,128)(2,1)}), bf16[16,2,128,128]{3,2,1,0:T(8,128)(2,1)S(1)}, u32[]{:S(2)}, u32[]{:S(2)}) async-start(bf16[16,2,128,128]{3,2,1,0:T(8,128)(2,1)} %shard_map.73), calls=%async_computation.1 | async-start | bytes 2097152 | tf_op jit(solution)/shard_map/all_to_all | solution.py:319
  77.6 32.0 %copy-start.1 = (bf16[4,512,128]{2,1,0:T(8,128)(2,1)S(1)}, bf16[4,512,128]{2,1,0:T(8,128)(2,1)}, u32[]{:S(2)}) copy-start(bf16[4,512,128]{2,1,0:T(8,128)(2,1)} %get-tuple-element.21.refs_0_) | copy-start | bytes 1572868
  83.8 22.8 %collective-permute-start.10 = (bf16[4,512,128]{2,1,0:T(8,128)(2,1)}, bf16[4,512,128]{2,1,0:T(8,128)(2,1)S(1)}, u32[]{:S(2)}, u32[]{:S(2)}) collective-permute-start(bf16[4,512,128]{2,1,0:T(8,128)(2,1)} %get-tuple-element.24), channel_id=1, source_target_pairs={{0,3},{1,2},{2,1},{3,0},{4,7},{5,6},{6,5},{7,4},{8,11},{9,10},{10,... | collective-permute-start | bytes 1572872 | tf_op jit(solution)/shard_map/ppermute | solution.py:323
  96.2 13.4 %collective-permute-start.11 = (bf16[4,512,128]{2,1,0:T(8,128)(2,1)}, bf16[4,512,128]{2,1,0:T(8,128)(2,1)S(1)}, u32[]{:S(2)}, u32[]{:S(2)}) collective-permute-start(bf16[4,512,128]{2,1,0:T(8,128)(2,1)} %get-tuple-element.25), channel_id=1, source_target_pairs={{0,4},{1,5},{2,6},{3,7},{4,0},{5,1},{6,2},{7,3},{8,12},{9,13},{10,... | collective-permute-start | bytes 1572872 | tf_op jit(solution)/shard_map/ppermute | solution.py:323

commit v4 on v3

--- a/solution.py
+++ b/solution.py
@@ -29,6 +29,7 @@
     short, slots, width = keys.shape
     stripes = slots // kv_heads
     rows = short * stripes
+    run = short // 2
 
     def kernel(spans_ref, k_ref, v_ref, *refs):
         outs, slot_ref = refs[:4], refs[4]
@@ -49,9 +50,10 @@
         for k in range(4):
             for t in range(2):
                 for stripe in range(stripes):
-                    outs[k][t, stripe * short : (stripe + 1) * short, :] = turned[
-                        t, stripe * kv_heads + (group ^ k)
-                    ]
+                    slot = stripe * kv_heads + (group ^ k)
+                    for half in range(2):
+                        at = (half * stripes + stripe) * run
+                        outs[k][t, at : at + run, :] = turned[t, slot, half * run : (half + 1) * run]
         for slot in range(slots):
             position = (
                 first + lax.broadcasted_iota(jnp.int32, (short, 1), 0) * stripes + slot // kv_heads
@@ -82,6 +84,7 @@
 def pack_queries(queries):
     rows, head_count, width = queries.shape
     heads = head_count // 4
+    chunk = rows // 4
 
     def kernel(q_ref, *refs):
         outs, turned = refs[:4], refs[4]
@@ -93,16 +96,18 @@
     piece = jax.ShapeDtypeStruct((heads, rows, width), jnp.bfloat16)
     return pl.pallas_call(
         kernel,
-        in_specs=[whole(queries)],
-        out_specs=[whole(piece)] * 4,
+        grid=(4,),
+        in_specs=[pl.BlockSpec((chunk, head_count, width), lambda i: (i, 0, 0))],
+        out_specs=[pl.BlockSpec((heads, chunk, width), lambda i: (0, i, 0))] * 4,
         out_shape=[piece] * 4,
-        scratch_shapes=[pltpu.VMEM((head_count, rows, width), jnp.bfloat16)],
-        compiler_params=small(16),
+        scratch_shapes=[pltpu.VMEM((head_count, chunk, width), jnp.bfloat16)],
+        compiler_params=small(62),
     )(queries)
 
 
 def join_heads(pieces):
     heads, rows, width = pieces[0].shape
+    chunk = rows // 4
 
     def kernel(*refs):
         ins, out, gathered = refs[:4], refs[4], refs[5]
@@ -111,13 +116,13 @@
             gathered[pl.ds((group ^ k) * heads, heads)] = ins[k][...]
         out[...] = jnp.swapaxes(gathered[...], 0, 1)
 
-    out_shape = jax.ShapeDtypeStruct((rows, 4 * heads, width), jnp.bfloat16)
-    return pl.pallas_call(
-        kernel,
-        in_specs=[whole(piece) for piece in pieces],
-        out_specs=whole(out_shape),
-        out_shape=out_shape,
-        scratch_shapes=[pltpu.VMEM((4 * heads, rows, width), jnp.bfloat16)],
+    return pl.pallas_call(
+        kernel,
+        grid=(4,),
+        in_specs=[pl.BlockSpec((heads, chunk, width), lambda i: (0, i, 0))] * 4,
+        out_specs=pl.BlockSpec((chunk, 4 * heads, width), lambda i: (i, 0, 0)),
+        out_shape=jax.ShapeDtypeStruct((rows, 4 * heads, width), jnp.bfloat16),
+        scratch_shapes=[pltpu.VMEM((4 * heads, chunk, width), jnp.bfloat16)],
         compiler_params=small(16),
     )(*pieces)
 
@@ -183,13 +188,15 @@
             def scores(j, part):
                 return jnp.dot(key_blocks[j], query_t[:, part], preferred_element_type=jnp.float32)
 
-            def fold(s, j, part):
+            def fold(s, j, part, depth=rows):
                 old = peak[:, part]
                 new = jnp.maximum(old, jnp.max(s, axis=0, keepdims=True))
                 weights = jnp.exp2((s - new) * log2_scale)
                 factor = jnp.exp2((old - new) * log2_scale)
                 mixed[:, part] = mixed[:, part] * factor + jnp.dot(
-                    values_t[j], weights.astype(jnp.bfloat16), preferred_element_type=jnp.float32
+                    values_t[j, :, :depth],
+                    weights.astype(jnp.bfloat16),
+                    preferred_element_type=jnp.float32,
                 )
                 peak[:, part] = new
 
@@ -202,12 +209,16 @@
                     fold(s, j, part)
 
             def diagonal(slot):
-                for part in parts:
-                    key_row = lax.broadcasted_iota(jnp.int32, (rows, part_size), 0)
-                    key_pos = lax.rem(key_row, rows // stripes) * stripes + key_row // (rows // stripes)
-                    query_pos = lax.broadcasted_iota(jnp.int32, (rows, part_size), 1) + part.start
-                    allowed = key_pos <= lax.rem(query_pos, rows)
-                    fold(jnp.where(allowed, held[slot, :, part], far_below), block, part)
+                half, run = rows // 2, rows // stripes // 2
+                for a in range(0, columns, half):
+                    part = slice(a, a + half)
+                    depth = half if a % rows == 0 else rows
+                    key_row = lax.broadcasted_iota(jnp.int32, (depth, half), 0)
+                    within = lax.rem(key_row, half)
+                    key_pos = key_row - within + lax.rem(within, run) * stripes + within // run
+                    query_pos = lax.broadcasted_iota(jnp.int32, (depth, half), 1) + a % rows
+                    s = jnp.where(key_pos <= query_pos, held[slot, :depth, part], far_below)
+                    fold(s, block, part, depth)
 
             for part in parts:
                 held[0, :, part] = scores(0, part)

time: 115 us -> 115 us (level)
  local copies, waits for them, and re-layouts: 3.21 us -> 0.83 us
  Pallas kernels: 32.6 us -> 34.8 us
    pallas_call x2, Pallas kernels: 5.18 us -> 8.03 us  [the longest x1 4.06 us: pack_queries(): pl.pallas_call(kernel, grid=(4,), in_specs=[pl.BlockSpec((chunk, head_cou...]
    unnamed x26 -> x16, local copies, waits for them, and re-layouts: 3.21 us -> 0.83 us
  transfers between devices with their start and end apart: 15 -> 15, of which waited for: 7 -> 7; matrix products, arithmetic and copies ran while one was open for 0% -> 0% of each run, Pallas kernels for 25% -> 27%
where the time goes in v4:
time: 115 us; the launch traced here: 113 us
  starting transfers between devices  45.5 us (40%)
  Pallas kernels  34.8 us (30%)
  waiting for transfers between devices  31.5 us (27%)
    ppermute x13, starting transfers between devices, send(): return lax.ppermute(array, 'ctx', route(flip))  34.3 us
    ppermute x13, waiting for transfers between devices, send(): return lax.ppermute(array, 'ctx', route(flip))  31.5 us
    pallas_call x2, Pallas kernels, attend(): pl.pallas_call(kernel, grid_spec=pltpu.PrefetchScalarGridSpec(num_scalar_...  21.4 us
    all_to_all x2, starting transfers between devices, swap(): return lax.all_to_all(array, axis, split_axis=0, concat_axis=0, tiled=True)  11.3 us
    pallas_call x1, Pallas kernels, pack_queries(): pl.pallas_call(kernel, grid=(4,), in_specs=[pl.BlockSpec((chunk, head_cou...  4.06 us
    pallas_call x1, Pallas kernels, join_heads(): pl.pallas_call(kernel, grid=(4,), in_specs=[pl.BlockSpec((heads, chunk, w...  3.96 us
    pallas_call x1, Pallas kernels, pack_kv(): pl.pallas_call(kernel, in_specs=[pl.BlockSpec(memory_space=pltpu.HBM)] *...  2.79 us
  transfers between devices with their start and end apart: 15, of which 7 were waited for; matrix products, arithmetic and copies ran while one was open for 0% of the time, Pallas kernels for 27%

profile of v4, /device:TPU:38, one launch (start us, length us, event | category | flops | bytes accessed | tf_op | source)
XLA Modules:
  0.0 113.4 jit_solution(2903183844373441508)
XLA Ops:
  0.6 2.8 %shard_map.69 = (bf16[2,512,128]{2,1,0:T(8,128)(2,1)}, bf16[2,512,128]{2,1,0:T(8,128)(2,1)}, bf16[2,512,128]{2,1,0:T(8,128)(2,1)}, bf16[2,512,128]{2,1,0:T(8,128)(2,1)}, bf16[16,2,128,128]{3,2,1,0:T(8,128)(2,1)}) custom-call(s32[1,2]{1,0:T(1,128)} %spans_ref.5, bf16[128,16,128]{2,1,0:T(8,128)(2,1)} %bitcast.2, bf16[128,16,128]{2,1,0:T(8,128)(2,1)} %bitcast.3), custom_call_target="tpu_custom_call" | custom-call | tf_op jit(solution)/shard_map/pallas_call | solution.py:68
  3.4 3.1 %collective-permute-start.1 = (bf16[2,512,128]{2,1,0:T(8,128)(2,1)}, bf16[2,512,128]{2,1,0:T(8,128)(2,1)}, u32[]{:S(2)}, u32[]{:S(2)}) collective-permute-start(bf16[2,512,128]{2,1,0:T(8,128)(2,1)} %get-tuple-element.18), channel_id=1, source_target_pairs={{0,3},{1,2},{2,1},{3,0},{4,7},{5,6},{6,5},{7,4},{8,11},{9,10},{10,... | collective-permute-start | bytes 786440 | tf_op jit(solution)/shard_map/ppermute | solution.py:334
  6.5 6.5 %all-to-all-start = ((bf16[16,2,128,128]{3,2,1,0:T(8,128)(2,1)}), bf16[16,2,128,128]{3,2,1,0:T(8,128)(2,1)S(1)}, u32[]{:S(2)}, u32[]{:S(2)}) async-start(bf16[16,2,128,128]{3,2,1,0:T(8,128)(2,1)} %get-tuple-element.27), calls=%async_computation | async-start | bytes 2097152 | tf_op jit(solution)/shard_map/all_to_all | solution.py:330
  13.0 1.4 %collective-permute-start.2 = (bf16[2,512,128]{2,1,0:T(8,128)(2,1)}, bf16[2,512,128]{2,1,0:T(8,128)(2,1)}, u32[]{:S(2)}, u32[]{:S(2)}) collective-permute-start(bf16[2,512,128]{2,1,0:T(8,128)(2,1)} %get-tuple-element.19), channel_id=1, source_target_pairs={{0,4},{1,5},{2,6},{3,7},{4,0},{5,1},{6,2},{7,3},{8,12},{9,13},{10,... | collective-permute-start | bytes 786440 | tf_op jit(solution)/shard_map/ppermute | solution.py:334
  14.4 1.8 %collective-permute-start.3 = (bf16[2,512,128]{2,1,0:T(8,128)(2,1)}, bf16[2,512,128]{2,1,0:T(8,128)(2,1)}, u32[]{:S(2)}, u32[]{:S(2)}) collective-permute-start(bf16[2,512,128]{2,1,0:T(8,128)(2,1)} %get-tuple-element.20), channel_id=1, source_target_pairs={{0,7},{1,6},{2,5},{3,4},{4,3},{5,2},{6,1},{7,0},{8,15},{9,14},{10,... | collective-permute-start | bytes 786440 | tf_op jit(solution)/shard_map/ppermute | solution.py:334
  16.2 4.1 %shard_map.68 = (bf16[4,512,128]{2,1,0:T(8,128)(2,1)}, bf16[4,512,128]{2,1,0:T(8,128)(2,1)}, bf16[4,512,128]{2,1,0:T(8,128)(2,1)}, bf16[4,512,128]{2,1,0:T(8,128)(2,1)}) custom-call(bf16[512,16,128]{2,1,0:T(8,128)(2,1)} %q_ref.1), custom_call_target="tpu_custom_call" | custom-call | tf_op jit(solution)/shard_map/pallas_call | solution.py:97
  20.2 3.9 %collective-permute-start = (bf16[4,512,128]{2,1,0:T(8,128)(2,1)}, bf16[4,512,128]{2,1,0:T(8,128)(2,1)S(1)}, u32[]{:S(2)}, u32[]{:S(2)}) collective-permute-start(bf16[4,512,128]{2,1,0:T(8,128)(2,1)} %get-tuple-element.15), channel_id=1, source_target_pairs={{0,7},{1,6},{2,5},{3,4},{4,3},{5,2},{6,1},{7,0},{8,15},{9,14},{10,... | collective-permute-start | bytes 1572872 | tf_op jit(solution)/shard_map/ppermute | solution.py:334
  24.1 0.0 collective-permute-start.4
  24.1 0.0 collective-permute-done.1.refs_3_
  24.1 2.0 %collective-permute-start.5 = (bf16[2,512,128]{2,1,0:T(8,128)(2,1)}, bf16[2,512,128]{2,1,0:T(8,128)(2,1)S(1)}, u32[]{:S(2)}, u32[]{:S(2)}) collective-permute-start(bf16[2,512,128]{2,1,0:T(8,128)(2,1)} %collective-permute-done.1.refs_3_), channel_id=1, source_target_pairs={{0,1},{1,0},{2,3},{3,2},{4,5},{5,4},{6,7},{7,6},{8,9},{9,8},{10,11... | collective-permute-start | bytes 786440 | tf_op jit(solution)/shard_map/ppermute | solution.py:334
  26.1 7.0 %collective-permute-done.2.refs_4_ = bf16[2,512,128]{2,1,0:T(8,128)(2,1)} collective-permute-done((bf16[2,512,128]{2,1,0:T(8,128)(2,1)}, bf16[2,512,128]{2,1,0:T(8,128)(2,1)}, u32[]{:S(2)}, u32[]{:S(2)}) %collective-permute-start.2) | collective-permute-done | bytes 262176 | tf_op jit(solution)/shard_map/ppermute | solution.py:334
  33.2 0.1 collective-permute-start.6
  33.3 5.1 %collective-permute-done.3.refs_5_ = bf16[2,512,128]{2,1,0:T(8,128)(2,1)} collective-permute-done((bf16[2,512,128]{2,1,0:T(8,128)(2,1)}, bf16[2,512,128]{2,1,0:T(8,128)(2,1)}, u32[]{:S(2)}, u32[]{:S(2)}) %collective-permute-start.3) | collective-permute-done | bytes 262176 | tf_op jit(solution)/shard_map/ppermute | solution.py:334
  38.5 0.4 collective-permute-start.7
  38.8 0.0 collective-permute-done.4.refs_6_
  38.8 2.7 %collective-permute-start.8 = (bf16[4,512,128]{2,1,0:T(8,128)(2,1)}, bf16[4,512,128]{2,1,0:T(8,128)(2,1)}, u32[]{:S(2)}, u32[]{:S(2)}) collective-permute-start(bf16[4,512,128]{2,1,0:T(8,128)(2,1)} %get-tuple-element.22), channel_id=1, source_target_pairs={{0,3},{1,2},{2,1},{3,0},{4,7},{5,6},{6,5},{7,4},{8,11},{9,10},{10,... | collective-permute-start | bytes 1572872 | tf_op jit(solution)/shard_map/ppermute | solution.py:334
  41.6 2.1 %collective-permute-start.9 = (bf16[4,512,128]{2,1,0:T(8,128)(2,1)}, bf16[4,512,128]{2,1,0:T(8,128)(2,1)}, u32[]{:S(2)}, u32[]{:S(2)}) collective-permute-start(bf16[4,512,128]{2,1,0:T(8,128)(2,1)} %get-tuple-element.23), channel_id=1, source_target_pairs={{0,4},{1,5},{2,6},{3,7},{4,0},{5,1},{6,2},{7,3},{8,12},{9,13},{10,... | collective-permute-start | bytes 1572872 | tf_op jit(solution)/shard_map/ppermute | solution.py:334
  43.7 0.8 collective-permute-done.6.refs_8_
  44.5 3.9 %collective-permute-done.7.refs_9_ = bf16[2,512,128]{2,1,0:T(8,128)(2,1)S(1)} collective-permute-done((bf16[2,512,128]{2,1,0:T(8,128)(2,1)}, bf16[2,512,128]{2,1,0:T(8,128)(2,1)S(1)}, u32[]{:S(2)}, u32[]{:S(2)}) %collective-permute-start.7) | collective-permute-done | bytes 262176 | tf_op jit(solution)/shard_map/ppermute | solution.py:334
  48.4 1.2 %collective-permute-done.refs_0_ = bf16[4,512,128]{2,1,0:T(8,128)(2,1)S(1)} collective-permute-done((bf16[4,512,128]{2,1,0:T(8,128)(2,1)}, bf16[4,512,128]{2,1,0:T(8,128)(2,1)S(1)}, u32[]{:S(2)}, u32[]{:S(2)}) %collective-permute-start) | collective-permute-done | bytes 524320 | tf_op jit(solution)/shard_map/ppermute | solution.py:334
  49.7 0.8 copy-done.2
  50.5 15.4 %shard_map.70 = (bf16[4,512,128]{2,1,0:T(8,128)(2,1)}, bf16[4,512,128]{2,1,0:T(8,128)(2,1)}) custom-call(s32[1,2]{1,0:T(1,128)} %spans_ref.5, bf16[4,512,128]{2,1,0:T(8,128)(2,1)} %copy-done.2, bf16[4,512,128]{2,1,0:T(8,128)(2,1)} %get-tuple-element.16.refs_1_, bf16[2,512,128]{2,1,0:T(8,128)(2,1)} %get-tuple-element.17.refs_2_, ...), custom_call_target="tpu_custom_call" | custom-call | flops 4294967296 | bytes 4194304 | tf_op jit(solution)/shard_map/pallas_call | solution.py:260
  65.8 4.7 %collective-permute-start.12 = (bf16[4,512,128]{2,1,0:T(8,128)(2,1)}, bf16[4,512,128]{2,1,0:T(8,128)(2,1)}, u32[]{:S(2)}, u32[]{:S(2)}) collective-permute-start(bf16[4,512,128]{2,1,0:T(8,128)(2,1)} %get-tuple-element.26), channel_id=1, source_target_pairs={{0,7},{1,6},{2,5},{3,4},{4,3},{5,2},{6,1},{7,0},{8,15},{9,14},{10,... | collective-permute-start | bytes 1572872 | tf_op jit(solution)/shard_map/ppermute | solution.py:334
  70.5 1.6 %shard_map.73 = bf16[16,2,128,128]{3,2,1,0:T(8,128)(2,1)} custom-call(s32[16]{0:T(128)S(1)} %copy-done.1, bf16[16,2,128,128]{3,2,1,0:T(8,128)(2,1)S(1)} %all-to-all-done.in_ref), custom_call_target="tpu_custom_call" | custom-call | tf_op jit(solution)/shard_map/pallas_call | solution.py:301
  72.1 4.8 %all-to-all-start.1 = ((bf16[16,2,128,128]{3,2,1,0:T(8,128)(2,1)}), bf16[16,2,128,128]{3,2,1,0:T(8,128)(2,1)S(1)}, u32[]{:S(2)}, u32[]{:S(2)}) async-start(bf16[16,2,128,128]{3,2,1,0:T(8,128)(2,1)} %shard_map.73), calls=%async_computation.1 | async-start | bytes 2097152 | tf_op jit(solution)/shard_map/all_to_all | solution.py:330
  76.9 0.0 collective-permute-done.9.refs_1_
  76.9 6.0 %shard_map.71 = (bf16[4,512,128]{2,1,0:T(8,128)(2,1)}, bf16[4,512,128]{2,1,0:T(8,128)(2,1)}) custom-call(s32[1,2]{1,0:T(1,128)} %spans_ref.5, bf16[4,512,128]{2,1,0:T(8,128)(2,1)} %collective-permute-done.8.refs_0_, bf16[4,512,128]{2,1,0:T(8,128)(2,1)} %collective-permute-done.9.refs_1_, bf16[2,512,128]{2,1,0:T(8,128)(2,1)} %get-tuple-element.17.refs_2_, ...), custom_call_target="tpu_custom_call" | custom-call | flops 4294967296 | bytes 4194304 | tf_op jit(solution)/shard_map/pallas_call | solution.py:260
  83.0 12.1 %collective-permute-start.10 = (bf16[4,512,128]{2,1,0:T(8,128)(2,1)}, bf16[4,512,128]{2,1,0:T(8,128)(2,1)S(1)}, u32[]{:S(2)}, u32[]{:S(2)}) collective-permute-start(bf16[4,512,128]{2,1,0:T(8,128)(2,1)} %get-tuple-element.24), channel_id=1, source_target_pairs={{0,3},{1,2},{2,1},{3,0},{4,7},{5,6},{6,5},{7,4},{8,11},{9,10},{10,... | collective-permute-start | bytes 1572872 | tf_op jit(solution)/shard_map/ppermute | solution.py:334
  95.0 10.4 %collective-permute-done.10.refs_1_ = bf16[4,512,128]{2,1,0:T(8,128)(2,1)S(1)} collective-permute-done((bf16[4,512,128]{2,1,0:T(8,128)(2,1)}, bf16[4,512,128]{2,1,0:T(8,128)(2,1)S(1)}, u32[]{:S(2)}, u32[]{:S(2)}) %collective-permute-start.10) | collective-permute-done | bytes 524320 | tf_op jit(solution)/shard_map/ppermute | solution.py:334
  105.4 3.0 %collective-permute-done.11.refs_2_ = bf16[4,512,128]{2,1,0:T(8,128)(2,1)S(1)} collective-permute-done((bf16[4,512,128]{2,1,0:T(8,128)(2,1)}, bf16[4,512,128]{2,1,0:T(8,128)(2,1)S(1)}, u32[]{:S(2)}, u32[]{:S(2)}) %collective-permute-start.11) | collective-permute-done | bytes 524320 | tf_op jit(solution)/shard_map/ppermute | solution.py:334
  108.4 4.0 %shard_map.72 = bf16[512,16,128]{2,1,0:T(8,128)(2,1)} custom-call(bf16[4,512,128]{2,1,0:T(8,128)(2,1)S(1)} %copy-done, bf16[4,512,128]{2,1,0:T(8,128)(2,1)S(1)} %collective-permute-done.10.refs_1_, bf16[4,512,128]{2,1,0:T(8,128)(2,1)S(1)} %collective-permute-done.11.refs_2_, bf16[4,512,128]{2,1,0:T(8,128)(2,1)} %collective-permute-done.12.refs_3_), custom_call_target="tpu_custom_call" | custom-call | tf_op jit(solution)/shard_map/pallas_call | solution.py:119
  112.4 1.0 shard_map.74
  (21 shorter events, 0.0 us)
Async XLA Ops:
  3.4 20.7 %collective-permute-start.1 = (bf16[2,512,128]{2,1,0:T(8,128)(2,1)}, bf16[2,512,128]{2,1,0:T(8,128)(2,1)}, u32[]{:S(2)}, u32[]{:S(2)}) collective-permute-start(bf16[2,512,128]{2,1,0:T(8,128)(2,1)} %get-tuple-element.18), channel_id=1, source_target_pairs={{0,3},{1,2},{2,1},{3,0},{4,7},{5,6},{6,5},{7,4},{8,11},{9,10},{10,... | collective-permute-start | bytes 786440 | tf_op jit(solution)/shard_map/ppermute | solution.py:334
  6.5 17.6 %copy-start.3 = (bf16[2,512,128]{2,1,0:T(8,128)(2,1)S(1)}, bf16[2,512,128]{2,1,0:T(8,128)(2,1)}, u32[]{:S(2)}) copy-start(bf16[2,512,128]{2,1,0:T(8,128)(2,1)} %get-tuple-element.17.refs_2_) | copy-start | bytes 786436
  6.5 64.0 %all-to-all-start = ((bf16[16,2,128,128]{3,2,1,0:T(8,128)(2,1)}), bf16[16,2,128,128]{3,2,1,0:T(8,128)(2,1)S(1)}, u32[]{:S(2)}, u32[]{:S(2)}) async-start(bf16[16,2,128,128]{3,2,1,0:T(8,128)(2,1)} %get-tuple-element.27), calls=%async_computation | async-start | bytes 2097152 | tf_op jit(solution)/shard_map/all_to_all | solution.py:330
  13.0 20.2 %collective-permute-start.2 = (bf16[2,512,128]{2,1,0:T(8,128)(2,1)}, bf16[2,512,128]{2,1,0:T(8,128)(2,1)}, u32[]{:S(2)}, u32[]{:S(2)}) collective-permute-start(bf16[2,512,128]{2,1,0:T(8,128)(2,1)} %get-tuple-element.19), channel_id=1, source_target_pairs={{0,4},{1,5},{2,6},{3,7},{4,0},{5,1},{6,2},{7,3},{8,12},{9,13},{10,... | collective-permute-start | bytes 786440 | tf_op jit(solution)/shard_map/ppermute | solution.py:334
  14.4 24.1 %collective-permute-start.3 = (bf16[2,512,128]{2,1,0:T(8,128)(2,1)}, bf16[2,512,128]{2,1,0:T(8,128)(2,1)}, u32[]{:S(2)}, u32[]{:S(2)}) collective-permute-start(bf16[2,512,128]{2,1,0:T(8,128)(2,1)} %get-tuple-element.20), channel_id=1, source_target_pairs={{0,7},{1,6},{2,5},{3,4},{4,3},{5,2},{6,1},{7,0},{8,15},{9,14},{10,... | collective-permute-start | bytes 786440 | tf_op jit(solution)/shard_map/ppermute | solution.py:334
  20.2 29.4 %collective-permute-start = (bf16[4,512,128]{2,1,0:T(8,128)(2,1)}, bf16[4,512,128]{2,1,0:T(8,128)(2,1)S(1)}, u32[]{:S(2)}, u32[]{:S(2)}) collective-permute-start(bf16[4,512,128]{2,1,0:T(8,128)(2,1)} %get-tuple-element.15), channel_id=1, source_target_pairs={{0,7},{1,6},{2,5},{3,4},{4,3},{5,2},{6,1},{7,0},{8,15},{9,14},{10,... | collective-permute-start | bytes 1572872 | tf_op jit(solution)/shard_map/ppermute | solution.py:334
  24.1 14.7 %collective-permute-start.4 = (bf16[2,512,128]{2,1,0:T(8,128)(2,1)S(1)}, bf16[2,512,128]{2,1,0:T(8,128)(2,1)S(1)}, u32[]{:S(2)}, u32[]{:S(2)}) collective-permute-start(bf16[2,512,128]{2,1,0:T(8,128)(2,1)S(1)} %copy-done.3), channel_id=1, source_target_pairs={{0,1},{1,0},{2,3},{3,2},{4,5},{5,4},{6,7},{7,6},{8,9},{9,8},{10,11... | collective-permute-start | bytes 786440 | tf_op jit(solution)/shard_map/ppermute | solution.py:334
  24.1 17.5 %collective-permute-start.5 = (bf16[2,512,128]{2,1,0:T(8,128)(2,1)}, bf16[2,512,128]{2,1,0:T(8,128)(2,1)S(1)}, u32[]{:S(2)}, u32[]{:S(2)}) collective-permute-start(bf16[2,512,128]{2,1,0:T(8,128)(2,1)} %collective-permute-done.1.refs_3_), channel_id=1, source_target_pairs={{0,1},{1,0},{2,3},{3,2},{4,5},{5,4},{6,7},{7,6},{8,9},{9,8},{10,11... | collective-permute-start | bytes 786440 | tf_op jit(solution)/shard_map/ppermute | solution.py:334
  33.2 11.3 %collective-permute-start.6 = (bf16[2,512,128]{2,1,0:T(8,128)(2,1)}, bf16[2,512,128]{2,1,0:T(8,128)(2,1)S(1)}, u32[]{:S(2)}, u32[]{:S(2)}) collective-permute-start(bf16[2,512,128]{2,1,0:T(8,128)(2,1)} %collective-permute-done.2.refs_4_), channel_id=1, source_target_pairs={{0,1},{1,0},{2,3},{3,2},{4,5},{5,4},{6,7},{7,6},{8,9},{9,8},{10,11... | collective-permute-start | bytes 786440 | tf_op jit(solution)/shard_map/ppermute | solution.py:334
  38.5 10.0 %collective-permute-start.7 = (bf16[2,512,128]{2,1,0:T(8,128)(2,1)}, bf16[2,512,128]{2,1,0:T(8,128)(2,1)S(1)}, u32[]{:S(2)}, u32[]{:S(2)}) collective-permute-start(bf16[2,512,128]{2,1,0:T(8,128)(2,1)} %collective-permute-done.3.refs_5_), channel_id=1, source_target_pairs={{0,1},{1,0},{2,3},{3,2},{4,5},{5,4},{6,7},{7,6},{8,9},{9,8},{10,11... | collective-permute-start | bytes 786440 | tf_op jit(solution)/shard_map/ppermute | solution.py:334
  38.8 10.8 %copy-start.4 = (bf16[2,512,128]{2,1,0:T(8,128)(2,1)}, bf16[2,512,128]{2,1,0:T(8,128)(2,1)S(1)}, u32[]{:S(2)}) copy-start(bf16[2,512,128]{2,1,0:T(8,128)(2,1)S(1)} %collective-permute-done.4.refs_6_) | copy-start | bytes 786436
  38.8 38.1 %collective-permute-start.8 = (bf16[4,512,128]{2,1,0:T(8,128)(2,1)}, bf16[4,512,128]{2,1,0:T(8,128)(2,1)}, u32[]{:S(2)}, u32[]{:S(2)}) collective-permute-start(bf16[4,512,128]{2,1,0:T(8,128)(2,1)} %get-tuple-element.22), channel_id=1, source_target_pairs={{0,3},{1,2},{2,1},{3,0},{4,7},{5,6},{6,5},{7,4},{8,11},{9,10},{10,... | collective-permute-start | bytes 1572872 | tf_op jit(solution)/shard_map/ppermute | solution.py:334
  41.6 8.1 %copy-start.5 = (bf16[2,512,128]{2,1,0:T(8,128)(2,1)}, bf16[2,512,128]{2,1,0:T(8,128)(2,1)S(1)}, u32[]{:S(2)}) copy-start(bf16[2,512,128]{2,1,0:T(8,128)(2,1)S(1)} %collective-permute-done.5.refs_7_) | copy-start | bytes 786436
  41.6 35.3 %collective-permute-start.9 = (bf16[4,512,128]{2,1,0:T(8,128)(2,1)}, bf16[4,512,128]{2,1,0:T(8,128)(2,1)}, u32[]{:S(2)}, u32[]{:S(2)}) collective-permute-start(bf16[4,512,128]{2,1,0:T(8,128)(2,1)} %get-tuple-element.23), channel_id=1, source_target_pairs={{0,4},{1,5},{2,6},{3,7},{4,0},{5,1},{6,2},{7,3},{8,12},{9,13},{10,... | collective-permute-start | bytes 1572872 | tf_op jit(solution)/shard_map/ppermute | solution.py:334
  44.5 5.1 %copy-start.6 = (bf16[2,512,128]{2,1,0:T(8,128)(2,1)}, bf16[2,512,128]{2,1,0:T(8,128)(2,1)S(1)}, u32[]{:S(2)}) copy-start(bf16[2,512,128]{2,1,0:T(8,128)(2,1)S(1)} %collective-permute-done.6.refs_8_) | copy-start | bytes 786436
  48.4 1.2 %copy-start.7 = (bf16[2,512,128]{2,1,0:T(8,128)(2,1)}, bf16[2,512,128]{2,1,0:T(8,128)(2,1)S(1)}, u32[]{:S(2)}) copy-start(bf16[2,512,128]{2,1,0:T(8,128)(2,1)S(1)} %collective-permute-done.7.refs_9_) | copy-start | bytes 786436
  49.7 0.8 copy-start.2
  50.5 20.0 %copy-start.1 = (s32[16]{0:T(128)S(1)}, s32[16]{0:T(128)}, u32[]{:S(2)}) copy-start(s32[16]{0:T(128)} %order_ref.1) | copy-start | bytes 196
  65.8 29.2 %collective-permute-start.12 = (bf16[4,512,128]{2,1,0:T(8,128)(2,1)}, bf16[4,512,128]{2,1,0:T(8,128)(2,1)}, u32[]{:S(2)}, u32[]{:S(2)}) collective-permute-start(bf16[4,512,128]{2,1,0:T(8,128)(2,1)} %get-tuple-element.26), channel_id=1, source_target_pairs={{0,7},{1,6},{2,5},{3,4},{4,3},{5,2},{6,1},{7,0},{8,15},{9,14},{10,... | collective-permute-start | bytes 1572872 | tf_op jit(solution)/shard_map/ppermute | solution.py:334
  72.1 40.3 %all-to-all-start.1 = ((bf16[16,2,128,128]{3,2,1,0:T(8,128)(2,1)}), bf16[16,2,128,128]{3,2,1,0:T(8,128)(2,1)S(1)}, u32[]{:S(2)}, u32[]{:S(2)}) async-start(bf16[16,2,128,128]{3,2,1,0:T(8,128)(2,1)} %shard_map.73), calls=%async_computation.1 | async-start | bytes 2097152 | tf_op jit(solution)/shard_map/all_to_all | solution.py:330
  76.9 31.5 %copy-start = (bf16[4,512,128]{2,1,0:T(8,128)(2,1)S(1)}, bf16[4,512,128]{2,1,0:T(8,128)(2,1)}, u32[]{:S(2)}) copy-start(bf16[4,512,128]{2,1,0:T(8,128)(2,1)} %get-tuple-element.21.refs_0_) | copy-start | bytes 1572868
  83.0 22.5 %collective-permute-start.10 = (bf16[4,512,128]{2,1,0:T(8,128)(2,1)}, bf16[4,512,128]{2,1,0:T(8,128)(2,1)S(1)}, u32[]{:S(2)}, u32[]{:S(2)}) collective-permute-start(bf16[4,512,128]{2,1,0:T(8,128)(2,1)} %get-tuple-element.24), channel_id=1, source_target_pairs={{0,3},{1,2},{2,1},{3,0},{4,7},{5,6},{6,5},{7,4},{8,11},{9,10},{10,... | collective-permute-start | bytes 1572872 | tf_op jit(solution)/shard_map/ppermute | solution.py:334
  95.0 13.4 %collective-permute-start.11 = (bf16[4,512,128]{2,1,0:T(8,128)(2,1)}, bf16[4,512,128]{2,1,0:T(8,128)(2,1)S(1)}, u32[]{:S(2)}, u32[]{:S(2)}) collective-permute-start(bf16[4,512,128]{2,1,0:T(8,128)(2,1)} %get-tuple-element.25), channel_id=1, source_target_pairs={{0,4},{1,5},{2,6},{3,7},{4,0},{5,1},{6,2},{7,3},{8,12},{9,13},{10,... | collective-permute-start | bytes 1572872 | tf_op jit(solution)/shard_map/ppermute | solution.py:334

commit v5 on v4

--- a/solution.py
+++ b/solution.py
@@ -84,7 +84,6 @@
 def pack_queries(queries):
     rows, head_count, width = queries.shape
     heads = head_count // 4
-    chunk = rows // 4
 
     def kernel(q_ref, *refs):
         outs, turned = refs[:4], refs[4]
@@ -96,18 +95,16 @@
     piece = jax.ShapeDtypeStruct((heads, rows, width), jnp.bfloat16)
     return pl.pallas_call(
         kernel,
-        grid=(4,),
-        in_specs=[pl.BlockSpec((chunk, head_count, width), lambda i: (i, 0, 0))],
-        out_specs=[pl.BlockSpec((heads, chunk, width), lambda i: (0, i, 0))] * 4,
+        in_specs=[whole(queries)],
+        out_specs=[whole(piece)] * 4,
         out_shape=[piece] * 4,
-        scratch_shapes=[pltpu.VMEM((head_count, chunk, width), jnp.bfloat16)],
-        compiler_params=small(62),
+        scratch_shapes=[pltpu.VMEM((head_count, rows, width), jnp.bfloat16)],
+        compiler_params=small(16),
     )(queries)
 
 
 def join_heads(pieces):
     heads, rows, width = pieces[0].shape
-    chunk = rows // 4
 
     def kernel(*refs):
         ins, out, gathered = refs[:4], refs[4], refs[5]
@@ -116,18 +113,18 @@
             gathered[pl.ds((group ^ k) * heads, heads)] = ins[k][...]
         out[...] = jnp.swapaxes(gathered[...], 0, 1)
 
-    return pl.pallas_call(
-        kernel,
-        grid=(4,),
-        in_specs=[pl.BlockSpec((heads, chunk, width), lambda i: (0, i, 0))] * 4,
-        out_specs=pl.BlockSpec((chunk, 4 * heads, width), lambda i: (i, 0, 0)),
-        out_shape=jax.ShapeDtypeStruct((rows, 4 * heads, width), jnp.bfloat16),
-        scratch_shapes=[pltpu.VMEM((4 * heads, chunk, width), jnp.bfloat16)],
+    out_shape = jax.ShapeDtypeStruct((rows, 4 * heads, width), jnp.bfloat16)
+    return pl.pallas_call(
+        kernel,
+        in_specs=[whole(piece) for piece in pieces],
+        out_specs=whole(out_shape),
+        out_shape=out_shape,
+        scratch_shapes=[pltpu.VMEM((4 * heads, rows, width), jnp.bfloat16)],
         compiler_params=small(16),
     )(*pieces)
 
 
-def attend(which, queries, own, other, spans, stripes):
+def attend(which, queries, own, other, spans, stripes, grant):
     asked = len(which)
     members = len(own)
     heads, rows, width = queries[0].shape
@@ -283,7 +280,7 @@
         ),
         out_shape=[jax.ShapeDtypeStruct(queries[0].shape, jnp.bfloat16)] * asked,
         compiler_params=pltpu.CompilerParams(
-            dimension_semantics=("arbitrary",), vmem_limit_bytes=62 * 1024 * 1024
+            dimension_semantics=("arbitrary",), vmem_limit_bytes=grant * 1024 * 1024
         ),
         cost_estimate=pl.CostEstimate(
             flops=4 * asked * members * heads * rows * rows * width,
@@ -355,9 +352,9 @@
     cache = place_rows(cache, slots // blocks)
 
     done = [None] * 4
-    for which in ((1, 2), (3, 0)):
+    for which, grant in (((1, 2), 62), ((3, 0), 62)):
         asked = [q_own[k] for k in which]
-        for k, result in zip(which, attend(which, asked, own, other, spans, stripes)):
+        for k, result in zip(which, attend(which, asked, own, other, spans, stripes, grant)):
             done[k] = result
     back = [done[0]] + [send(done[k], flips[k]) for k in (1, 2, 3)]
     return join_heads(back), cache

time: 115 us -> 114 us (level)
  Pallas kernels: 34.8 us -> 32 us
  local copies, waits for them, and re-layouts: 0.83 us -> 3.21 us
    pallas_call x2, Pallas kernels: 8.03 us -> 5.18 us  [the longest x1 3.38 us: join_heads(): pl.pallas_call(kernel, in_specs=[whole(piece) for piece in pieces], out_s...]
    unnamed x16 -> x26, local copies, waits for them, and re-layouts: 0.83 us -> 3.21 us
  transfers between devices with their start and end apart: 15 -> 15, of which waited for: 7 -> 7; matrix products, arithmetic and copies ran while one was open for 0% -> 0% of each run, Pallas kernels for 27% -> 25%
where the time goes in v5:
time: 114 us; the launch traced here: 113 us
  starting transfers between devices  45.5 us (40%)
  Pallas kernels  32 us (28%)
  waiting for transfers between devices  31.4 us (28%)
  local copies, waits for them, and re-layouts  3.21 us (3%)
    ppermute x13, starting transfers between devices, send(): return lax.ppermute(array, 'ctx', route(flip))  34.3 us
    ppermute x13, waiting for transfers between devices, send(): return lax.ppermute(array, 'ctx', route(flip))  31.4 us
    pallas_call x2, Pallas kernels, attend(): pl.pallas_call(kernel, grid_spec=pltpu.PrefetchScalarGridSpec(num_scalar_...  21.4 us
    all_to_all x2, starting transfers between devices, swap(): return lax.all_to_all(array, axis, split_axis=0, concat_axis=0, tiled=True)  11.3 us
    pallas_call x1, Pallas kernels, join_heads(): pl.pallas_call(kernel, in_specs=[whole(piece) for piece in pieces], out_s...  3.38 us
    unnamed x26, local copies, waits for them, and re-layouts  3.21 us
    pallas_call x1, Pallas kernels, pack_kv(): pl.pallas_call(kernel, in_specs=[pl.BlockSpec(memory_space=pltpu.HBM)] *...  2.79 us
  transfers between devices with their start and end apart: 15, of which 7 were waited for; matrix products, arithmetic and copies ran while one was open for 0% of the time, Pallas kernels for 25%

profile of v5, /device:TPU:38, one launch (start us, length us, event | category | flops | bytes accessed | tf_op | source)
XLA Modules:
  0.0 112.9 jit_solution(2722187355685188046)
XLA Ops:
  0.6 2.8 %shard_map.69 = (bf16[2,512,128]{2,1,0:T(8,128)(2,1)}, bf16[2,512,128]{2,1,0:T(8,128)(2,1)}, bf16[2,512,128]{2,1,0:T(8,128)(2,1)}, bf16[2,512,128]{2,1,0:T(8,128)(2,1)}, bf16[16,2,128,128]{3,2,1,0:T(8,128)(2,1)}) custom-call(s32[1,2]{1,0:T(1,128)} %spans_ref.5, bf16[128,16,128]{2,1,0:T(8,128)(2,1)} %bitcast.2, bf16[128,16,128]{2,1,0:T(8,128)(2,1)} %bitcast.3), custom_call_target="tpu_custom_call" | custom-call | tf_op jit(solution)/shard_map/pallas_call | solution.py:68
  3.4 3.1 %collective-permute-start.1 = (bf16[2,512,128]{2,1,0:T(8,128)(2,1)}, bf16[2,512,128]{2,1,0:T(8,128)(2,1)S(1)}, u32[]{:S(2)}, u32[]{:S(2)}) collective-permute-start(bf16[2,512,128]{2,1,0:T(8,128)(2,1)} %get-tuple-element.18), channel_id=1, source_target_pairs={{0,3},{1,2},{2,1},{3,0},{4,7},{5,6},{6,5},{7,4},{8,11},{9,10},{10,... | collective-permute-start | bytes 786440 | tf_op jit(solution)/shard_map/ppermute | solution.py:331
  6.5 6.5 %all-to-all-start = ((bf16[16,2,128,128]{3,2,1,0:T(8,128)(2,1)}), bf16[16,2,128,128]{3,2,1,0:T(8,128)(2,1)S(1)}, u32[]{:S(2)}, u32[]{:S(2)}) async-start(bf16[16,2,128,128]{3,2,1,0:T(8,128)(2,1)} %get-tuple-element.27), calls=%async_computation | async-start | bytes 2097152 | tf_op jit(solution)/shard_map/all_to_all | solution.py:327
  13.0 1.4 %collective-permute-start.2 = (bf16[2,512,128]{2,1,0:T(8,128)(2,1)}, bf16[2,512,128]{2,1,0:T(8,128)(2,1)S(1)}, u32[]{:S(2)}, u32[]{:S(2)}) collective-permute-start(bf16[2,512,128]{2,1,0:T(8,128)(2,1)} %get-tuple-element.19), channel_id=1, source_target_pairs={{0,4},{1,5},{2,6},{3,7},{4,0},{5,1},{6,2},{7,3},{8,12},{9,13},{10,... | collective-permute-start | bytes 786440 | tf_op jit(solution)/shard_map/ppermute | solution.py:331
  14.4 1.8 %collective-permute-start.3 = (bf16[2,512,128]{2,1,0:T(8,128)(2,1)}, bf16[2,512,128]{2,1,0:T(8,128)(2,1)S(1)}, u32[]{:S(2)}, u32[]{:S(2)}) collective-permute-start(bf16[2,512,128]{2,1,0:T(8,128)(2,1)} %get-tuple-element.20), channel_id=1, source_target_pairs={{0,7},{1,6},{2,5},{3,4},{4,3},{5,2},{6,1},{7,0},{8,15},{9,14},{10,... | collective-permute-start | bytes 786440 | tf_op jit(solution)/shard_map/ppermute | solution.py:331
  16.2 1.6 %copy-done = bf16[512,16,128]{2,1,0:T(8,128)(2,1)S(1)} copy-done((bf16[512,16,128]{2,1,0:T(8,128)(2,1)S(1)}, bf16[512,16,128]{2,1,0:T(8,128)(2,1)}, u32[]{:S(2)}) %copy-start) | copy-done | bytes 2097176
  17.8 1.8 %shard_map.68 = (bf16[4,512,128]{2,1,0:T(8,128)(2,1)S(1)}, bf16[4,512,128]{2,1,0:T(8,128)(2,1)}, bf16[4,512,128]{2,1,0:T(8,128)(2,1)}, bf16[4,512,128]{2,1,0:T(8,128)(2,1)S(1)}) custom-call(bf16[512,16,128]{2,1,0:T(8,128)(2,1)S(1)} %copy-done), custom_call_target="tpu_custom_call" | custom-call | tf_op jit(solution)/shard_map/pallas_call | solution.py:96
  19.6 0.8 copy-done.3
  20.4 3.9 %collective-permute-start = (bf16[4,512,128]{2,1,0:T(8,128)(2,1)S(1)}, bf16[4,512,128]{2,1,0:T(8,128)(2,1)S(1)}, u32[]{:S(2)}, u32[]{:S(2)}) collective-permute-start(bf16[4,512,128]{2,1,0:T(8,128)(2,1)S(1)} %get-tuple-element.15), channel_id=1, source_target_pairs={{0,7},{1,6},{2,5},{3,4},{4,3},{5,2},{6,1},{7,0},{8,15},{9,14},{10,... | collective-permute-start | bytes 1572872 | tf_op jit(solution)/shard_map/ppermute | solution.py:331
  24.2 0.0 collective-permute-start.4
  24.2 0.0 collective-permute-done.1.refs_3_
  24.2 2.0 %collective-permute-start.5 = (bf16[2,512,128]{2,1,0:T(8,128)(2,1)S(1)}, bf16[2,512,128]{2,1,0:T(8,128)(2,1)S(1)}, u32[]{:S(2)}, u32[]{:S(2)}) collective-permute-start(bf16[2,512,128]{2,1,0:T(8,128)(2,1)S(1)} %collective-permute-done.1.refs_3_), channel_id=1, source_target_pairs={{0,1},{1,0},{2,3},{3,2},{4,5},{5,4},{6,7},{7,6},{8,9},{9,8},{10,11... | collective-permute-start | bytes 786440 | tf_op jit(solution)/shard_map/ppermute | solution.py:331
  26.2 6.8 %collective-permute-done.2.refs_4_ = bf16[2,512,128]{2,1,0:T(8,128)(2,1)S(1)} collective-permute-done((bf16[2,512,128]{2,1,0:T(8,128)(2,1)}, bf16[2,512,128]{2,1,0:T(8,128)(2,1)S(1)}, u32[]{:S(2)}, u32[]{:S(2)}) %collective-permute-start.2) | collective-permute-done | bytes 262176 | tf_op jit(solution)/shard_map/ppermute | solution.py:331
  33.1 0.1 collective-permute-start.6
  33.2 5.1 %collective-permute-done.3.refs_5_ = bf16[2,512,128]{2,1,0:T(8,128)(2,1)S(1)} collective-permute-done((bf16[2,512,128]{2,1,0:T(8,128)(2,1)}, bf16[2,512,128]{2,1,0:T(8,128)(2,1)S(1)}, u32[]{:S(2)}, u32[]{:S(2)}) %collective-permute-start.3) | collective-permute-done | bytes 262176 | tf_op jit(solution)/shard_map/ppermute | solution.py:331
  38.4 0.4 collective-permute-start.7
  38.7 2.7 %collective-permute-start.8 = (bf16[4,512,128]{2,1,0:T(8,128)(2,1)}, bf16[4,512,128]{2,1,0:T(8,128)(2,1)}, u32[]{:S(2)}, u32[]{:S(2)}) collective-permute-start(bf16[4,512,128]{2,1,0:T(8,128)(2,1)} %get-tuple-element.22), channel_id=1, source_target_pairs={{0,3},{1,2},{2,1},{3,0},{4,7},{5,6},{6,5},{7,4},{8,11},{9,10},{10,... | collective-permute-start | bytes 1572872 | tf_op jit(solution)/shard_map/ppermute | solution.py:331
  41.5 2.1 %collective-permute-start.9 = (bf16[4,512,128]{2,1,0:T(8,128)(2,1)}, bf16[4,512,128]{2,1,0:T(8,128)(2,1)}, u32[]{:S(2)}, u32[]{:S(2)}) collective-permute-start(bf16[4,512,128]{2,1,0:T(8,128)(2,1)} %get-tuple-element.23), channel_id=1, source_target_pairs={{0,4},{1,5},{2,6},{3,7},{4,0},{5,1},{6,2},{7,3},{8,12},{9,13},{10,... | collective-permute-start | bytes 1572872 | tf_op jit(solution)/shard_map/ppermute | solution.py:331
  43.6 1.0 collective-permute-done.6.refs_8_
  44.6 3.9 %collective-permute-done.7.refs_9_ = bf16[2,512,128]{2,1,0:T(8,128)(2,1)S(1)} collective-permute-done((bf16[2,512,128]{2,1,0:T(8,128)(2,1)S(1)}, bf16[2,512,128]{2,1,0:T(8,128)(2,1)S(1)}, u32[]{:S(2)}, u32[]{:S(2)}) %collective-permute-start.7) | collective-permute-done | bytes 262176 | tf_op jit(solution)/shard_map/ppermute | solution.py:331
  48.6 1.1 collective-permute-done.refs_0_
  49.7 0.8 copy-done.4
  50.5 15.4 %shard_map.70 = (bf16[4,512,128]{2,1,0:T(8,128)(2,1)}, bf16[4,512,128]{2,1,0:T(8,128)(2,1)}) custom-call(s32[1,2]{1,0:T(1,128)} %spans_ref.5, bf16[4,512,128]{2,1,0:T(8,128)(2,1)} %copy-done.4, bf16[4,512,128]{2,1,0:T(8,128)(2,1)} %copy-done.3, bf16[2,512,128]{2,1,0:T(8,128)(2,1)} %get-tuple-element.17.refs_2_, bf16[2,512,128]{2,1,0:T(8,128)(2,1)} %copy-done.6, ...), custom_call_target="tpu_custom_call" | custom-call | flops 4294967296 | bytes 4194304 | tf_op jit(solution)/shard_map/pallas_call | solution.py:257
  65.9 4.6 %collective-permute-start.12 = (bf16[4,512,128]{2,1,0:T(8,128)(2,1)}, bf16[4,512,128]{2,1,0:T(8,128)(2,1)}, u32[]{:S(2)}, u32[]{:S(2)}) collective-permute-start(bf16[4,512,128]{2,1,0:T(8,128)(2,1)} %get-tuple-element.26), channel_id=1, source_target_pairs={{0,7},{1,6},{2,5},{3,4},{4,3},{5,2},{6,1},{7,0},{8,15},{9,14},{10,... | collective-permute-start | bytes 1572872 | tf_op jit(solution)/shard_map/ppermute | solution.py:331
  70.5 1.6 %shard_map.73 = bf16[16,2,128,128]{3,2,1,0:T(8,128)(2,1)} custom-call(s32[16]{0:T(128)S(1)} %copy-done.2, bf16[16,2,128,128]{3,2,1,0:T(8,128)(2,1)S(1)} %all-to-all-done.in_ref), custom_call_target="tpu_custom_call" | custom-call | tf_op jit(solution)/shard_map/pallas_call | solution.py:298
  72.1 4.8 %all-to-all-start.1 = ((bf16[16,2,128,128]{3,2,1,0:T(8,128)(2,1)}), bf16[16,2,128,128]{3,2,1,0:T(8,128)(2,1)S(1)}, u32[]{:S(2)}, u32[]{:S(2)}) async-start(bf16[16,2,128,128]{3,2,1,0:T(8,128)(2,1)} %shard_map.73), calls=%async_computation.1 | async-start | bytes 2097152 | tf_op jit(solution)/shard_map/all_to_all | solution.py:327
  76.9 6.0 %shard_map.71 = (bf16[4,512,128]{2,1,0:T(8,128)(2,1)}, bf16[4,512,128]{2,1,0:T(8,128)(2,1)}) custom-call(s32[1,2]{1,0:T(1,128)} %spans_ref.5, bf16[4,512,128]{2,1,0:T(8,128)(2,1)} %collective-permute-done.8.refs_0_, bf16[4,512,128]{2,1,0:T(8,128)(2,1)} %collective-permute-done.9.refs_1_, bf16[2,512,128]{2,1,0:T(8,128)(2,1)} %get-tuple-element.17.refs_2_, ...), custom_call_target="tpu_custom_call" | custom-call | flops 4294967296 | bytes 4194304 | tf_op jit(solution)/shard_map/pallas_call | solution.py:257
  83.0 12.1 %collective-permute-start.10 = (bf16[4,512,128]{2,1,0:T(8,128)(2,1)}, bf16[4,512,128]{2,1,0:T(8,128)(2,1)S(1)}, u32[]{:S(2)}, u32[]{:S(2)}) collective-permute-start(bf16[4,512,128]{2,1,0:T(8,128)(2,1)} %get-tuple-element.24), channel_id=1, source_target_pairs={{0,3},{1,2},{2,1},{3,0},{4,7},{5,6},{6,5},{7,4},{8,11},{9,10},{10,... | collective-permute-start | bytes 1572872 | tf_op jit(solution)/shard_map/ppermute | solution.py:331
  95.1 10.4 %collective-permute-done.10.refs_1_ = bf16[4,512,128]{2,1,0:T(8,128)(2,1)S(1)} collective-permute-done((bf16[4,512,128]{2,1,0:T(8,128)(2,1)}, bf16[4,512,128]{2,1,0:T(8,128)(2,1)S(1)}, u32[]{:S(2)}, u32[]{:S(2)}) %collective-permute-start.10) | collective-permute-done | bytes 524320 | tf_op jit(solution)/shard_map/ppermute | solution.py:331
  105.5 3.0 %collective-permute-done.11.refs_2_ = bf16[4,512,128]{2,1,0:T(8,128)(2,1)S(1)} collective-permute-done((bf16[4,512,128]{2,1,0:T(8,128)(2,1)}, bf16[4,512,128]{2,1,0:T(8,128)(2,1)S(1)}, u32[]{:S(2)}, u32[]{:S(2)}) %collective-permute-start.11) | collective-permute-done | bytes 524320 | tf_op jit(solution)/shard_map/ppermute | solution.py:331
  108.4 3.4 %shard_map.72 = bf16[512,16,128]{2,1,0:T(8,128)(2,1)} custom-call(bf16[4,512,128]{2,1,0:T(8,128)(2,1)S(1)} %copy-done.1, bf16[4,512,128]{2,1,0:T(8,128)(2,1)S(1)} %collective-permute-done.10.refs_1_, bf16[4,512,128]{2,1,0:T(8,128)(2,1)S(1)} %collective-permute-done.11.refs_2_, bf16[4,512,128]{2,1,0:T(8,128)(2,1)} %collective-permute-done.12.refs_3_), custom_call_target="tpu_custom_call" | custom-call | tf_op jit(solution)/shard_map/pallas_call | solution.py:117
  111.8 1.0 shard_map.74
  (31 shorter events, 0.1 us)
Async XLA Ops:
  3.4 20.8 %collective-permute-start.1 = (bf16[2,512,128]{2,1,0:T(8,128)(2,1)}, bf16[2,512,128]{2,1,0:T(8,128)(2,1)S(1)}, u32[]{:S(2)}, u32[]{:S(2)}) collective-permute-start(bf16[2,512,128]{2,1,0:T(8,128)(2,1)} %get-tuple-element.18), channel_id=1, source_target_pairs={{0,3},{1,2},{2,1},{3,0},{4,7},{5,6},{6,5},{7,4},{8,11},{9,10},{10,... | collective-permute-start | bytes 786440 | tf_op jit(solution)/shard_map/ppermute | solution.py:331
  6.5 17.7 %copy-start.5 = (bf16[2,512,128]{2,1,0:T(8,128)(2,1)S(1)}, bf16[2,512,128]{2,1,0:T(8,128)(2,1)}, u32[]{:S(2)}) copy-start(bf16[2,512,128]{2,1,0:T(8,128)(2,1)} %get-tuple-element.17.refs_2_) | copy-start | bytes 786436
  6.5 64.0 %all-to-all-start = ((bf16[16,2,128,128]{3,2,1,0:T(8,128)(2,1)}), bf16[16,2,128,128]{3,2,1,0:T(8,128)(2,1)S(1)}, u32[]{:S(2)}, u32[]{:S(2)}) async-start(bf16[16,2,128,128]{3,2,1,0:T(8,128)(2,1)} %get-tuple-element.27), calls=%async_computation | async-start | bytes 2097152 | tf_op jit(solution)/shard_map/all_to_all | solution.py:327
  13.0 20.1 %collective-permute-start.2 = (bf16[2,512,128]{2,1,0:T(8,128)(2,1)}, bf16[2,512,128]{2,1,0:T(8,128)(2,1)S(1)}, u32[]{:S(2)}, u32[]{:S(2)}) collective-permute-start(bf16[2,512,128]{2,1,0:T(8,128)(2,1)} %get-tuple-element.19), channel_id=1, source_target_pairs={{0,4},{1,5},{2,6},{3,7},{4,0},{5,1},{6,2},{7,3},{8,12},{9,13},{10,... | collective-permute-start | bytes 786440 | tf_op jit(solution)/shard_map/ppermute | solution.py:331
  14.4 24.0 %collective-permute-start.3 = (bf16[2,512,128]{2,1,0:T(8,128)(2,1)}, bf16[2,512,128]{2,1,0:T(8,128)(2,1)S(1)}, u32[]{:S(2)}, u32[]{:S(2)}) collective-permute-start(bf16[2,512,128]{2,1,0:T(8,128)(2,1)} %get-tuple-element.20), channel_id=1, source_target_pairs={{0,7},{1,6},{2,5},{3,4},{4,3},{5,2},{6,1},{7,0},{8,15},{9,14},{10,... | collective-permute-start | bytes 786440 | tf_op jit(solution)/shard_map/ppermute | solution.py:331
  16.2 1.6 %copy-start = (bf16[512,16,128]{2,1,0:T(8,128)(2,1)S(1)}, bf16[512,16,128]{2,1,0:T(8,128)(2,1)}, u32[]{:S(2)}) copy-start(bf16[512,16,128]{2,1,0:T(8,128)(2,1)} %q_ref.1) | copy-start | bytes 6291460
  19.6 0.8 copy-start.3
  20.4 29.3 %collective-permute-start = (bf16[4,512,128]{2,1,0:T(8,128)(2,1)S(1)}, bf16[4,512,128]{2,1,0:T(8,128)(2,1)S(1)}, u32[]{:S(2)}, u32[]{:S(2)}) collective-permute-start(bf16[4,512,128]{2,1,0:T(8,128)(2,1)S(1)} %get-tuple-element.15), channel_id=1, source_target_pairs={{0,7},{1,6},{2,5},{3,4},{4,3},{5,2},{6,1},{7,0},{8,15},{9,14},{10,... | collective-permute-start | bytes 1572872 | tf_op jit(solution)/shard_map/ppermute | solution.py:331
  24.2 14.5 %collective-permute-start.4 = (bf16[2,512,128]{2,1,0:T(8,128)(2,1)S(1)}, bf16[2,512,128]{2,1,0:T(8,128)(2,1)S(1)}, u32[]{:S(2)}, u32[]{:S(2)}) collective-permute-start(bf16[2,512,128]{2,1,0:T(8,128)(2,1)S(1)} %copy-done.5), channel_id=1, source_target_pairs={{0,1},{1,0},{2,3},{3,2},{4,5},{5,4},{6,7},{7,6},{8,9},{9,8},{10,11... | collective-permute-start | bytes 786440 | tf_op jit(solution)/shard_map/ppermute | solution.py:331
  24.2 25.4 %copy-start.6 = (bf16[2,512,128]{2,1,0:T(8,128)(2,1)}, bf16[2,512,128]{2,1,0:T(8,128)(2,1)S(1)}, u32[]{:S(2)}) copy-start(bf16[2,512,128]{2,1,0:T(8,128)(2,1)S(1)} %collective-permute-done.1.refs_3_) | copy-start | bytes 786436
  24.2 17.2 %collective-permute-start.5 = (bf16[2,512,128]{2,1,0:T(8,128)(2,1)S(1)}, bf16[2,512,128]{2,1,0:T(8,128)(2,1)S(1)}, u32[]{:S(2)}, u32[]{:S(2)}) collective-permute-start(bf16[2,512,128]{2,1,0:T(8,128)(2,1)S(1)} %collective-permute-done.1.refs_3_), channel_id=1, source_target_pairs={{0,1},{1,0},{2,3},{3,2},{4,5},{5,4},{6,7},{7,6},{8,9},{9,8},{10,11... | collective-permute-start | bytes 786440 | tf_op jit(solution)/shard_map/ppermute | solution.py:331
  33.1 16.6 %copy-start.7 = (bf16[2,512,128]{2,1,0:T(8,128)(2,1)}, bf16[2,512,128]{2,1,0:T(8,128)(2,1)S(1)}, u32[]{:S(2)}) copy-start(bf16[2,512,128]{2,1,0:T(8,128)(2,1)S(1)} %collective-permute-done.2.refs_4_) | copy-start | bytes 786436
  33.1 11.5 %collective-permute-start.6 = (bf16[2,512,128]{2,1,0:T(8,128)(2,1)S(1)}, bf16[2,512,128]{2,1,0:T(8,128)(2,1)S(1)}, u32[]{:S(2)}, u32[]{:S(2)}) collective-permute-start(bf16[2,512,128]{2,1,0:T(8,128)(2,1)S(1)} %collective-permute-done.2.refs_4_), channel_id=1, source_target_pairs={{0,1},{1,0},{2,3},{3,2},{4,5},{5,4},{6,7},{7,6},{8,9},{9,8},{10,11... | collective-permute-start | bytes 786440 | tf_op jit(solution)/shard_map/ppermute | solution.py:331
  38.4 11.3 %copy-start.8 = (bf16[2,512,128]{2,1,0:T(8,128)(2,1)}, bf16[2,512,128]{2,1,0:T(8,128)(2,1)S(1)}, u32[]{:S(2)}) copy-start(bf16[2,512,128]{2,1,0:T(8,128)(2,1)S(1)} %collective-permute-done.3.refs_5_) | copy-start | bytes 786436
  38.4 10.2 %collective-permute-start.7 = (bf16[2,512,128]{2,1,0:T(8,128)(2,1)S(1)}, bf16[2,512,128]{2,1,0:T(8,128)(2,1)S(1)}, u32[]{:S(2)}, u32[]{:S(2)}) collective-permute-start(bf16[2,512,128]{2,1,0:T(8,128)(2,1)S(1)} %collective-permute-done.3.refs_5_), channel_id=1, source_target_pairs={{0,1},{1,0},{2,3},{3,2},{4,5},{5,4},{6,7},{7,6},{8,9},{9,8},{10,11... | collective-permute-start | bytes 786440 | tf_op jit(solution)/shard_map/ppermute | solution.py:331
  38.7 10.9 %copy-start.9 = (bf16[2,512,128]{2,1,0:T(8,128)(2,1)}, bf16[2,512,128]{2,1,0:T(8,128)(2,1)S(1)}, u32[]{:S(2)}) copy-start(bf16[2,512,128]{2,1,0:T(8,128)(2,1)S(1)} %collective-permute-done.4.refs_6_) | copy-start | bytes 786436
  38.7 38.2 %collective-permute-start.8 = (bf16[4,512,128]{2,1,0:T(8,128)(2,1)}, bf16[4,512,128]{2,1,0:T(8,128)(2,1)}, u32[]{:S(2)}, u32[]{:S(2)}) collective-permute-start(bf16[4,512,128]{2,1,0:T(8,128)(2,1)} %get-tuple-element.22), channel_id=1, source_target_pairs={{0,3},{1,2},{2,1},{3,0},{4,7},{5,6},{6,5},{7,4},{8,11},{9,10},{10,... | collective-permute-start | bytes 1572872 | tf_op jit(solution)/shard_map/ppermute | solution.py:331
  41.5 8.2 %copy-start.10 = (bf16[2,512,128]{2,1,0:T(8,128)(2,1)}, bf16[2,512,128]{2,1,0:T(8,128)(2,1)S(1)}, u32[]{:S(2)}) copy-start(bf16[2,512,128]{2,1,0:T(8,128)(2,1)S(1)} %collective-permute-done.5.refs_7_) | copy-start | bytes 786436
  41.5 35.4 %collective-permute-start.9 = (bf16[4,512,128]{2,1,0:T(8,128)(2,1)}, bf16[4,512,128]{2,1,0:T(8,128)(2,1)}, u32[]{:S(2)}, u32[]{:S(2)}) collective-permute-start(bf16[4,512,128]{2,1,0:T(8,128)(2,1)} %get-tuple-element.23), channel_id=1, source_target_pairs={{0,4},{1,5},{2,6},{3,7},{4,0},{5,1},{6,2},{7,3},{8,12},{9,13},{10,... | collective-permute-start | bytes 1572872 | tf_op jit(solution)/shard_map/ppermute | solution.py:331
  44.6 5.0 %copy-start.11 = (bf16[2,512,128]{2,1,0:T(8,128)(2,1)}, bf16[2,512,128]{2,1,0:T(8,128)(2,1)S(1)}, u32[]{:S(2)}) copy-start(bf16[2,512,128]{2,1,0:T(8,128)(2,1)S(1)} %collective-permute-done.6.refs_8_) | copy-start | bytes 786436
  48.6 1.1 copy-start.12
  49.7 0.8 copy-start.4
  50.5 20.0 %copy-start.2 = (s32[16]{0:T(128)S(1)}, s32[16]{0:T(128)}, u32[]{:S(2)}) copy-start(s32[16]{0:T(128)} %order_ref.1) | copy-start | bytes 196
  65.9 29.2 %collective-permute-start.12 = (bf16[4,512,128]{2,1,0:T(8,128)(2,1)}, bf16[4,512,128]{2,1,0:T(8,128)(2,1)}, u32[]{:S(2)}, u32[]{:S(2)}) collective-permute-start(bf16[4,512,128]{2,1,0:T(8,128)(2,1)} %get-tuple-element.26), channel_id=1, source_target_pairs={{0,7},{1,6},{2,5},{3,4},{4,3},{5,2},{6,1},{7,0},{8,15},{9,14},{10,... | collective-permute-start | bytes 1572872 | tf_op jit(solution)/shard_map/ppermute | solution.py:331
  72.1 39.7 %all-to-all-start.1 = ((bf16[16,2,128,128]{3,2,1,0:T(8,128)(2,1)}), bf16[16,2,128,128]{3,2,1,0:T(8,128)(2,1)S(1)}, u32[]{:S(2)}, u32[]{:S(2)}) async-start(bf16[16,2,128,128]{3,2,1,0:T(8,128)(2,1)} %shard_map.73), calls=%async_computation.1 | async-start | bytes 2097152 | tf_op jit(solution)/shard_map/all_to_all | solution.py:327
  76.9 31.5 %copy-start.1 = (bf16[4,512,128]{2,1,0:T(8,128)(2,1)S(1)}, bf16[4,512,128]{2,1,0:T(8,128)(2,1)}, u32[]{:S(2)}) copy-start(bf16[4,512,128]{2,1,0:T(8,128)(2,1)} %get-tuple-element.21.refs_0_) | copy-start | bytes 1572868
  83.0 22.5 %collective-permute-start.10 = (bf16[4,512,128]{2,1,0:T(8,128)(2,1)}, bf16[4,512,128]{2,1,0:T(8,128)(2,1)S(1)}, u32[]{:S(2)}, u32[]{:S(2)}) collective-permute-start(bf16[4,512,128]{2,1,0:T(8,128)(2,1)} %get-tuple-element.24), channel_id=1, source_target_pairs={{0,3},{1,2},{2,1},{3,0},{4,7},{5,6},{6,5},{7,4},{8,11},{9,10},{10,... | collective-permute-start | bytes 1572872 | tf_op jit(solution)/shard_map/ppermute | solution.py:331
  95.1 13.4 %collective-permute-start.11 = (bf16[4,512,128]{2,1,0:T(8,128)(2,1)}, bf16[4,512,128]{2,1,0:T(8,128)(2,1)S(1)}, u32[]{:S(2)}, u32[]{:S(2)}) collective-permute-start(bf16[4,512,128]{2,1,0:T(8,128)(2,1)} %get-tuple-element.25), channel_id=1, source_target_pairs={{0,4},{1,5},{2,6},{3,7},{4,0},{5,1},{6,2},{7,3},{8,12},{9,13},{10,... | collective-permute-start | bytes 1572872 | tf_op jit(solution)/shard_map/ppermute | solution.py:331
